TPU v7x, 512 devices: a whole 4x4x16 slice. The times are simulated.
512 devices in a mesh: seq: 64 (over z, y), head: 8 (over x, core).
Axes of the slice: x: 4, y: 4, z: 16, core: 2. Of those that a mesh axis runs over, the one named last changes fastest.
Arguments:
- queries: bfloat16 [24576, 4096], P('seq', 'head'), may hold values from -32 to 32
- keys: bfloat16 [24576, 1024], P('seq', 'head'), may hold values from -9 to 9
- values: bfloat16 [24576, 1024], P('seq', 'head'), may hold values from -96 to 96
- block_ids: int32 [64, 32, 3], P('seq', 'head'), may hold values from 0 to 63, as said below
- out_weight: bfloat16 [4096, 4096], P('head'), may hold values from -0.09375 to 0.09375
Outputs:
- projected: bfloat16 [4096, 24576], P('head', 'seq')
Inputs may be any that keep to these rules, and one draw needn't show every extreme that they name: `block_ids`: for each query block and key/value head, the 12 ids of the query heads that share that key/value head are all different. An id at or above its own query block's index names a block that the causal rule removes.
All inputs are finite; a program needn't handle non-finite values.
Results may differ from a plain program's by a relative error of at most 0.02.
Values may be sent and summed in bfloat16 or wider, within the bound.
No kernel may reach another device: no remote copies, remote signals or barrier semaphores. Data moves between devices by JAX's collectives and lax.ppermute only.
A program may use at most 128 MiB of HBM per device.

v0:
```python
import math

import jax
import jax.numpy as jnp
from jax import lax
from jax.sharding import PartitionSpec as P

HEAD_DIMENSION = 128


def in_one_piece(arrays, axis, dim, along):
    widths = [a.shape[along] for a in arrays]
    both = jnp.concatenate(arrays, axis=along)
    out = lax.all_gather(both, axis, axis=dim, tiled=True)
    return tuple(jnp.split(out, [sum(widths[:k]) for k in range(1, len(widths))], axis=along))


def finish(block_scores, keep):
    if keep is not None:
        block_scores = jnp.where(keep, block_scores, -1e30)
    top = jnp.max(block_scores, axis=-1)
    prob = jnp.exp(block_scores - top[..., None])
    if keep is not None:
        prob = jnp.where(keep, prob, 0.0)
    return (prob, top, jnp.sum(prob, axis=-1))


def local(queries, keys, values, block_ids, out_weight):
    rows = queries.shape[0]
    kv_heads = keys.shape[1] // HEAD_DIMENSION
    group = queries.shape[1] // HEAD_DIMENSION // kv_heads
    picked_block_index = block_ids.shape[2]
    scale = 1.0 / math.sqrt(HEAD_DIMENSION)
    owners = lax.axis_size("seq")
    own_index = lax.axis_index("seq")
    q_all = queries.reshape(rows, kv_heads, group, HEAD_DIMENSION)
    k_own = keys.reshape(rows, kv_heads, HEAD_DIMENSION)
    v_own = values.reshape(rows, kv_heads, HEAD_DIMENSION)
    position = jnp.arange(rows, dtype=jnp.int32)
    causal = position[:, None] >= position[None, :]
    block_scores = (
        jnp.einsum("tcid,kcd->citk", q_all, k_own, preferred_element_type=jnp.float32) * scale
    )
    prob, own_top, own_total = finish(block_scores, causal)
    own_part = jnp.einsum(
        "citk,kcd->citd", prob.astype(jnp.bfloat16), v_own, preferred_element_type=jnp.float32
    ).astype(jnp.bfloat16)
    chosen = block_ids[0].reshape(kv_heads, group, picked_block_index)
    live = chosen < own_index
    kv_index = jnp.arange(kv_heads, dtype=jnp.int32)[:, None, None]
    k_whole, v_whole = in_one_piece((keys, values), "seq", 0, 1)
    key_block_tiles = k_whole.reshape(owners, rows, kv_heads, HEAD_DIMENSION)
    value_block_tiles = v_whole.reshape(owners, rows, kv_heads, HEAD_DIMENSION)
    k_sel = key_block_tiles[chosen, :, kv_index]
    v_sel = value_block_tiles[chosen, :, kv_index]
    sel_scores = (
        jnp.einsum("tcid,cijkd->cijtk", q_all, k_sel, preferred_element_type=jnp.float32) * scale
    )
    sel_prob, sel_top, sel_total = finish(sel_scores, None)
    sel_part = jnp.einsum(
        "cijtk,cijkd->cijtd",
        sel_prob.astype(jnp.bfloat16),
        v_sel,
        preferred_element_type=jnp.float32,
    ).astype(jnp.bfloat16)
    safe_top = jnp.where(live[..., None], sel_top, own_top[:, :, None, :])
    top = jnp.maximum(own_top, jnp.max(safe_top, axis=2))
    own_weight = jnp.exp(own_top - top)
    sel_weight = jnp.where(live[..., None], jnp.exp(safe_top - top[:, :, None, :]), 0.0)
    total = own_weight * own_total + jnp.sum(sel_weight * sel_total, axis=2)
    accum = own_weight[..., None] * own_part.astype(jnp.float32) + jnp.sum(
        sel_weight[..., None] * sel_part.astype(jnp.float32), axis=2
    )
    attended = (
        (accum / total[..., None])
        .transpose(2, 0, 1, 3)
        .reshape(rows, kv_heads * group * HEAD_DIMENSION)
        .astype(jnp.bfloat16)
    )
    return lax.psum_scatter(
        lax.dot_general(
            out_weight, attended, (((0,), (1,)), ((), ())), preferred_element_type=jnp.float32
        ).astype(jnp.bfloat16),
        "head",
        scatter_dimension=0,
        tiled=True,
    )


def solution(mesh):
    return jax.shard_map(
        local,
        mesh=mesh,
        in_specs=(
            P("seq", "head"),
            P("seq", "head"),
            P("seq", "head"),
            P("seq", "head", None),
            P("head", None),
        ),
        out_specs=P("head", "seq"),
        check_vma=False,
    )
```

profile of v0, /device:TPU:8, one launch (start us, length us, event | category | flops | bytes accessed | tf_op | source)
XLA Modules:
  0.0 269.5 jit_solution(2000248079897891150)
XLA Ops:
  6.5 1.6 pad_maximum_fusion
  8.3 0.7 fusion.36
  9.0 0.1 copy.27
  9.2 1.8 reshape.144
  11.0 0.7 broadcast_compare_fusion
  11.7 0.1 copy.25
  11.8 1.7 fusion.9
  13.5 1.2 fusion.10
  14.7 168.9 %all-gather.2.cloned.1.call-done = bf16[24576,256]{1,0:T(8,128)(2,1)} async-done(((bf16[384,256]{1,0:T(8,128)(2,1)}), bf16[24576,256]{1,0:T(8,128)(2,1)}) %all-gather.2.cloned.1.call-update) | async-done | bytes 12582928 | tf_op jit(solution)/shard_map/all_gather | solution.py:14
  183.6 10.1 %fusion.44 = (bf16[24576,128]{1,0:T(8,128)(2,1)}, bf16[24576,128]{1,0:T(8,128)(2,1)}) fusion(bf16[24576,256]{1,0:T(8,128)(2,1)} %all-gather.2.cloned.1.call-done), kind=kLoop, calls=%fused_computation.59 | loop fusion | bytes 25165824 | tf_op jit(solution)/shard_map/split | solution.py:15
  193.7 3.6 %gather_fusion = bf16[12,384,128]{2,1,0:T(8,128)(2,1)S(1)} fusion(bf16[64,384,1,128]{3,1,0,2:T(8,128)(2,1)} %bitcast.86, s32[12]{0:T(128)S(1)} %reshape.153), kind=kCustom, calls=%fused_computation | custom fusion | bytes 2359392 | tf_op jit(solution)/shard_map/gather | solution.py:54
  197.3 2.1 bitcast_reduce_fusion
  199.4 1.2 fusion.1
  200.6 1.7 copy-done
  202.4 0.1 select_reduce_fusion
  202.5 4.5 %gather_fusion.1 = bf16[12,384,128]{2,1,0:T(8,128)(2,1)} fusion(bf16[64,384,1,128]{3,1,0,2:T(8,128)(2,1)} %bitcast.85, s32[12]{0:T(128)S(1)} %reshape.153), kind=kCustom, calls=%fused_computation.1 | custom fusion | bytes 2359392 | tf_op jit(solution)/shard_map/gather | solution.py:55
  207.0 0.1 multiply_reduce_fusion.1
  207.2 6.4 %multiply_reduce_fusion = f32[4,384,128]{2,1,0:T(8,128)} fusion(f32[4,3,384]{2,1,0:T(4,128)S(1)} %get-tuple-element.8, bf16[4,3,384,128]{3,2,1,0:T(8,128)(2,1)} %bitcast.89, f32[4,3,384,384]{3,2,1,0:T(8,128)} %copy-done, f32[4,3,384]{2,1,0:T(4,128)S(1)} %copy-done.5), kind=kOutput, calls=%fused_computation.14 | convolution fusion | flops 460455936 | bytes 9080832 | tf_op jit(solution)/shard_map/cijtk,cijkd->cijtd/dot_general | solution.py:60
  213.6 1.4 copy.32
  215.0 0.7 fusion.19
  215.7 1.5 copy-done.1
  217.2 3.5 %fusion.3 = bf16[4096,384]{0,1:T(8,128)(2,1)} fusion(bf16[384,512]{0,1:T(8,128)(2,1)S(1)} %bitcast.90, bf16[512,4096]{1,0:T(8,128)(2,1)S(1)} %copy-done.1), kind=kOutput, calls=%fused_computation.8 | convolution fusion | flops 1612185600 | bytes 7733248 | tf_op jit(solution)/shard_map/dot_general | solution.py:81
  220.8 40.0 %reduce-scatter.2.cloned.1.call-done = bf16[512,384]{0,1:T(8,128)(2,1)} async-done(((bf16[4096,384]{0,1:T(8,128)(2,1)}), bf16[512,384]{0,1:T(8,128)(2,1)}) %reduce-scatter.2.cloned.1.call-update) | async-done | bytes 393232 | tf_op jit(solution)/shard_map/reduce_scatter | solution.py:80
  260.7 1.9 copy.33
  (24 shorter events, 0.3 us)
Async XLA Ops:
  6.5 177.1 %all-gather.2.cloned.1.call-start = ((), (), s32[]{:S(2)}) async-start(), calls=%async_computation.1 | async-start | bytes 12779520 | tf_op jit(solution)/shard_map/all_gather | solution.py:14
  8.2 252.5 %reduce-scatter.2.cloned.1.call-start = ((), (), s32[]{:S(2)}) async-start(), calls=%async_computation.2 | async-start | bytes 3538944 | tf_op jit(solution)/shard_map/reduce_scatter | solution.py:80
  11.8 1.7 copy-start.2
  199.4 2.9 %copy-start = (f32[4,3,384,384]{3,2,1,0:T(8,128)}, f32[4,3,384,384]{3,2,1,0:T(8,128)S(1)}, u32[]{:S(2)}) copy-start(f32[4,3,384,384]{3,2,1,0:T(8,128)S(1)} %get-tuple-element.12) | copy-start | bytes 21233668
  199.4 2.9 %copy-start.4 = (f32[4,3,384]{2,1,0:T(4,128)}, f32[4,3,384]{2,1,0:T(4,128)S(1)}, u32[]{:S(2)}) copy-start(f32[4,3,384]{2,1,0:T(4,128)S(1)} %get-tuple-element.11) | copy-start | bytes 55300
  202.5 4.6 %copy-start.5 = (f32[4,3,384]{2,1,0:T(4,128)S(1)}, f32[4,3,384]{2,1,0:T(4,128)}, u32[]{:S(2)}) copy-start(f32[4,3,384]{2,1,0:T(4,128)} %copy-done.4) | copy-start | bytes 55300
  207.1 7.8 %copy-start.7 = (f32[4,384]{1,0:T(4,128)S(1)}, f32[4,384]{1,0:T(4,128)}, u32[]{:S(2)}) copy-start(f32[4,384]{1,0:T(4,128)} %fusion.10) | copy-start | bytes 18436
  207.1 7.8 %copy-start.3 = (pred[384,384]{0,1:T(8,128)(4,1)S(1)}, pred[384,384]{0,1:T(8,128)(4,1)}, u32[]{:S(2)}) copy-start(pred[384,384]{0,1:T(8,128)(4,1)} %copy-done.2) | copy-start | bytes 442372
  207.2 7.8 %copy-start.6 = (bf16[384,128]{1,0:T(8,128)(2,1)S(1)}, bf16[384,128]{1,0:T(8,128)(2,1)}, u32[]{:S(2)}) copy-start(bf16[384,128]{1,0:T(8,128)(2,1)} %param.7) | copy-start | bytes 294916
  215.0 2.2 copy-start.1
Sparse Core Ops, SparseCore 0:
  10.3 173.2 all-gather.1
  220.9 39.7 reduce-scatter.1
where the time goes:
time: 270 us; the launch traced here: 269 us
  waiting for transfers between devices  209 us (77%)
  local copies, waits for them, and re-layouts  26.9 us (10%)
  matrix products  14.4 us (5%)
  between operations  13.6 us (5%)
  other arithmetic  5.68 us (2%)
    all_gather x1, waiting for transfers between devices, in_one_piece(): out = lax.all_gather(both, axis, axis=dim, tiled=True)  169 us
    reduce_scatter x1, waiting for transfers between devices, local(): lax.psum_scatter(lax.dot_general(out_weight, attended, (((0,), (1,)), (()...  40 us
    split x1, local copies, waits for them, and re-layouts, in_one_piece(): jnp.split(out, [sum(widths[:k]) for k in range(1, len(widths))], axis=along)  10.1 us
    dot_general x1, matrix products, local(): jnp.einsum('cijtk,cijkd->cijtd', sel_prob.astype(jnp.bfloat16), v_sel, pr...  6.38 us
  transfers between devices with their start and end apart: 2, of which 2 were waited for; matrix products, arithmetic and copies ran while one was open for 2% of the time, Pallas kernels for 0%

commit v1 on v0

v1 whole, which is shorter than its diff:
```python
import math

import jax
import jax.numpy as jnp
from jax import lax
from jax.experimental import pallas as pl
from jax.experimental.pallas import tpu as pltpu
from jax.sharding import Mesh, PartitionSpec as P

HD = 128
HEADS = 4
TOP = 3
NZ, NY, NX = 16, 4, 4
TOK = 384
SL = TOK // NY
EXT = HEADS * HD + 16
LOG2E = 1.4426950408889634
COEF = LOG2E / math.sqrt(HD)
DEAD = -1e30
SLOTS = (2, 10, 14, 7, 3, 11, 15, 4, 0, 8, 12, 5, 1, 9, 13, 6)


def shift(n, s):
    return [(i, (i + s) % n) for i in range(n)]


def tn(a, b):
    return lax.dot_general(a, b, (((0,), (0,)), ((), ())), preferred_element_type=jnp.float32)


def own_kernel(q_ref, k_ref, v_ref, o_ref, lse_ref):
    keep = lax.broadcasted_iota(jnp.int32, (TOK, TOK), 0) <= lax.broadcasted_iota(
        jnp.int32, (TOK, TOK), 1
    )
    k = k_ref[...]
    v = v_ref[...]
    rows = []
    for h in range(HEADS):
        s = jnp.dot(k, q_ref[h * HD : (h + 1) * HD, :], preferred_element_type=jnp.float32)
        s = jnp.where(keep, s * COEF, DEAD)
        top = jnp.max(s, axis=0, keepdims=True)
        p = jnp.exp2(s - top)
        total = jnp.sum(p, axis=0, keepdims=True)
        o = tn(v, p.astype(jnp.bfloat16)) * (1.0 / total)
        o_ref[h * HD : (h + 1) * HD, :] = o.astype(jnp.bfloat16)
        rows.append(top + jnp.log2(total))
    lse_ref[...] = jnp.concatenate(rows + rows, axis=0)


def slices_of(idx_ref, bias_ref, kv, q_ref, o_ref, base):
    rows = []
    for h in range(HEADS):
        at = base + h * TOP
        picked = [kv[idx_ref[at + j]] for j in range(TOP)]
        k = jnp.concatenate([t[:, :HD] for t in picked], axis=0)
        v = jnp.concatenate([t[:, HD:] for t in picked], axis=0)
        s = jnp.dot(k, q_ref[h * HD : (h + 1) * HD, :], preferred_element_type=jnp.float32)
        s = [s[j * SL : (j + 1) * SL] * COEF + bias_ref[at + j] for j in range(TOP)]
        s = jnp.concatenate(s, axis=0)
        top = jnp.max(s, axis=0, keepdims=True)
        p = jnp.exp2(s - top)
        total = jnp.sum(p, axis=0, keepdims=True)
        o = tn(v, p.astype(jnp.bfloat16)) * (1.0 / total)
        o_ref[h * HD : (h + 1) * HD, :] = o.astype(jnp.bfloat16)
        lse = top + jnp.log2(total)
        hi = lse.astype(jnp.bfloat16).astype(jnp.float32)
        mid = (lse - hi).astype(jnp.bfloat16).astype(jnp.float32)
        rows += [hi, mid, lse - hi - mid]
    rows += [jnp.zeros((4, TOK), jnp.float32)]
    o_ref[HEADS * HD :, :] = jnp.concatenate(rows, axis=0).astype(jnp.bfloat16)


def make_slices(n):
    def kernel(idx_ref, bias_ref, a0, a1, a2, a3, a4, *rest):
        q_refs, o_refs, (kv, sems) = rest[:n], rest[n : 2 * n], rest[2 * n :]
        copies = []
        at = 0
        for i, src in enumerate((a0, a1, a2, a3, a4)):
            width = src.shape[0]
            copies.append(pltpu.make_async_copy(src, kv.at[pl.ds(at, width)], sems.at[i]))
            at += width
        for c in copies:
            c.start()
        for c in copies:
            c.wait()
        for i in range(n):
            slices_of(idx_ref, bias_ref, kv, q_refs[i], o_refs[i], i * HEADS * TOP)

    smem = pl.BlockSpec(memory_space=pltpu.SMEM)
    vmem = pl.BlockSpec(memory_space=pltpu.VMEM)
    hbm = pl.BlockSpec(memory_space=pl.ANY)
    return pl.pallas_call(
        kernel,
        in_specs=[smem, smem] + [hbm] * 5 + [vmem] * n,
        out_specs=[vmem] * n,
        out_shape=[jax.ShapeDtypeStruct((EXT, TOK), jnp.bfloat16)] * n,
        scratch_shapes=[
            pltpu.VMEM((NZ * NY, SL, 2 * HD), jnp.bfloat16),
            pltpu.SemaphoreType.DMA((5,)),
        ],
    )


def merge_kernel(own_ref, lse_ref, p0, p1, p2, p3, out_ref):
    parts = (p0, p1, p2, p3)
    tails = [p[HEADS * HD :, :].astype(jnp.float32) for p in parts]
    for h in range(HEADS):
        span = slice(h * HD, (h + 1) * HD)
        own = lse_ref[h : h + 1, :]
        lses = [
            t[3 * h : 3 * h + 1] + t[3 * h + 1 : 3 * h + 2] + t[3 * h + 2 : 3 * h + 3]
            for t in tails
        ]
        top = own
        for x in lses:
            top = jnp.maximum(top, x)
        w = jnp.exp2(own - top)
        total = w
        acc = w * own_ref[span, :].astype(jnp.float32)
        for p, x in zip(parts, lses):
            w = jnp.exp2(x - top)
            total = total + w
            acc = acc + w * p[span, :].astype(jnp.float32)
        out_ref[span, :] = (acc * (1.0 / total)).astype(jnp.bfloat16)


def local(queries, keys, values, block_ids, out_weight):
    z = lax.axis_index("z")
    y = lax.axis_index("y")
    x = lax.axis_index("x")
    core = lax.axis_index("core")
    kv = jnp.concatenate([keys, values], axis=1).reshape(NY, SL, 2 * HD)
    row = lax.all_to_all(kv, "y", 0, 0)
    far = lax.ppermute(row, "z", shift(NZ, 8))
    up = lax.ppermute(row, "z", shift(NZ, 4))
    down = lax.ppermute(row, "z", shift(NZ, -4))
    c = jnp.concatenate([far, up, row, down], axis=0)
    n1 = lax.ppermute(c, "z", shift(NZ, 1))
    n2 = lax.ppermute(c, "z", shift(NZ, -1))
    m1 = lax.ppermute(c[NY : 3 * NY], "z", shift(NZ, 2))
    m2 = lax.ppermute(c[2 * NY :], "z", shift(NZ, -2))
    qt = queries.T
    id_rows = jnp.zeros((16, TOK), jnp.bfloat16)
    id_rows = lax.dynamic_update_slice(
        id_rows, block_ids.reshape(1, HEADS * TOP).astype(jnp.bfloat16), (0, 0)
    )
    qx = jnp.concatenate([qt, id_rows], axis=0)
    qs = [qx] + [lax.ppermute(qx, "y", shift(NY, s)) for s in (1, 2, 3)]
    ids = jnp.stack(
        [a[HEADS * HD, : HEADS * TOP].astype(jnp.int32) for a in qs], axis=0
    )
    theirs = z * NY + (y - jnp.arange(NY, dtype=jnp.int32)) % NY
    bias = jnp.where(ids < theirs[:, None], 0.0, DEAD).astype(jnp.float32)
    slot = jnp.array(SLOTS, jnp.int32)[(ids // NY - z) % NZ] * NY + ids % NY
    vmem = pl.BlockSpec(memory_space=pltpu.VMEM)
    own, own_lse = pl.pallas_call(
        own_kernel,
        in_specs=[vmem] * 3,
        out_specs=[vmem] * 2,
        out_shape=[
            jax.ShapeDtypeStruct((HEADS * HD, TOK), jnp.bfloat16),
            jax.ShapeDtypeStruct((2 * HEADS, TOK), jnp.float32),
        ],
    )(qt, keys, values)
    gathered = (c, n1, n2, m1, m2)
    q2, q1, q3 = qs[2], qs[1], qs[3]
    order = jnp.array([2, 1, 3], jnp.int32)
    o2, o1, o3 = make_slices(3)(
        slot[order].reshape(-1), bias[order].reshape(-1), *gathered, q2, q1, q3
    )
    r2 = lax.ppermute(o2, "y", shift(NY, -2))
    r1 = lax.ppermute(o1, "y", shift(NY, -1))
    r3 = lax.ppermute(o3, "y", shift(NY, -3))
    (o0,) = make_slices(1)(slot[0], bias[0], *gathered, qs[0])
    att = pl.pallas_call(
        merge_kernel,
        in_specs=[vmem] * 6,
        out_specs=vmem,
        out_shape=jax.ShapeDtypeStruct((HEADS * HD, TOK), jnp.bfloat16),
    )(own, own_lse, o0, r1, r2, r3)
    pair = [(0, 1), (1, 0)]
    feats = out_weight.reshape(HEADS * HD, NX, 2, HEADS * HD)
    w_mine = lax.dynamic_index_in_dim(feats, core, axis=2, keepdims=False)
    w_give = lax.dynamic_index_in_dim(feats, 1 - core, axis=2, keepdims=False)
    w_got = lax.ppermute(w_give, "core", pair)
    w = jnp.concatenate([w_mine, w_got], axis=0)
    att_got = lax.ppermute(att, "core", pair)
    att_both = jnp.concatenate([att, att_got], axis=0)

    def piece(s):
        cut = lax.dynamic_index_in_dim(w, (x + s) % NX, axis=1, keepdims=False)
        return tn(cut, att_both)

    got = [
        lax.ppermute(piece(s).astype(jnp.bfloat16), "x", shift(NX, s)) for s in (2, 1, 3)
    ]
    total = piece(0)
    for g in got:
        total = total + g.astype(jnp.float32)
    return total.astype(jnp.bfloat16)


def solution(mesh):
    grid = Mesh(mesh.devices.reshape(NZ, NY, NX, 2), ("z", "y", "x", "core"))
    rows, cols = ("z", "y"), ("x", "core")
    return jax.shard_map(
        local,
        mesh=grid,
        in_specs=(P(rows, cols), P(rows, cols), P(rows, cols), P(rows, cols, None), P(cols, None)),
        out_specs=P(cols, rows),
        check_vma=False,
    )
```

time: 270 us -> 217 us (0.80)
  the two profiles are of different devices: /device:TPU:8 before, /device:TPU:70 now
where the time goes in v1:
time: 217 us; the launch traced here: 215 us
  starting transfers between devices  82.5 us (38%)
  waiting for transfers between devices  71.2 us (33%)
  local copies, waits for them, and re-layouts  25.9 us (12%)
  Pallas kernels  19 us (9%)
  matrix products  10.8 us (5%)
  other arithmetic  5.51 us (3%)
    ppermute x1, waiting for transfers between devices, local(): m2 = lax.ppermute(c[2 * NY:], 'z', shift(NZ, -2))  22.1 us
    ppermute x1, waiting for transfers between devices, local(): down = lax.ppermute(row, 'z', shift(NZ, -4))  15.9 us
    ppermute x1, starting transfers between devices, local(): far = lax.ppermute(row, 'z', shift(NZ, 8))  13.9 us
    ppermute x3, waiting for transfers between devices, local(): lax.ppermute(piece(s).astype(jnp.bfloat16), 'x', shift(NX, s))  12.4 us
    ppermute x3, starting transfers between devices, local(): qs = [qx] + [lax.ppermute(qx, 'y', shift(NY, s)) for s in (1, 2, 3)]  11.6 us
    unnamed x29, local copies, waits for them, and re-layouts  10.9 us
    dot_general x4, matrix products, tn(): lax.dot_general(a, b, (((0,), (0,)), ((), ())), preferred_element_type=jn...  10.8 us
    ppermute x3, starting transfers between devices, local(): lax.ppermute(piece(s).astype(jnp.bfloat16), 'x', shift(NX, s))  9.25 us
  transfers between devices with their start and end apart: 19, of which 9 were waited for; matrix products, arithmetic and copies ran while one was open for 15% of the time, Pallas kernels for 9%

profile of v1, /device:TPU:70, one launch (start us, length us, event | category | flops | bytes accessed | tf_op | source)
XLA Modules:
  0.0 215.2 jit_solution(4031912748258124598)
XLA Ops:
  2.2 3.5 %collective-permute-start.1 = (bf16[528,384]{1,0:T(8,128)(2,1)S(1)}, bf16[528,384]{1,0:T(8,128)(2,1)}, u32[]{:S(2)}, u32[]{:S(2)}) collective-permute-start(bf16[528,384]{1,0:T(8,128)(2,1)S(1)} %fusion.16.rest_0_), channel_id=1, source_target_pairs={{0,8},{8,16},{16,24},{24,0},{1,9},{9,17},{17,25},{25,1},{2,10},{10... | collective-permute-start | bytes 1216520 | tf_op jit(solution)/shard_map/ppermute | solution.py:148
  5.7 4.8 %collective-permute-start.2 = (bf16[528,384]{1,0:T(8,128)(2,1)S(1)}, bf16[528,384]{1,0:T(8,128)(2,1)}, u32[]{:S(2)}, u32[]{:S(2)}) collective-permute-start(bf16[528,384]{1,0:T(8,128)(2,1)S(1)} %fusion.16.rest_0_), channel_id=1, source_target_pairs={{0,16},{8,24},{16,0},{24,8},{1,17},{9,25},{17,1},{25,9},{2,18},{10... | collective-permute-start | bytes 1216520 | tf_op jit(solution)/shard_map/ppermute | solution.py:148
  15.4 3.4 %all-to-all-start = ((bf16[4,96,256]{2,1,0:T(8,128)(2,1)}), bf16[4,96,256]{2,1,0:T(8,128)(2,1)S(1)}, u32[]{:S(2)}, u32[]{:S(2)}) async-start(bf16[4,96,256]{2,1,0:T(8,128)(2,1)} %bitcast.11), calls=%async_computation | async-start | bytes 393216 | tf_op jit(solution)/shard_map/all_to_all | solution.py:133
  18.8 6.5 %copy.12 = bf16[512,4096]{0,1:T(8,128)(2,1)} copy(bf16[512,4096]{1,0:T(8,128)(2,1)} %param.11) | data formatting | bytes 8388608 | tf_op args[4]
  25.3 4.0 %all-to-all-done = bf16[4,96,256]{2,1,0:T(8,128)(2,1)S(1)} async-done(((bf16[4,96,256]{2,1,0:T(8,128)(2,1)}), bf16[4,96,256]{2,1,0:T(8,128)(2,1)S(1)}, u32[]{:S(2)}, u32[]{:S(2)}) %all-to-all-start) | async-done | bytes 196640 | tf_op jit(solution)/shard_map/all_to_all | solution.py:133
  29.3 13.9 %collective-permute-start.4 = (bf16[4,96,256]{2,1,0:T(8,128)(2,1)S(1)}, bf16[4,96,256]{2,1,0:T(8,128)(2,1)S(1)}, u32[]{:S(2)}, u32[]{:S(2)}) collective-permute-start(bf16[4,96,256]{2,1,0:T(8,128)(2,1)S(1)} %all-to-all-done), channel_id=1, source_target_pairs={{0,256},{32,288},{64,320},{96,352},{128,384},{160,416},{192,448},{... | collective-permute-start | bytes 589832 | tf_op jit(solution)/shard_map/ppermute | solution.py:134
  43.2 3.9 %constant_dynamic-slice_fusion = (bf16[512,4,1,512]{0,3,2,1:T(8,128)(2,1)}, bf16[512,4,1,512]{0,3,2,1:T(8,128)(2,1)S(1)}) fusion(bf16[512,4,2,512]{0,3,2,1:T(8,128)(2,1)} %bitcast.29, s32[]{:T(128)S(6)} %select_n.97, s32[]{:T(128)S(6)} %select_n.96), kind=kLoop, calls=%fused_computation.54 | loop fusion | bytes 8388616 | tf_op jit(solution)/shard_map/jit(dynamic_index_in_dim)/dynamic_slice | solution.py:184
  50.3 4.2 %copy.14 = bf16[512,4,1,512]{3,0,2,1:T(8,128)(2,1)} copy(bf16[512,4,1,512]{0,3,2,1:T(8,128)(2,1)} %get-tuple-element.15) | data formatting | bytes 4194304 | tf_op jit(solution)/shard_map/jit(dynamic_index_in_dim)/dynamic_slice | solution.py:184
  54.4 4.4 %collective-permute-start.5 = (bf16[4,96,256]{2,1,0:T(8,128)(2,1)S(1)}, bf16[4,96,256]{2,1,0:T(8,128)(2,1)S(1)}, u32[]{:S(2)}, u32[]{:S(2)}) collective-permute-start(bf16[4,96,256]{2,1,0:T(8,128)(2,1)S(1)} %all-to-all-done), channel_id=1, source_target_pairs={{0,128},{32,160},{64,192},{96,224},{128,256},{160,288},{192,320},{... | collective-permute-start | bytes 589832 | tf_op jit(solution)/shard_map/ppermute | solution.py:135
  62.4 6.5 %collective-permute-done.5 = bf16[4,96,256]{2,1,0:T(8,128)(2,1)S(1)} collective-permute-done((bf16[4,96,256]{2,1,0:T(8,128)(2,1)S(1)}, bf16[4,96,256]{2,1,0:T(8,128)(2,1)S(1)}, u32[]{:S(2)}, u32[]{:S(2)}) %collective-permute-start.5) | collective-permute-done | bytes 196640 | tf_op jit(solution)/shard_map/ppermute | solution.py:135
  68.9 8.5 %collective-permute-start.6 = (bf16[4,96,256]{2,1,0:T(8,128)(2,1)S(1)}, bf16[4,96,256]{2,1,0:T(8,128)(2,1)S(1)}, u32[]{:S(2)}, u32[]{:S(2)}) collective-permute-start(bf16[4,96,256]{2,1,0:T(8,128)(2,1)S(1)} %all-to-all-done), channel_id=1, source_target_pairs={{0,384},{32,416},{64,448},{96,480},{128,0},{160,32},{192,64},{224,... | collective-permute-start | bytes 589832 | tf_op jit(solution)/shard_map/ppermute | solution.py:136
  77.5 15.9 %collective-permute-done.6 = bf16[4,96,256]{2,1,0:T(8,128)(2,1)S(1)} collective-permute-done((bf16[4,96,256]{2,1,0:T(8,128)(2,1)S(1)}, bf16[4,96,256]{2,1,0:T(8,128)(2,1)S(1)}, u32[]{:S(2)}, u32[]{:S(2)}) %collective-permute-start.6) | collective-permute-done | bytes 196640 | tf_op jit(solution)/shard_map/ppermute | solution.py:136
  93.5 4.9 %collective-permute-start.7 = (bf16[16,96,256]{2,1,0:T(8,128)(2,1)S(1)}, bf16[16,96,256]{2,1,0:T(8,128)(2,1)}, u32[]{:S(2)}, u32[]{:S(2)}) collective-permute-start(bf16[16,96,256]{2,1,0:T(8,128)(2,1)S(1)} %constant_dynamic-update-slice_fusion.a0), channel_id=1, source_target_pairs={{0,32},{32,64},{64,96},{96,128},{128,160},{160,192},{192,224},{224... | collective-permute-start | bytes 2359304 | tf_op jit(solution)/shard_map/ppermute | solution.py:138
  107.4 4.6 %collective-permute-start.9 = (bf16[8,96,256]{2,1,0:T(8,128)(2,1)}, bf16[8,96,256]{2,1,0:T(8,128)(2,1)S(1)}, u32[]{:S(2)}, u32[]{:S(2)}) collective-permute-start(bf16[8,96,256]{2,1,0:T(8,128)(2,1)} %get-tuple-element.24), channel_id=1, source_target_pairs={{0,64},{32,96},{64,128},{96,160},{128,192},{160,224},{192,256},{22... | collective-permute-start | bytes 1179656 | tf_op jit(solution)/shard_map/ppermute | solution.py:140
  116.2 22.1 %collective-permute-done.10.a4 = bf16[8,96,256]{2,1,0:T(8,128)(2,1)} collective-permute-done((bf16[8,96,256]{2,1,0:T(8,128)(2,1)}, bf16[8,96,256]{2,1,0:T(8,128)(2,1)}, u32[]{:S(2)}, u32[]{:S(2)}) %collective-permute-start.10) | collective-permute-done | bytes 393248 | tf_op jit(solution)/shard_map/ppermute | solution.py:141
  139.0 8.0 %shard_map.75 = (bf16[528,384]{1,0:T(8,128)(2,1)}, bf16[528,384]{1,0:T(8,128)(2,1)}, bf16[528,384]{1,0:T(8,128)(2,1)}) custom-call(s32[36]{0:T(128)} %reshape.329.idx_ref, f32[36]{0:T(128)} %reshape.330.bias_ref, bf16[16,96,256]{2,1,0:T(8,128)(2,1)} %copy-done.1, bf16[16,96,256]{2,1,0:T(8,128)(2,1)} %collective-permute-done.7.a1, ...), custom_call_target="tpu_custom_call" | custom-call | tf_op jit(solution)/shard_map/pallas_call | solution.py:168
  147.0 5.6 %collective-permute-start.11 = (bf16[528,384]{1,0:T(8,128)(2,1)}, bf16[528,384]{1,0:T(8,128)(2,1)S(1)}, u32[]{:S(2)}, u32[]{:S(2)}) collective-permute-start(bf16[528,384]{1,0:T(8,128)(2,1)} %get-tuple-element.12), channel_id=1, source_target_pairs={{0,24},{8,0},{16,8},{24,16},{1,25},{9,1},{17,9},{25,17},{2,26},{10... | collective-permute-start | bytes 1216520 | tf_op jit(solution)/shard_map/ppermute | solution.py:172
  152.6 3.9 %collective-permute-start.12 = (bf16[528,384]{1,0:T(8,128)(2,1)}, bf16[528,384]{1,0:T(8,128)(2,1)S(1)}, u32[]{:S(2)}, u32[]{:S(2)}) collective-permute-start(bf16[528,384]{1,0:T(8,128)(2,1)} %get-tuple-element.13), channel_id=1, source_target_pairs={{0,16},{8,24},{16,0},{24,8},{1,17},{9,25},{17,1},{25,9},{2,18},{10... | collective-permute-start | bytes 1216520 | tf_op jit(solution)/shard_map/ppermute | solution.py:171
  159.5 5.0 %shard_map.74.p0 = bf16[528,384]{1,0:T(8,128)(2,1)} custom-call(s32[12]{0:T(128)} %slice_bitcast_fusion.1.idx_ref, f32[12]{0:T(128)} %slice_bitcast_fusion.bias_ref, bf16[16,96,256]{2,1,0:T(8,128)(2,1)} %copy-done.1, bf16[16,96,256]{2,1,0:T(8,128)(2,1)} %collective-permute-done.7.a1, bf16[16,96,256]{2,1,0:T(8,128)(2,1)} %collective-permute-done.8.a2, ...), custom_call_target="tpu_custom_call" | custom-call | tf_op jit(solution)/shard_map/pallas_call | solution.py:174
  164.6 4.8 %collective-permute-done.11.p1 = bf16[528,384]{1,0:T(8,128)(2,1)S(1)} collective-permute-done((bf16[528,384]{1,0:T(8,128)(2,1)}, bf16[528,384]{1,0:T(8,128)(2,1)S(1)}, u32[]{:S(2)}, u32[]{:S(2)}) %collective-permute-start.11) | collective-permute-done | bytes 405536 | tf_op jit(solution)/shard_map/ppermute | solution.py:172
  169.3 5.5 %collective-permute-done.13.p3 = bf16[528,384]{1,0:T(8,128)(2,1)S(1)} collective-permute-done((bf16[528,384]{1,0:T(8,128)(2,1)}, bf16[528,384]{1,0:T(8,128)(2,1)S(1)}, u32[]{:S(2)}, u32[]{:S(2)}) %collective-permute-start.13) | collective-permute-done | bytes 405536 | tf_op jit(solution)/shard_map/ppermute | solution.py:173
  191.5 4.0 %collective-permute-start.16 = (bf16[512,384]{1,0:T(8,128)(2,1)}, bf16[512,384]{1,0:T(8,128)(2,1)}, u32[]{:S(2)}, u32[]{:S(2)}) collective-permute-start(bf16[512,384]{1,0:T(8,128)(2,1)} %convolution_convert_fusion.1), channel_id=1, source_target_pairs={{0,2},{2,4},{4,6},{6,0},{1,3},{3,5},{5,7},{7,1},{8,10},{10,12},{12... | collective-permute-start | bytes 1179656 | tf_op jit(solution)/shard_map/ppermute | solution.py:195
  200.7 6.4 %collective-permute-done.16 = bf16[512,384]{1,0:T(8,128)(2,1)} collective-permute-done((bf16[512,384]{1,0:T(8,128)(2,1)}, bf16[512,384]{1,0:T(8,128)(2,1)}, u32[]{:S(2)}, u32[]{:S(2)}) %collective-permute-start.16) | collective-permute-done | bytes 393248 | tf_op jit(solution)/shard_map/ppermute | solution.py:195
  207.1 5.4 %collective-permute-done.17 = bf16[512,384]{1,0:T(8,128)(2,1)} collective-permute-done((bf16[512,384]{1,0:T(8,128)(2,1)}, bf16[512,384]{1,0:T(8,128)(2,1)}, u32[]{:S(2)}, u32[]{:S(2)}) %collective-permute-start.17) | collective-permute-done | bytes 393248 | tf_op jit(solution)/shard_map/ppermute | solution.py:195
  (80 shorter events, 55.3 us)
Async XLA Ops:
  1.2 24.1 %copy-start.2 = (bf16[384,512]{0,1:T(8,128)(2,1)}, bf16[384,512]{0,1:T(8,128)(2,1)S(1)}, u32[]{:S(2)}) copy-start(bf16[384,512]{0,1:T(8,128)(2,1)S(1)} %copy.15) | copy-start | bytes 1179652
  2.2 23.1 %copy-start.4 = (bf16[528,384]{1,0:T(8,128)(2,1)}, bf16[528,384]{1,0:T(8,128)(2,1)S(1)}, u32[]{:S(2)}) copy-start(bf16[528,384]{1,0:T(8,128)(2,1)S(1)} %fusion.16.rest_0_) | copy-start | bytes 1216516
  2.2 97.2 %collective-permute-start.1 = (bf16[528,384]{1,0:T(8,128)(2,1)S(1)}, bf16[528,384]{1,0:T(8,128)(2,1)}, u32[]{:S(2)}, u32[]{:S(2)}) collective-permute-start(bf16[528,384]{1,0:T(8,128)(2,1)S(1)} %fusion.16.rest_0_), channel_id=1, source_target_pairs={{0,8},{8,16},{16,24},{24,0},{1,9},{9,17},{17,25},{25,1},{2,10},{10... | collective-permute-start | bytes 1216520 | tf_op jit(solution)/shard_map/ppermute | solution.py:148
  5.7 97.7 %collective-permute-start.2 = (bf16[528,384]{1,0:T(8,128)(2,1)S(1)}, bf16[528,384]{1,0:T(8,128)(2,1)}, u32[]{:S(2)}, u32[]{:S(2)}) collective-permute-start(bf16[528,384]{1,0:T(8,128)(2,1)S(1)} %fusion.16.rest_0_), channel_id=1, source_target_pairs={{0,16},{8,24},{16,0},{24,8},{1,17},{9,25},{17,1},{25,9},{2,18},{10... | collective-permute-start | bytes 1216520 | tf_op jit(solution)/shard_map/ppermute | solution.py:148
  10.5 96.9 %collective-permute-start.3 = (bf16[528,384]{1,0:T(8,128)(2,1)S(1)}, bf16[528,384]{1,0:T(8,128)(2,1)}, u32[]{:S(2)}, u32[]{:S(2)}) collective-permute-start(bf16[528,384]{1,0:T(8,128)(2,1)S(1)} %fusion.16.rest_0_), channel_id=1, source_target_pairs={{0,24},{8,0},{16,8},{24,16},{1,25},{9,1},{17,9},{25,17},{2,26},{10... | collective-permute-start | bytes 1216520 | tf_op jit(solution)/shard_map/ppermute | solution.py:148
  15.4 13.9 %all-to-all-start = ((bf16[4,96,256]{2,1,0:T(8,128)(2,1)}), bf16[4,96,256]{2,1,0:T(8,128)(2,1)S(1)}, u32[]{:S(2)}, u32[]{:S(2)}) async-start(bf16[4,96,256]{2,1,0:T(8,128)(2,1)} %bitcast.11), calls=%async_computation | async-start | bytes 393216 | tf_op jit(solution)/shard_map/all_to_all | solution.py:133
  29.3 29.6 %collective-permute-start.4 = (bf16[4,96,256]{2,1,0:T(8,128)(2,1)S(1)}, bf16[4,96,256]{2,1,0:T(8,128)(2,1)S(1)}, u32[]{:S(2)}, u32[]{:S(2)}) collective-permute-start(bf16[4,96,256]{2,1,0:T(8,128)(2,1)S(1)} %all-to-all-done), channel_id=1, source_target_pairs={{0,256},{32,288},{64,320},{96,352},{128,384},{160,416},{192,448},{... | collective-permute-start | bytes 589832 | tf_op jit(solution)/shard_map/ppermute | solution.py:134
  54.4 58.4 %copy-start.11 = (s32[3]{0:T(128)S(1)}, s32[3]{0:T(128)}, u32[]{:S(2)}) copy-start(s32[3]{0:T(128)} %constant.127) | copy-start | bytes 40
  54.4 58.4 %copy-start = (s32[16]{0:T(128)S(1)}, s32[16]{0:T(128)}, u32[]{:S(2)}) copy-start(s32[16]{0:T(128)} %constant.118.clone) | copy-start | bytes 196
  54.4 14.5 %collective-permute-start.5 = (bf16[4,96,256]{2,1,0:T(8,128)(2,1)S(1)}, bf16[4,96,256]{2,1,0:T(8,128)(2,1)S(1)}, u32[]{:S(2)}, u32[]{:S(2)}) collective-permute-start(bf16[4,96,256]{2,1,0:T(8,128)(2,1)S(1)} %all-to-all-done), channel_id=1, source_target_pairs={{0,128},{32,160},{64,192},{96,224},{128,256},{160,288},{192,320},{... | collective-permute-start | bytes 589832 | tf_op jit(solution)/shard_map/ppermute | solution.py:135
  59.6 123.2 %collective-permute-start = (bf16[512,4,512]{2,0,1:T(8,128)(2,1)}, bf16[512,4,512]{2,0,1:T(8,128)(2,1)}, u32[]{:S(2)}, u32[]{:S(2)}) collective-permute-start(bf16[512,4,512]{2,0,1:T(8,128)(2,1)} %bitcast.32), channel_id=1, source_target_pairs={{0,1},{1,0},{2,3},{3,2},{4,5},{5,4},{6,7},{7,6},{8,9},{9,8},{10,11... | collective-permute-start | bytes 6291464 | tf_op jit(solution)/shard_map/ppermute | solution.py:185
  68.9 24.5 %collective-permute-start.6 = (bf16[4,96,256]{2,1,0:T(8,128)(2,1)S(1)}, bf16[4,96,256]{2,1,0:T(8,128)(2,1)S(1)}, u32[]{:S(2)}, u32[]{:S(2)}) collective-permute-start(bf16[4,96,256]{2,1,0:T(8,128)(2,1)S(1)} %all-to-all-done), channel_id=1, source_target_pairs={{0,384},{32,416},{64,448},{96,480},{128,0},{160,32},{192,64},{224,... | collective-permute-start | bytes 589832 | tf_op jit(solution)/shard_map/ppermute | solution.py:136
  93.4 44.8 %copy-start.1 = (bf16[16,96,256]{2,1,0:T(8,128)(2,1)}, bf16[16,96,256]{2,1,0:T(8,128)(2,1)S(1)}, u32[]{:S(2)}) copy-start(bf16[16,96,256]{2,1,0:T(8,128)(2,1)S(1)} %constant_dynamic-update-slice_fusion.a0) | copy-start | bytes 2359300
  93.5 44.8 %collective-permute-start.7 = (bf16[16,96,256]{2,1,0:T(8,128)(2,1)S(1)}, bf16[16,96,256]{2,1,0:T(8,128)(2,1)}, u32[]{:S(2)}, u32[]{:S(2)}) collective-permute-start(bf16[16,96,256]{2,1,0:T(8,128)(2,1)S(1)} %constant_dynamic-update-slice_fusion.a0), channel_id=1, source_target_pairs={{0,32},{32,64},{64,96},{96,128},{128,160},{160,192},{192,224},{224... | collective-permute-start | bytes 2359304 | tf_op jit(solution)/shard_map/ppermute | solution.py:138
  99.3 38.9 %collective-permute-start.8 = (bf16[16,96,256]{2,1,0:T(8,128)(2,1)S(1)}, bf16[16,96,256]{2,1,0:T(8,128)(2,1)}, u32[]{:S(2)}, u32[]{:S(2)}) collective-permute-start(bf16[16,96,256]{2,1,0:T(8,128)(2,1)S(1)} %constant_dynamic-update-slice_fusion.a0), channel_id=1, source_target_pairs={{0,480},{32,0},{64,32},{96,64},{128,96},{160,128},{192,160},{224,1... | collective-permute-start | bytes 2359304 | tf_op jit(solution)/shard_map/ppermute | solution.py:139
  103.4 34.8 %collective-permute-start.10 = (bf16[8,96,256]{2,1,0:T(8,128)(2,1)}, bf16[8,96,256]{2,1,0:T(8,128)(2,1)}, u32[]{:S(2)}, u32[]{:S(2)}) collective-permute-start(bf16[8,96,256]{2,1,0:T(8,128)(2,1)} %get-tuple-element.23), channel_id=1, source_target_pairs={{0,448},{32,480},{64,0},{96,32},{128,64},{160,96},{192,128},{224,1... | collective-permute-start | bytes 1179656 | tf_op jit(solution)/shard_map/ppermute | solution.py:141
  107.4 30.8 %collective-permute-start.9 = (bf16[8,96,256]{2,1,0:T(8,128)(2,1)}, bf16[8,96,256]{2,1,0:T(8,128)(2,1)S(1)}, u32[]{:S(2)}, u32[]{:S(2)}) collective-permute-start(bf16[8,96,256]{2,1,0:T(8,128)(2,1)} %get-tuple-element.24), channel_id=1, source_target_pairs={{0,64},{32,96},{64,128},{96,160},{128,192},{160,224},{192,256},{22... | collective-permute-start | bytes 1179656 | tf_op jit(solution)/shard_map/ppermute | solution.py:140
  147.0 22.3 %collective-permute-start.11 = (bf16[528,384]{1,0:T(8,128)(2,1)}, bf16[528,384]{1,0:T(8,128)(2,1)S(1)}, u32[]{:S(2)}, u32[]{:S(2)}) collective-permute-start(bf16[528,384]{1,0:T(8,128)(2,1)} %get-tuple-element.12), channel_id=1, source_target_pairs={{0,24},{8,0},{16,8},{24,16},{1,25},{9,1},{17,9},{25,17},{2,26},{10... | collective-permute-start | bytes 1216520 | tf_op jit(solution)/shard_map/ppermute | solution.py:172
  152.6 16.7 %collective-permute-start.12 = (bf16[528,384]{1,0:T(8,128)(2,1)}, bf16[528,384]{1,0:T(8,128)(2,1)S(1)}, u32[]{:S(2)}, u32[]{:S(2)}) collective-permute-start(bf16[528,384]{1,0:T(8,128)(2,1)} %get-tuple-element.13), channel_id=1, source_target_pairs={{0,16},{8,24},{16,0},{24,8},{1,17},{9,25},{17,1},{25,9},{2,18},{10... | collective-permute-start | bytes 1216520 | tf_op jit(solution)/shard_map/ppermute | solution.py:171
  156.5 18.3 %collective-permute-start.13 = (bf16[528,384]{1,0:T(8,128)(2,1)}, bf16[528,384]{1,0:T(8,128)(2,1)S(1)}, u32[]{:S(2)}, u32[]{:S(2)}) collective-permute-start(bf16[528,384]{1,0:T(8,128)(2,1)} %get-tuple-element.14), channel_id=1, source_target_pairs={{0,8},{8,16},{16,24},{24,0},{1,9},{9,17},{17,25},{25,1},{2,10},{10... | collective-permute-start | bytes 1216520 | tf_op jit(solution)/shard_map/ppermute | solution.py:173
  178.4 4.4 %collective-permute-start.14 = (bf16[512,384]{1,0:T(8,128)(2,1)}, bf16[512,384]{1,0:T(8,128)(2,1)S(1)}, u32[]{:S(2)}, u32[]{:S(2)}) collective-permute-start(bf16[512,384]{1,0:T(8,128)(2,1)} %shard_map.76), channel_id=1, source_target_pairs={{0,1},{1,0},{2,3},{3,2},{4,5},{5,4},{6,7},{7,6},{8,9},{9,8},{10,11... | collective-permute-start | bytes 1179656 | tf_op jit(solution)/shard_map/ppermute | solution.py:187
  185.6 15.1 %collective-permute-start.15 = (bf16[512,384]{1,0:T(8,128)(2,1)}, bf16[512,384]{1,0:T(8,128)(2,1)S(1)}, u32[]{:S(2)}, u32[]{:S(2)}) collective-permute-start(bf16[512,384]{1,0:T(8,128)(2,1)} %convolution_convert_fusion.2), channel_id=1, source_target_pairs={{0,4},{2,6},{4,0},{6,2},{1,5},{3,7},{5,1},{7,3},{8,12},{10,14},{12... | collective-permute-start | bytes 1179656 | tf_op jit(solution)/shard_map/ppermute | solution.py:195
  191.5 15.6 %collective-permute-start.16 = (bf16[512,384]{1,0:T(8,128)(2,1)}, bf16[512,384]{1,0:T(8,128)(2,1)}, u32[]{:S(2)}, u32[]{:S(2)}) collective-permute-start(bf16[512,384]{1,0:T(8,128)(2,1)} %convolution_convert_fusion.1), channel_id=1, source_target_pairs={{0,2},{2,4},{4,6},{6,0},{1,3},{3,5},{5,7},{7,1},{8,10},{10,12},{12... | collective-permute-start | bytes 1179656 | tf_op jit(solution)/shard_map/ppermute | solution.py:195
  198.0 14.4 %collective-permute-start.17 = (bf16[512,384]{1,0:T(8,128)(2,1)}, bf16[512,384]{1,0:T(8,128)(2,1)}, u32[]{:S(2)}, u32[]{:S(2)}) collective-permute-start(bf16[512,384]{1,0:T(8,128)(2,1)} %convolution_convert_fusion), channel_id=1, source_target_pairs={{0,6},{2,0},{4,2},{6,4},{1,7},{3,1},{5,3},{7,5},{8,14},{10,8},{12,... | collective-permute-start | bytes 1179656 | tf_op jit(solution)/shard_map/ppermute | solution.py:195
  (7 other events, 21.8 us)

commit v2 on v1

v2 whole, which is shorter than its diff:
```python
import math

import jax
import jax.numpy as jnp
from jax import lax
from jax.experimental import pallas as pl
from jax.experimental.pallas import tpu as pltpu
from jax.sharding import Mesh, PartitionSpec as P


HD = 128
HEADS = 4
HALF = HEADS * HD
TOP = 3
NZ, NY, NX = 16, 4, 4
TOK = 384
SL = TOK // NY
EXT = HALF + 16
LOG2E = 1.4426950408889634
COEF = LOG2E / math.sqrt(HD)
DEAD = -1e30
NONE = NZ * NY
SLOTS = (2, 10, 14, 7, 3, 11, 15, 4, 0, 8, 12, 5, 1, 9, 13, 6)


def pallas(mib, kernel, **kw):
    grant = pltpu.CompilerParams(vmem_limit_bytes=mib * 1024 * 1024)
    return pl.pallas_call(kernel, compiler_params=grant, **kw)


def send(a, axis, s):
    n = lax.axis_size(axis)
    return lax.ppermute(a, axis, [(i, (i + s) % n) for i in range(n)])


def tn(a, b):
    return lax.dot_general(a, b, (((0,), (0,)), ((), ())), preferred_element_type=jnp.float32)


def pack_kernel(k_ref, v_ref, out_ref):
    for y in range(NY):
        out_ref[y, :, :HD] = k_ref[y * SL : (y + 1) * SL, :]
        out_ref[y, :, HD:] = v_ref[y * SL : (y + 1) * SL, :]


def own_kernel(code_ref, q_ref, k_ref, v_ref, qx_ref, o_ref, lse_ref):
    keep = lax.broadcasted_iota(jnp.int32, (TOK, TOK), 0) <= lax.broadcasted_iota(
        jnp.int32, (TOK, TOK), 1
    )
    k = k_ref[...]
    v = v_ref[...]
    rows = []
    for h in range(HEADS):
        q = q_ref[:, h * HD : (h + 1) * HD].T
        qx_ref[h * HD : (h + 1) * HD, :] = q
        s = jnp.dot(k, q, preferred_element_type=jnp.float32)
        s = jnp.where(keep, s * COEF, DEAD)
        top = jnp.max(s, axis=0, keepdims=True)
        p = jnp.exp2(s - top)
        total = jnp.sum(p, axis=0, keepdims=True)
        o = tn(v, p.astype(jnp.bfloat16)) * (1.0 / total)
        o_ref[h * HD : (h + 1) * HD, :] = o.astype(jnp.bfloat16)
        rows.append(top + jnp.log2(total))
    lse_ref[...] = jnp.concatenate(rows + rows, axis=0)
    lane = lax.broadcasted_iota(jnp.int32, (16, TOK), 1)
    codes = jnp.zeros((16, TOK), jnp.float32)
    for i in range(HEADS * TOP):
        codes = jnp.where(lane == i, code_ref[i].astype(jnp.float32), codes)
    qx_ref[HALF:, :] = codes.astype(jnp.bfloat16)


def slices_of(code_ref, kv_ref, q_ref, o_ref, base):
    rows = []
    for h in range(HEADS):
        codes = [code_ref[base + h * TOP + j] for j in range(TOP)]
        picked = [kv_ref[jnp.minimum(c, NONE - 1)] for c in codes]
        bias = [jnp.where(c < NONE, 0.0, DEAD).astype(jnp.float32) for c in codes]
        k = jnp.concatenate([t[:, :HD] for t in picked], axis=0)
        v = jnp.concatenate([t[:, HD:] for t in picked], axis=0)
        s = jnp.dot(k, q_ref[h * HD : (h + 1) * HD, :], preferred_element_type=jnp.float32)
        s = [s[j * SL : (j + 1) * SL] * COEF + bias[j] for j in range(TOP)]
        s = jnp.concatenate(s, axis=0)
        top = jnp.max(s, axis=0, keepdims=True)
        p = jnp.exp2(s - top)
        total = jnp.sum(p, axis=0, keepdims=True)
        o = tn(v, p.astype(jnp.bfloat16)) * (1.0 / total)
        o_ref[h * HD : (h + 1) * HD, :] = o.astype(jnp.bfloat16)
        lse = top + jnp.log2(total)
        hi = lse.astype(jnp.bfloat16).astype(jnp.float32)
        mid = (lse - hi).astype(jnp.bfloat16).astype(jnp.float32)
        rows += [hi, mid, lse - hi - mid]
    rows += [jnp.zeros((4, TOK), jnp.float32)]
    o_ref[HALF:, :] = jnp.concatenate(rows, axis=0).astype(jnp.bfloat16)


def slices_kernel(code_ref, kv_ref, *rest):
    n = len(rest) // 2
    for i in range(n):
        slices_of(code_ref, kv_ref, rest[i], rest[n + i], i * HEADS * TOP)


def merge_kernel(own_ref, lse_ref, p0, p1, p2, p3, out_ref):
    parts = (p0, p1, p2, p3)
    tails = [p[HALF:, :].astype(jnp.float32) for p in parts]
    for h in range(HEADS):
        span = slice(h * HD, (h + 1) * HD)
        own = lse_ref[h : h + 1, :]
        lses = [
            t[3 * h : 3 * h + 1] + t[3 * h + 1 : 3 * h + 2] + t[3 * h + 2 : 3 * h + 3]
            for t in tails
        ]
        top = own
        for x in lses:
            top = jnp.maximum(top, x)
        w = jnp.exp2(own - top)
        total = w
        acc = w * own_ref[span, :].astype(jnp.float32)
        for p, x in zip(parts, lses):
            w = jnp.exp2(x - top)
            total = total + w
            acc = acc + w * p[span, :].astype(jnp.float32)
        out_ref[span, :] = (acc * (1.0 / total)).astype(jnp.bfloat16)


def turn_kernel(cols_ref, mine_ref, got_ref, out_ref):
    out_ref[0, :, :HALF] = mine_ref[...].T
    out_ref[0, :, HALF:] = got_ref[...].T


def piece_of(w_ref, s, mine_ref, got_ref):
    out = jnp.dot(w_ref[s, :, :HALF], mine_ref[...], preferred_element_type=jnp.float32)
    return out + jnp.dot(w_ref[s, :, HALF:], got_ref[...], preferred_element_type=jnp.float32)


def pieces_kernel(w_ref, mine_ref, got_ref, *outs):
    for s, out in zip((2, 1, 3), outs):
        out[...] = piece_of(w_ref, s, mine_ref, got_ref).astype(jnp.bfloat16)


def mine_kernel(w_ref, mine_ref, got_ref, out_ref):
    out_ref[...] = piece_of(w_ref, 0, mine_ref, got_ref)


def sum_kernel(mine_ref, g1, g2, g3, out_ref):
    out = mine_ref[...]
    for g in (g1, g2, g3):
        out += g[...].astype(jnp.float32)
    out_ref[...] = out.astype(jnp.bfloat16)


def bf16(*shape):
    return jax.ShapeDtypeStruct(shape, jnp.bfloat16)


def f32(*shape):
    return jax.ShapeDtypeStruct(shape, jnp.float32)


def steps(queries, keys, values, block_ids, out_weight):
    z = lax.axis_index("z")
    y = lax.axis_index("y")
    x = lax.axis_index("x")
    core = lax.axis_index("core")
    vmem = pl.BlockSpec(memory_space=pltpu.VMEM)
    smem = pl.BlockSpec(memory_space=pltpu.SMEM)
    packed = pallas(
        4, pack_kernel, in_specs=[vmem] * 2, out_specs=vmem, out_shape=bf16(NY, SL, 2 * HD)
    )(keys, values)
    row = lax.all_to_all(packed, "y", 0, 0)
    ids = block_ids.reshape(HEADS * TOP)
    slot = jnp.zeros_like(ids)
    offset = (ids // NY - z) % NZ
    for d, place in enumerate(SLOTS):
        slot = jnp.where(offset == d, place, slot)
    code = jnp.where(ids < z * NY + y, slot * NY + ids % NY, NONE)
    up = send(row, "z", 4)
    down = send(row, "z", -4)
    w_got = send(out_weight, "core", 1)
    qx, own, own_lse = pallas(
        8,
        own_kernel,
        in_specs=[smem] + [vmem] * 3,
        out_specs=[vmem] * 3,
        out_shape=[bf16(EXT, TOK), bf16(HALF, TOK), f32(2 * HEADS, TOK)],
    )(code, queries, keys, values)
    order = (2, 1, 3)
    qs = [send(qx, "y", s) for s in order]
    far1 = send(up[: NY // 2], "z", 4)
    far2 = send(down[NY // 2 :], "z", -4)
    c = jnp.concatenate([far1, far2, up, row, down], axis=0)
    n1 = send(c, "z", 1)
    n2 = send(c, "z", -1)
    codes = jnp.stack([a[HALF, : HEADS * TOP] for a in qs], axis=0).astype(jnp.int32).reshape(-1)
    cols = (x + jnp.arange(NX, dtype=jnp.int32)) % NX * 2 + core
    w = pallas(
        12,
        turn_kernel,
        grid_spec=pltpu.PrefetchScalarGridSpec(
            num_scalar_prefetch=1,
            grid=(NX,),
            in_specs=[pl.BlockSpec((HALF, HALF), lambda s, cols: (0, cols[s]))] * 2,
            out_specs=pl.BlockSpec((1, HALF, 2 * HALF), lambda s, cols: (s, 0, 0)),
        ),
        out_shape=bf16(NX, HALF, 2 * HALF),
    )(cols, out_weight, w_got)
    m1 = send(n1[NY : 3 * NY], "z", 1)
    m2 = send(n2[2 * NY :], "z", -1)
    kv = jnp.concatenate([c, n1, n2, m1, m2], axis=0)
    parts = pallas(
        12,
        slices_kernel,
        in_specs=[smem] + [vmem] * 4,
        out_specs=[vmem] * 3,
        out_shape=[bf16(EXT, TOK)] * 3,
    )(codes, kv, *qs)
    back = [send(o, "y", -s) for s, o in zip(order, parts)]
    (home,) = pallas(
        12,
        slices_kernel,
        in_specs=[smem] + [vmem] * 2,
        out_specs=[vmem],
        out_shape=[bf16(EXT, TOK)],
    )(code, kv, qx)
    att = pallas(
        8, merge_kernel, in_specs=[vmem] * 6, out_specs=vmem, out_shape=bf16(HALF, TOK)
    )(own, own_lse, home, *back)
    att_got = send(att, "core", 1)
    pieces = pallas(
        16,
        pieces_kernel,
        in_specs=[vmem] * 3,
        out_specs=[vmem] * 3,
        out_shape=[bf16(HALF, TOK)] * 3,
    )(w, att, att_got)
    got = [send(p, "x", s) for s, p in zip(order, pieces)]
    mine = pallas(
        12, mine_kernel, in_specs=[vmem] * 3, out_specs=vmem, out_shape=f32(HALF, TOK)
    )(w, att, att_got)
    return pallas(
        8, sum_kernel, in_specs=[vmem] * 4, out_specs=vmem, out_shape=bf16(HALF, TOK)
    )(mine, *got)


def solution(mesh):
    axes = ("z", "y", "x", "core")
    grid = Mesh(mesh.devices.reshape(NZ, NY, NX, 2), axes)
    rows, cols = axes[:2], axes[2:]
    return jax.shard_map(
        steps,
        mesh=grid,
        in_specs=(P(rows, cols), P(rows, cols), P(rows, cols), P(rows, cols, None), P(cols, None)),
        out_specs=P(cols, rows),
        check_vma=False,
    )
```

time: 217 us -> 184 us (0.85)
  the two profiles are of different devices: /device:TPU:70 before, /device:TPU:1 now
where the time goes in v2:
time: 184 us; the launch traced here: 182 us
  starting transfers between devices  82.6 us (45%)
  waiting for transfers between devices  52.3 us (28%)
  local copies, waits for them, and re-layouts  21.7 us (12%)
  Pallas kernels  16.4 us (9%)
  blocking collectives  8.41 us (5%)
    ppermute x19, starting transfers between devices, send(): return lax.ppermute(a, axis, [(i, (i + s) % n) for i in range(n)])  82.6 us
    ppermute x19, waiting for transfers between devices, send(): return lax.ppermute(a, axis, [(i, (i + s) % n) for i in range(n)])  52.3 us
    unnamed x44, local copies, waits for them, and re-layouts  15 us
    all_to_all x1, blocking collectives, steps(): row = lax.all_to_all(packed, 'y', 0, 0)  8.41 us
    pallas_call x1, Pallas kernels, steps(): pallas(12, slices_kernel, in_specs=[smem] + [vmem] * 4, out_specs=[vmem]...  4.63 us
    pallas_call x1, Pallas kernels, steps(): pallas(12, turn_kernel, grid_spec=pltpu.PrefetchScalarGridSpec(num_scalar...  3.88 us
  transfers between devices with their start and end apart: 19, of which 11 were waited for; matrix products, arithmetic and copies ran while one was open for 7% of the time, Pallas kernels for 8%

profile of v2, /device:TPU:1, one launch (start us, length us, event | category | flops | bytes accessed | tf_op | source)
XLA Modules:
  0.0 182.4 jit_solution(11906545760909423688)
XLA Ops:
  0.0 8.9 %collective-permute-start = (bf16[512,4096]{1,0:T(8,128)(2,1)}, bf16[512,4096]{1,0:T(8,128)(2,1)}, u32[]{:S(2)}, u32[]{:S(2)}) collective-permute-start(bf16[512,4096]{1,0:T(8,128)(2,1)} %mine_ref.1), channel_id=1, source_target_pairs={{0,1},{1,0},{2,3},{3,2},{4,5},{5,4},{6,7},{7,6},{8,9},{9,8},{10,11... | collective-permute-start | bytes 12582920 | tf_op jit(solution)/shard_map/ppermute | solution.py:33
  10.7 8.4 %all_to_all.5 = bf16[4,96,256]{2,1,0:T(8,128)(2,1)S(1)} all-to-all(bf16[4,96,256]{2,1,0:T(8,128)(2,1)S(1)} %shard_map.57), channel_id=1, replica_groups=mesh['z'=16,'y'=4,'x'=4,'core'=2] {'y'}, dimensions={0} | all-to-all | bytes 393216 | tf_op jit(solution)/shard_map/all_to_all | solution.py:169
  19.1 4.5 %collective-permute-start.1 = (bf16[4,96,256]{2,1,0:T(8,128)(2,1)S(1)}, bf16[4,96,256]{2,1,0:T(8,128)(2,1)S(1)}, u32[]{:S(2)}, u32[]{:S(2)}) collective-permute-start(bf16[4,96,256]{2,1,0:T(8,128)(2,1)S(1)} %all_to_all.5), channel_id=1, source_target_pairs={{0,128},{32,160},{64,192},{96,224},{128,256},{160,288},{192,320},{... | collective-permute-start | bytes 589832 | tf_op jit(solution)/shard_map/ppermute | solution.py:33
  23.6 5.6 %collective-permute-start.3 = (bf16[4,96,256]{2,1,0:T(8,128)(2,1)S(1)}, bf16[4,96,256]{2,1,0:T(8,128)(2,1)S(1)}, u32[]{:S(2)}, u32[]{:S(2)}) collective-permute-start(bf16[4,96,256]{2,1,0:T(8,128)(2,1)S(1)} %all_to_all.5), channel_id=1, source_target_pairs={{0,384},{32,416},{64,448},{96,480},{128,0},{160,32},{192,64},{224,... | collective-permute-start | bytes 589832 | tf_op jit(solution)/shard_map/ppermute | solution.py:33
  31.3 17.7 %collective-permute-start.2 = (bf16[2,96,256]{2,1,0:T(8,128)(2,1)S(1)}, bf16[2,96,256]{2,1,0:T(8,128)(2,1)S(1)}, u32[]{:S(2)}, u32[]{:S(2)}) collective-permute-start(bf16[2,96,256]{2,1,0:T(8,128)(2,1)S(1)} %slice.28), channel_id=1, source_target_pairs={{0,128},{32,160},{64,192},{96,224},{128,256},{160,288},{192,320},{... | collective-permute-start | bytes 294920 | tf_op jit(solution)/shard_map/ppermute | solution.py:33
  50.1 4.1 %collective-permute-start.4 = (bf16[2,96,256]{2,1,0:T(8,128)(2,1)S(1)}, bf16[2,96,256]{2,1,0:T(8,128)(2,1)S(1)}, u32[]{:S(2)}, u32[]{:S(2)}) collective-permute-start(bf16[2,96,256]{2,1,0:T(8,128)(2,1)S(1)} %slice.29), channel_id=1, source_target_pairs={{0,384},{32,416},{64,448},{96,480},{128,0},{160,32},{192,64},{224,... | collective-permute-start | bytes 294920 | tf_op jit(solution)/shard_map/ppermute | solution.py:33
  54.8 9.1 %collective-permute-done.4 = bf16[2,96,256]{2,1,0:T(8,128)(2,1)S(1)} collective-permute-done((bf16[2,96,256]{2,1,0:T(8,128)(2,1)S(1)}, bf16[2,96,256]{2,1,0:T(8,128)(2,1)S(1)}, u32[]{:S(2)}, u32[]{:S(2)}) %collective-permute-start.4) | collective-permute-done | bytes 98336 | tf_op jit(solution)/shard_map/ppermute | solution.py:33
  68.7 5.2 %collective-permute-start.6 = (bf16[16,96,256]{2,1,0:T(8,128)(2,1)}, bf16[16,96,256]{2,1,0:T(8,128)(2,1)}, u32[]{:S(2)}, u32[]{:S(2)}) collective-permute-start(bf16[16,96,256]{2,1,0:T(8,128)(2,1)} %get-tuple-element.23), channel_id=1, source_target_pairs={{0,480},{32,0},{64,32},{96,64},{128,96},{160,128},{192,160},{224,1... | collective-permute-start | bytes 2359304 | tf_op jit(solution)/shard_map/ppermute | solution.py:33
  79.4 2.7 %collective-permute-start.9 = (bf16[528,384]{1,0:T(8,128)(2,1)S(1)}, bf16[528,384]{1,0:T(8,128)(2,1)S(1)}, u32[]{:S(2)}, u32[]{:S(2)}) collective-permute-start(bf16[528,384]{1,0:T(8,128)(2,1)S(1)} %get-tuple-element.16.rest_0_), channel_id=1, source_target_pairs={{0,16},{8,24},{16,0},{24,8},{1,17},{9,25},{17,1},{25,9},{2,18},{10... | collective-permute-start | bytes 1216520 | tf_op jit(solution)/shard_map/ppermute | solution.py:33
  84.6 5.1 %collective-permute-done.5 = bf16[16,96,256]{2,1,0:T(8,128)(2,1)} collective-permute-done((bf16[16,96,256]{2,1,0:T(8,128)(2,1)}, bf16[16,96,256]{2,1,0:T(8,128)(2,1)}, u32[]{:S(2)}, u32[]{:S(2)}) %collective-permute-start.5) | collective-permute-done | bytes 786464 | tf_op jit(solution)/shard_map/ppermute | solution.py:33
  89.7 2.8 %collective-permute-start.11 = (bf16[528,384]{1,0:T(8,128)(2,1)S(1)}, bf16[528,384]{1,0:T(8,128)(2,1)S(1)}, u32[]{:S(2)}, u32[]{:S(2)}) collective-permute-start(bf16[528,384]{1,0:T(8,128)(2,1)S(1)} %get-tuple-element.16.rest_0_), channel_id=1, source_target_pairs={{0,24},{8,0},{16,8},{24,16},{1,25},{9,1},{17,9},{25,17},{2,26},{10... | collective-permute-start | bytes 1216520 | tf_op jit(solution)/shard_map/ppermute | solution.py:33
  96.3 6.6 %collective-permute-done.10.rest_1_ = bf16[528,384]{1,0:T(8,128)(2,1)S(1)} collective-permute-done((bf16[528,384]{1,0:T(8,128)(2,1)S(1)}, bf16[528,384]{1,0:T(8,128)(2,1)S(1)}, u32[]{:S(2)}, u32[]{:S(2)}) %collective-permute-start.10) | collective-permute-done | bytes 405536 | tf_op jit(solution)/shard_map/ppermute | solution.py:33
  106.2 3.2 %collective-permute-start.8 = (bf16[8,96,256]{2,1,0:T(8,128)(2,1)}, bf16[8,96,256]{2,1,0:T(8,128)(2,1)}, u32[]{:S(2)}, u32[]{:S(2)}) collective-permute-start(bf16[8,96,256]{2,1,0:T(8,128)(2,1)} %slice.31), channel_id=1, source_target_pairs={{0,480},{32,0},{64,32},{96,64},{128,96},{160,128},{192,160},{224,1... | collective-permute-start | bytes 1179656 | tf_op jit(solution)/shard_map/ppermute | solution.py:33
  114.8 3.9 %collective-permute-done.8 = bf16[8,96,256]{2,1,0:T(8,128)(2,1)} collective-permute-done((bf16[8,96,256]{2,1,0:T(8,128)(2,1)}, bf16[8,96,256]{2,1,0:T(8,128)(2,1)}, u32[]{:S(2)}, u32[]{:S(2)}) %collective-permute-start.8) | collective-permute-done | bytes 393248 | tf_op jit(solution)/shard_map/ppermute | solution.py:33
  119.8 4.6 %shard_map.59 = (bf16[528,384]{1,0:T(8,128)(2,1)S(1)}, bf16[528,384]{1,0:T(8,128)(2,1)S(1)}, bf16[528,384]{1,0:T(8,128)(2,1)S(1)}) custom-call(s32[36]{0:T(128)S(1)} %copy-done.16, bf16[64,96,256]{2,1,0:T(8,128)(2,1)S(1)} %constant_dynamic-update-slice_fusion.5.kv_ref, bf16[528,384]{1,0:T(8,128)(2,1)S(1)} %collective-permute-done.9.rest_0_, ...), custom_call_target="tpu_custom_call" | custom-call | tf_op jit(solution)/shard_map/pallas_call | solution.py:209
  124.4 2.7 %collective-permute-start.12 = (bf16[528,384]{1,0:T(8,128)(2,1)S(1)}, bf16[528,384]{1,0:T(8,128)(2,1)S(1)}, u32[]{:S(2)}, u32[]{:S(2)}) collective-permute-start(bf16[528,384]{1,0:T(8,128)(2,1)S(1)} %get-tuple-element.17), channel_id=1, source_target_pairs={{0,16},{8,24},{16,0},{24,8},{1,17},{9,25},{17,1},{25,9},{2,18},{10... | collective-permute-start | bytes 1216520 | tf_op jit(solution)/shard_map/ppermute | solution.py:33
  129.1 3.4 %collective-permute-start.14 = (bf16[528,384]{1,0:T(8,128)(2,1)S(1)}, bf16[528,384]{1,0:T(8,128)(2,1)S(1)}, u32[]{:S(2)}, u32[]{:S(2)}) collective-permute-start(bf16[528,384]{1,0:T(8,128)(2,1)S(1)} %get-tuple-element.19), channel_id=1, source_target_pairs={{0,8},{8,16},{16,24},{24,0},{1,9},{9,17},{17,25},{25,1},{2,10},{10... | collective-permute-start | bytes 1216520 | tf_op jit(solution)/shard_map/ppermute | solution.py:33
  134.4 3.1 %collective-permute-done.12.p1 = bf16[528,384]{1,0:T(8,128)(2,1)S(1)} collective-permute-done((bf16[528,384]{1,0:T(8,128)(2,1)S(1)}, bf16[528,384]{1,0:T(8,128)(2,1)S(1)}, u32[]{:S(2)}, u32[]{:S(2)}) %collective-permute-start.12) | collective-permute-done | bytes 405536 | tf_op jit(solution)/shard_map/ppermute | solution.py:33
  137.5 5.5 %collective-permute-done.13.p2 = bf16[528,384]{1,0:T(8,128)(2,1)S(1)} collective-permute-done((bf16[528,384]{1,0:T(8,128)(2,1)S(1)}, bf16[528,384]{1,0:T(8,128)(2,1)S(1)}, u32[]{:S(2)}, u32[]{:S(2)}) %collective-permute-start.13) | collective-permute-done | bytes 405536 | tf_op jit(solution)/shard_map/ppermute | solution.py:33
  143.0 4.7 %collective-permute-done.14.p3 = bf16[528,384]{1,0:T(8,128)(2,1)S(1)} collective-permute-done((bf16[528,384]{1,0:T(8,128)(2,1)S(1)}, bf16[528,384]{1,0:T(8,128)(2,1)S(1)}, u32[]{:S(2)}, u32[]{:S(2)}) %collective-permute-start.14) | collective-permute-done | bytes 405536 | tf_op jit(solution)/shard_map/ppermute | solution.py:33
  152.9 3.9 %shard_map.55.w_ref = bf16[4,512,1024]{2,1,0:T(8,128)(2,1)S(1)} custom-call(s32[4]{0:T(128)S(1)} %fusion.2.cols_ref, bf16[512,4096]{1,0:T(8,128)(2,1)S(1)} %copy-done, bf16[512,4096]{1,0:T(8,128)(2,1)} %collective-permute-done.got_ref), custom_call_target="tpu_custom_call" | custom-call | tf_op jit(solution)/shard_map/pallas_call | solution.py:195
  158.6 4.7 %collective-permute-start.16 = (bf16[512,384]{1,0:T(8,128)(2,1)S(1)}, bf16[512,384]{1,0:T(8,128)(2,1)S(1)}, u32[]{:S(2)}, u32[]{:S(2)}) collective-permute-start(bf16[512,384]{1,0:T(8,128)(2,1)S(1)} %get-tuple-element.20), channel_id=1, source_target_pairs={{0,4},{2,6},{4,0},{6,2},{1,5},{3,7},{5,1},{7,3},{8,12},{10,14},{12... | collective-permute-start | bytes 1179656 | tf_op jit(solution)/shard_map/ppermute | solution.py:33
  165.5 4.3 %collective-permute-start.18 = (bf16[512,384]{1,0:T(8,128)(2,1)S(1)}, bf16[512,384]{1,0:T(8,128)(2,1)S(1)}, u32[]{:S(2)}, u32[]{:S(2)}) collective-permute-start(bf16[512,384]{1,0:T(8,128)(2,1)S(1)} %get-tuple-element.22), channel_id=1, source_target_pairs={{0,6},{2,0},{4,2},{6,4},{1,7},{3,1},{5,3},{7,5},{8,14},{10,8},{12,... | collective-permute-start | bytes 1179656 | tf_op jit(solution)/shard_map/ppermute | solution.py:33
  172.7 8.8 %collective-permute-done.17.g2 = bf16[512,384]{1,0:T(8,128)(2,1)S(1)} collective-permute-done((bf16[512,384]{1,0:T(8,128)(2,1)S(1)}, bf16[512,384]{1,0:T(8,128)(2,1)S(1)}, u32[]{:S(2)}, u32[]{:S(2)}) %collective-permute-start.17) | collective-permute-done | bytes 393248 | tf_op jit(solution)/shard_map/ppermute | solution.py:33
  (82 shorter events, 48.5 us)
Async XLA Ops:
  0.0 74.2 %copy-start.9 = (bf16[384,512]{1,0:T(8,128)(2,1)S(1)}, bf16[384,512]{1,0:T(8,128)(2,1)}, u32[]{:S(2)}) copy-start(bf16[384,512]{1,0:T(8,128)(2,1)} %q_ref.1) | copy-start | bytes 1179652
  0.0 150.7 %collective-permute-start = (bf16[512,4096]{1,0:T(8,128)(2,1)}, bf16[512,4096]{1,0:T(8,128)(2,1)}, u32[]{:S(2)}, u32[]{:S(2)}) collective-permute-start(bf16[512,4096]{1,0:T(8,128)(2,1)} %mine_ref.1), channel_id=1, source_target_pairs={{0,1},{1,0},{2,3},{3,2},{4,5},{5,4},{6,7},{7,6},{8,9},{9,8},{10,11... | collective-permute-start | bytes 12582920 | tf_op jit(solution)/shard_map/ppermute | solution.py:33
  10.7 63.3 %copy-start.17 = (s32[1,4,3]{1,0,2:T(1,128)S(1)}, s32[1,4,3]{1,0,2:T(1,128)}, u32[]{:S(2)}) copy-start(s32[1,4,3]{1,0,2:T(1,128)} %param.8) | copy-start | bytes 148
  19.1 12.2 %collective-permute-start.1 = (bf16[4,96,256]{2,1,0:T(8,128)(2,1)S(1)}, bf16[4,96,256]{2,1,0:T(8,128)(2,1)S(1)}, u32[]{:S(2)}, u32[]{:S(2)}) collective-permute-start(bf16[4,96,256]{2,1,0:T(8,128)(2,1)S(1)} %all_to_all.5), channel_id=1, source_target_pairs={{0,128},{32,160},{64,192},{96,224},{128,256},{160,288},{192,320},{... | collective-permute-start | bytes 589832 | tf_op jit(solution)/shard_map/ppermute | solution.py:33
  23.6 26.4 %collective-permute-start.3 = (bf16[4,96,256]{2,1,0:T(8,128)(2,1)S(1)}, bf16[4,96,256]{2,1,0:T(8,128)(2,1)S(1)}, u32[]{:S(2)}, u32[]{:S(2)}) collective-permute-start(bf16[4,96,256]{2,1,0:T(8,128)(2,1)S(1)} %all_to_all.5), channel_id=1, source_target_pairs={{0,384},{32,416},{64,448},{96,480},{128,0},{160,32},{192,64},{224,... | collective-permute-start | bytes 589832 | tf_op jit(solution)/shard_map/ppermute | solution.py:33
  31.3 22.8 %collective-permute-start.2 = (bf16[2,96,256]{2,1,0:T(8,128)(2,1)S(1)}, bf16[2,96,256]{2,1,0:T(8,128)(2,1)S(1)}, u32[]{:S(2)}, u32[]{:S(2)}) collective-permute-start(bf16[2,96,256]{2,1,0:T(8,128)(2,1)S(1)} %slice.28), channel_id=1, source_target_pairs={{0,128},{32,160},{64,192},{96,224},{128,256},{160,288},{192,320},{... | collective-permute-start | bytes 294920 | tf_op jit(solution)/shard_map/ppermute | solution.py:33
  50.1 13.9 %collective-permute-start.4 = (bf16[2,96,256]{2,1,0:T(8,128)(2,1)S(1)}, bf16[2,96,256]{2,1,0:T(8,128)(2,1)S(1)}, u32[]{:S(2)}, u32[]{:S(2)}) collective-permute-start(bf16[2,96,256]{2,1,0:T(8,128)(2,1)S(1)} %slice.29), channel_id=1, source_target_pairs={{0,384},{32,416},{64,448},{96,480},{128,0},{160,32},{192,64},{224,... | collective-permute-start | bytes 294920 | tf_op jit(solution)/shard_map/ppermute | solution.py:33
  66.8 23.0 %collective-permute-start.5 = (bf16[16,96,256]{2,1,0:T(8,128)(2,1)}, bf16[16,96,256]{2,1,0:T(8,128)(2,1)}, u32[]{:S(2)}, u32[]{:S(2)}) collective-permute-start(bf16[16,96,256]{2,1,0:T(8,128)(2,1)} %get-tuple-element.23), channel_id=1, source_target_pairs={{0,32},{32,64},{64,96},{96,128},{128,160},{160,192},{192,224},{224... | collective-permute-start | bytes 2359304 | tf_op jit(solution)/shard_map/ppermute | solution.py:33
  68.7 35.7 %collective-permute-start.6 = (bf16[16,96,256]{2,1,0:T(8,128)(2,1)}, bf16[16,96,256]{2,1,0:T(8,128)(2,1)}, u32[]{:S(2)}, u32[]{:S(2)}) collective-permute-start(bf16[16,96,256]{2,1,0:T(8,128)(2,1)} %get-tuple-element.23), channel_id=1, source_target_pairs={{0,480},{32,0},{64,32},{96,64},{128,96},{160,128},{192,160},{224,1... | collective-permute-start | bytes 2359304 | tf_op jit(solution)/shard_map/ppermute | solution.py:33
  79.4 24.3 %copy-start.5 = (bf16[528,384]{1,0:T(8,128)(2,1)}, bf16[528,384]{1,0:T(8,128)(2,1)S(1)}, u32[]{:S(2)}) copy-start(bf16[528,384]{1,0:T(8,128)(2,1)S(1)} %get-tuple-element.16.rest_0_) | copy-start | bytes 1216516
  79.4 15.0 %collective-permute-start.9 = (bf16[528,384]{1,0:T(8,128)(2,1)S(1)}, bf16[528,384]{1,0:T(8,128)(2,1)S(1)}, u32[]{:S(2)}, u32[]{:S(2)}) collective-permute-start(bf16[528,384]{1,0:T(8,128)(2,1)S(1)} %get-tuple-element.16.rest_0_), channel_id=1, source_target_pairs={{0,16},{8,24},{16,0},{24,8},{1,17},{9,25},{17,1},{25,9},{2,18},{10... | collective-permute-start | bytes 1216520 | tf_op jit(solution)/shard_map/ppermute | solution.py:33
  82.1 20.7 %collective-permute-start.10 = (bf16[528,384]{1,0:T(8,128)(2,1)S(1)}, bf16[528,384]{1,0:T(8,128)(2,1)S(1)}, u32[]{:S(2)}, u32[]{:S(2)}) collective-permute-start(bf16[528,384]{1,0:T(8,128)(2,1)S(1)} %get-tuple-element.16.rest_0_), channel_id=1, source_target_pairs={{0,8},{8,16},{16,24},{24,0},{1,9},{9,17},{17,25},{25,1},{2,10},{10... | collective-permute-start | bytes 1216520 | tf_op jit(solution)/shard_map/ppermute | solution.py:33
  89.7 13.9 %collective-permute-start.11 = (bf16[528,384]{1,0:T(8,128)(2,1)S(1)}, bf16[528,384]{1,0:T(8,128)(2,1)S(1)}, u32[]{:S(2)}, u32[]{:S(2)}) collective-permute-start(bf16[528,384]{1,0:T(8,128)(2,1)S(1)} %get-tuple-element.16.rest_0_), channel_id=1, source_target_pairs={{0,24},{8,0},{16,8},{24,16},{1,25},{9,1},{17,9},{25,17},{2,26},{10... | collective-permute-start | bytes 1216520 | tf_op jit(solution)/shard_map/ppermute | solution.py:33
  94.3 19.3 %collective-permute-start.7 = (bf16[8,96,256]{2,1,0:T(8,128)(2,1)}, bf16[8,96,256]{2,1,0:T(8,128)(2,1)}, u32[]{:S(2)}, u32[]{:S(2)}) collective-permute-start(bf16[8,96,256]{2,1,0:T(8,128)(2,1)} %slice.30), channel_id=1, source_target_pairs={{0,32},{32,64},{64,96},{96,128},{128,160},{160,192},{192,224},{224... | collective-permute-start | bytes 1179656 | tf_op jit(solution)/shard_map/ppermute | solution.py:33
  106.2 12.5 %collective-permute-start.8 = (bf16[8,96,256]{2,1,0:T(8,128)(2,1)}, bf16[8,96,256]{2,1,0:T(8,128)(2,1)}, u32[]{:S(2)}, u32[]{:S(2)}) collective-permute-start(bf16[8,96,256]{2,1,0:T(8,128)(2,1)} %slice.31), channel_id=1, source_target_pairs={{0,480},{32,0},{64,32},{96,64},{128,96},{160,128},{192,160},{224,1... | collective-permute-start | bytes 1179656 | tf_op jit(solution)/shard_map/ppermute | solution.py:33
  119.7 28.1 %copy-start.8 = (bf16[512,384]{1,0:T(8,128)(2,1)S(1)}, bf16[512,384]{1,0:T(8,128)(2,1)}, u32[]{:S(2)}) copy-start(bf16[512,384]{1,0:T(8,128)(2,1)} %copy-done.7) | copy-start | bytes 1179652
  119.7 28.0 %copy-start.15 = (f32[8,384]{1,0:T(8,128)S(1)}, f32[8,384]{1,0:T(8,128)}, u32[]{:S(2)}) copy-start(f32[8,384]{1,0:T(8,128)} %copy-done.14) | copy-start | bytes 36868
  124.4 13.1 %collective-permute-start.12 = (bf16[528,384]{1,0:T(8,128)(2,1)S(1)}, bf16[528,384]{1,0:T(8,128)(2,1)S(1)}, u32[]{:S(2)}, u32[]{:S(2)}) collective-permute-start(bf16[528,384]{1,0:T(8,128)(2,1)S(1)} %get-tuple-element.17), channel_id=1, source_target_pairs={{0,16},{8,24},{16,0},{24,8},{1,17},{9,25},{17,1},{25,9},{2,18},{10... | collective-permute-start | bytes 1216520 | tf_op jit(solution)/shard_map/ppermute | solution.py:33
  127.1 15.9 %collective-permute-start.13 = (bf16[528,384]{1,0:T(8,128)(2,1)S(1)}, bf16[528,384]{1,0:T(8,128)(2,1)S(1)}, u32[]{:S(2)}, u32[]{:S(2)}) collective-permute-start(bf16[528,384]{1,0:T(8,128)(2,1)S(1)} %get-tuple-element.18), channel_id=1, source_target_pairs={{0,24},{8,0},{16,8},{24,16},{1,25},{9,1},{17,9},{25,17},{2,26},{10... | collective-permute-start | bytes 1216520 | tf_op jit(solution)/shard_map/ppermute | solution.py:33
  129.1 18.7 %collective-permute-start.14 = (bf16[528,384]{1,0:T(8,128)(2,1)S(1)}, bf16[528,384]{1,0:T(8,128)(2,1)S(1)}, u32[]{:S(2)}, u32[]{:S(2)}) collective-permute-start(bf16[528,384]{1,0:T(8,128)(2,1)S(1)} %get-tuple-element.19), channel_id=1, source_target_pairs={{0,8},{8,16},{16,24},{24,0},{1,9},{9,17},{17,25},{25,1},{2,10},{10... | collective-permute-start | bytes 1216520 | tf_op jit(solution)/shard_map/ppermute | solution.py:33
  148.3 8.5 %collective-permute-start.15 = (bf16[512,384]{1,0:T(8,128)(2,1)S(1)}, bf16[512,384]{1,0:T(8,128)(2,1)S(1)}, u32[]{:S(2)}, u32[]{:S(2)}) collective-permute-start(bf16[512,384]{1,0:T(8,128)(2,1)S(1)} %shard_map.60.mine_ref), channel_id=1, source_target_pairs={{0,1},{1,0},{2,3},{3,2},{4,5},{5,4},{6,7},{7,6},{8,9},{9,8},{10,11... | collective-permute-start | bytes 1179656 | tf_op jit(solution)/shard_map/ppermute | solution.py:33
  158.6 14.1 %collective-permute-start.16 = (bf16[512,384]{1,0:T(8,128)(2,1)S(1)}, bf16[512,384]{1,0:T(8,128)(2,1)S(1)}, u32[]{:S(2)}, u32[]{:S(2)}) collective-permute-start(bf16[512,384]{1,0:T(8,128)(2,1)S(1)} %get-tuple-element.20), channel_id=1, source_target_pairs={{0,4},{2,6},{4,0},{6,2},{1,5},{3,7},{5,1},{7,3},{8,12},{10,14},{12... | collective-permute-start | bytes 1179656 | tf_op jit(solution)/shard_map/ppermute | solution.py:33
  163.3 18.2 %collective-permute-start.17 = (bf16[512,384]{1,0:T(8,128)(2,1)S(1)}, bf16[512,384]{1,0:T(8,128)(2,1)S(1)}, u32[]{:S(2)}, u32[]{:S(2)}) collective-permute-start(bf16[512,384]{1,0:T(8,128)(2,1)S(1)} %get-tuple-element.21), channel_id=1, source_target_pairs={{0,2},{2,4},{4,6},{6,0},{1,3},{3,5},{5,7},{7,1},{8,10},{10,12},{12... | collective-permute-start | bytes 1179656 | tf_op jit(solution)/shard_map/ppermute | solution.py:33
  165.5 16.0 %collective-permute-start.18 = (bf16[512,384]{1,0:T(8,128)(2,1)S(1)}, bf16[512,384]{1,0:T(8,128)(2,1)S(1)}, u32[]{:S(2)}, u32[]{:S(2)}) collective-permute-start(bf16[512,384]{1,0:T(8,128)(2,1)S(1)} %get-tuple-element.22), channel_id=1, source_target_pairs={{0,6},{2,0},{4,2},{6,4},{1,7},{3,1},{5,3},{7,5},{8,14},{10,8},{12,... | collective-permute-start | bytes 1179656 | tf_op jit(solution)/shard_map/ppermute | solution.py:33
  (13 other events, 52.9 us)

commit v3 on v2

--- a/solution.py
+++ b/solution.py
@@ -20,7 +20,8 @@
 COEF = LOG2E / math.sqrt(HD)
 DEAD = -1e30
 NONE = NZ * NY
-SLOTS = (2, 10, 14, 7, 3, 11, 15, 4, 0, 8, 12, 5, 1, 9, 13, 6)
+HOPS = NZ // 2
+SLOTS = tuple(2 * d if d < HOPS else 2 * (NZ - d) - 1 for d in range(NZ))
 
 
 def pallas(mib, kernel, **kw):
@@ -31,6 +32,14 @@
 def send(a, axis, s):
     n = lax.axis_size(axis)
     return lax.ppermute(a, axis, [(i, (i + s) % n) for i in range(n)])
+
+
+def ahead(k):
+    return [(i, i + 1) for i in range(k - 1, NZ - 1)]
+
+
+def astern(k):
+    return [((r - k + 1) % NZ, (r - k) % NZ) for r in range(HOPS - 1)]
 
 
 def tn(a, b):
@@ -122,9 +131,24 @@
         out_ref[span, :] = (acc * (1.0 / total)).astype(jnp.bfloat16)
 
 
-def turn_kernel(cols_ref, mine_ref, got_ref, out_ref):
-    out_ref[0, :, :HALF] = mine_ref[...].T
-    out_ref[0, :, HALF:] = got_ref[...].T
+def turn_kernel(cols_ref, mine_ref, got_ref, out_ref, blocks, turned, sems, out_sems):
+    loads = []
+    for s in range(NX):
+        cols = pl.ds(pl.multiple_of(cols_ref[s] * HALF, HALF), HALF)
+        for i, src in enumerate((mine_ref, got_ref)):
+            at = 2 * s + i
+            loads.append(pltpu.make_async_copy(src.at[:, cols], blocks.at[at], sems.at[at]))
+    for load in loads:
+        load.start()
+    stores = []
+    for s in range(NX):
+        for i in range(2):
+            loads[2 * s + i].wait()
+            turned[s, :, i * HALF : (i + 1) * HALF] = blocks[2 * s + i].T
+        stores.append(pltpu.make_async_copy(turned.at[s], out_ref.at[s], out_sems.at[s]))
+        stores[s].start()
+    for store in stores:
+        store.wait()
 
 
 def piece_of(w_ref, s, mine_ref, got_ref):
@@ -173,8 +197,15 @@
     for d, place in enumerate(SLOTS):
         slot = jnp.where(offset == d, place, slot)
     code = jnp.where(ids < z * NY + y, slot * NY + ids % NY, NONE)
-    up = send(row, "z", 4)
-    down = send(row, "z", -4)
+    kept = [row]
+    p = m = row
+    for k in range(1, HOPS + 1):
+        p = lax.ppermute(p, "z", ahead(k))
+        kept.append(p)
+        if k < HOPS:
+            m = lax.ppermute(m, "z", astern(k))
+            kept.append(m)
+    kv = jnp.concatenate(kept, axis=0)
     w_got = send(out_weight, "core", 1)
     qx, own, own_lse = pallas(
         8,
@@ -185,27 +216,21 @@
     )(code, queries, keys, values)
     order = (2, 1, 3)
     qs = [send(qx, "y", s) for s in order]
-    far1 = send(up[: NY // 2], "z", 4)
-    far2 = send(down[NY // 2 :], "z", -4)
-    c = jnp.concatenate([far1, far2, up, row, down], axis=0)
-    n1 = send(c, "z", 1)
-    n2 = send(c, "z", -1)
     codes = jnp.stack([a[HALF, : HEADS * TOP] for a in qs], axis=0).astype(jnp.int32).reshape(-1)
     cols = (x + jnp.arange(NX, dtype=jnp.int32)) % NX * 2 + core
     w = pallas(
         12,
         turn_kernel,
-        grid_spec=pltpu.PrefetchScalarGridSpec(
-            num_scalar_prefetch=1,
-            grid=(NX,),
-            in_specs=[pl.BlockSpec((HALF, HALF), lambda s, cols: (0, cols[s]))] * 2,
-            out_specs=pl.BlockSpec((1, HALF, 2 * HALF), lambda s, cols: (s, 0, 0)),
-        ),
+        in_specs=[smem] + [pl.BlockSpec(memory_space=pltpu.HBM)] * 2,
+        out_specs=pl.BlockSpec(memory_space=pltpu.HBM),
         out_shape=bf16(NX, HALF, 2 * HALF),
+        scratch_shapes=[
+            pltpu.VMEM((2 * NX, HALF, HALF), jnp.bfloat16),
+            pltpu.VMEM((NX, HALF, 2 * HALF), jnp.bfloat16),
+            pltpu.SemaphoreType.DMA((2 * NX,)),
+            pltpu.SemaphoreType.DMA((NX,)),
+        ],
     )(cols, out_weight, w_got)
-    m1 = send(n1[NY : 3 * NY], "z", 1)
-    m2 = send(n2[2 * NY :], "z", -1)
-    kv = jnp.concatenate([c, n1, n2, m1, m2], axis=0)
     parts = pallas(
         12,
         slices_kernel,

time: 184 us -> 165 us (0.90)
  waiting for transfers between devices: 52.3 us -> 37.5 us
  starting transfers between devices: 82.6 us -> 92.1 us
  blocking collectives: 8.41 us -> 0 us
  local copies, waits for them, and re-layouts: 21.7 us -> 16.7 us
    ppermute x0 -> x15, starting transfers between devices: none -> 42.4 us  [the longest x7 34.8 us: steps(): m = lax.ppermute(m, 'z', astern(k))]
    ppermute x19 -> x11, starting transfers between devices: 82.6 us -> 45.7 us  [send(): return lax.ppermute(a, axis, [(i, (i + s) % n) for i in range(n)])]
    ppermute x19 -> x11, waiting for transfers between devices: 52.3 us -> 20.8 us  [send(): return lax.ppermute(a, axis, [(i, (i + s) % n) for i in range(n)])]
    ppermute x0 -> x15, waiting for transfers between devices: none -> 11.5 us  [the longest x7 11.5 us: steps(): m = lax.ppermute(m, 'z', astern(k))]
    all_to_all x1 -> x0, blocking collectives: 8.41 us -> none  [steps(): row = lax.all_to_all(packed, 'y', 0, 0)]
    all_to_all x0 -> x1, waiting for transfers between devices: none -> 5.25 us  [steps(): row = lax.all_to_all(packed, 'y', 0, 0)]
    all_to_all x0 -> x1, starting transfers between devices: none -> 3.99 us  [steps(): row = lax.all_to_all(packed, 'y', 0, 0)]
    slice x4 -> x0, local copies, waits for them, and re-layouts: 3.6 us -> none  [the longest x1 1.8 us: steps(): m1 = send(n1[NY:3 * NY], 'z', 1)]
  transfers between devices with their start and end apart: 19 -> 27, of which waited for: 11 -> 11; matrix products, arithmetic and copies ran while one was open for 7% -> 5% of each run, Pallas kernels for 8% -> 9%
where the time goes in v3:
time: 165 us; the launch traced here: 164 us
  starting transfers between devices  92.1 us (56%)
  waiting for transfers between devices  37.5 us (23%)
  local copies, waits for them, and re-layouts  16.7 us (10%)
  Pallas kernels  16.7 us (10%)
    ppermute x11, starting transfers between devices, send(): return lax.ppermute(a, axis, [(i, (i + s) % n) for i in range(n)])  45.7 us
    ppermute x7, starting transfers between devices, steps(): m = lax.ppermute(m, 'z', astern(k))  34.8 us
    ppermute x11, waiting for transfers between devices, send(): return lax.ppermute(a, axis, [(i, (i + s) % n) for i in range(n)])  20.8 us
    unnamed x50, local copies, waits for them, and re-layouts  15.3 us
    ppermute x7, waiting for transfers between devices, steps(): m = lax.ppermute(m, 'z', astern(k))  11.5 us
    ppermute x8, starting transfers between devices, steps(): p = lax.ppermute(p, 'z', ahead(k))  7.58 us
    all_to_all x1, waiting for transfers between devices, steps(): row = lax.all_to_all(packed, 'y', 0, 0)  5.25 us
    pallas_call x1, Pallas kernels, steps(): pallas(12, slices_kernel, in_specs=[smem] + [vmem] * 4, out_specs=[vmem]...  4.64 us
  transfers between devices with their start and end apart: 27, of which 11 were waited for; matrix products, arithmetic and copies ran while one was open for 5% of the time, Pallas kernels for 9%

profile of v3, /device:TPU:1, one launch (start us, length us, event | category | flops | bytes accessed | tf_op | source)
XLA Modules:
  0.0 164.2 jit_solution(4507820447236311658)
XLA Ops:
  0.0 8.7 %collective-permute-start = (bf16[512,4096]{1,0:T(8,128)(2,1)}, bf16[512,4096]{1,0:T(8,128)(2,1)}, u32[]{:S(2)}, u32[]{:S(2)}) collective-permute-start(bf16[512,4096]{1,0:T(8,128)(2,1)} %mine_ref.1), channel_id=1, source_target_pairs={{0,1},{1,0},{2,3},{3,2},{4,5},{5,4},{6,7},{7,6},{8,9},{9,8},{10,11... | collective-permute-start | bytes 12582920 | tf_op jit(solution)/shard_map/ppermute | solution.py:34
  11.2 4.0 %all-to-all-start = ((bf16[4,96,256]{2,1,0:T(8,128)(2,1)}), bf16[4,96,256]{2,1,0:T(8,128)(2,1)}, u32[]{:S(2)}, u32[]{:S(2)}) async-start(bf16[4,96,256]{2,1,0:T(8,128)(2,1)} %shard_map.57), calls=%async_computation | async-start | bytes 393216 | tf_op jit(solution)/shard_map/all_to_all | solution.py:193
  16.1 5.2 %all-to-all-done = bf16[4,96,256]{2,1,0:T(8,128)(2,1)} async-done(((bf16[4,96,256]{2,1,0:T(8,128)(2,1)}), bf16[4,96,256]{2,1,0:T(8,128)(2,1)}, u32[]{:S(2)}, u32[]{:S(2)}) %all-to-all-start) | async-done | bytes 196640 | tf_op jit(solution)/shard_map/all_to_all | solution.py:193
  31.7 3.1 %collective-permute-start.17 = (bf16[528,384]{1,0:T(8,128)(2,1)S(1)}, bf16[528,384]{1,0:T(8,128)(2,1)S(1)}, u32[]{:S(2)}, u32[]{:S(2)}) collective-permute-start(bf16[528,384]{1,0:T(8,128)(2,1)S(1)} %get-tuple-element.16.rest_0_), channel_id=1, source_target_pairs={{0,8},{8,16},{16,24},{24,0},{1,9},{9,17},{17,25},{25,1},{2,10},{10... | collective-permute-start | bytes 1216520 | tf_op jit(solution)/shard_map/ppermute | solution.py:34
  34.8 3.4 %collective-permute-start.18 = (bf16[528,384]{1,0:T(8,128)(2,1)S(1)}, bf16[528,384]{1,0:T(8,128)(2,1)S(1)}, u32[]{:S(2)}, u32[]{:S(2)}) collective-permute-start(bf16[528,384]{1,0:T(8,128)(2,1)S(1)} %get-tuple-element.16.rest_0_), channel_id=1, source_target_pairs={{0,24},{8,0},{16,8},{24,16},{1,25},{9,1},{17,9},{25,17},{2,26},{10... | collective-permute-start | bytes 1216520 | tf_op jit(solution)/shard_map/ppermute | solution.py:34
  38.2 5.1 %collective-permute-start.2 = (bf16[4,96,256]{2,1,0:T(8,128)(2,1)}, bf16[4,96,256]{2,1,0:T(8,128)(2,1)}, u32[]{:S(2)}, u32[]{:S(2)}) collective-permute-start(bf16[4,96,256]{2,1,0:T(8,128)(2,1)} %all-to-all-done), channel_id=1, source_target_pairs={{0,480},{32,0},{64,32},{96,64},{128,96},{160,128},{192,160},{1,481... | collective-permute-start | bytes 589832 | tf_op jit(solution)/shard_map/ppermute | solution.py:206
  47.5 5.2 %collective-permute-start.4 = (bf16[4,96,256]{2,1,0:T(8,128)(2,1)}, bf16[4,96,256]{2,1,0:T(8,128)(2,1)}, u32[]{:S(2)}, u32[]{:S(2)}) collective-permute-start(bf16[4,96,256]{2,1,0:T(8,128)(2,1)} %collective-permute-done.2), channel_id=1, source_target_pairs={{480,448},{0,480},{32,0},{64,32},{96,64},{128,96},{160,128},{481,4... | collective-permute-start | bytes 589832 | tf_op jit(solution)/shard_map/ppermute | solution.py:206
  57.9 4.6 %collective-permute-start.6 = (bf16[4,96,256]{2,1,0:T(8,128)(2,1)}, bf16[4,96,256]{2,1,0:T(8,128)(2,1)S(1)}, u32[]{:S(2)}, u32[]{:S(2)}) collective-permute-start(bf16[4,96,256]{2,1,0:T(8,128)(2,1)} %collective-permute-done.4), channel_id=1, source_target_pairs={{448,416},{480,448},{0,480},{32,0},{64,32},{96,64},{128,96},{449,4... | collective-permute-start | bytes 589832 | tf_op jit(solution)/shard_map/ppermute | solution.py:206
  65.5 4.9 %collective-permute-start.8 = (bf16[4,96,256]{2,1,0:T(8,128)(2,1)S(1)}, bf16[4,96,256]{2,1,0:T(8,128)(2,1)S(1)}, u32[]{:S(2)}, u32[]{:S(2)}) collective-permute-start(bf16[4,96,256]{2,1,0:T(8,128)(2,1)S(1)} %collective-permute-done.6), channel_id=1, source_target_pairs={{416,384},{448,416},{480,448},{0,480},{32,0},{64,32},{96,64},{417,... | collective-permute-start | bytes 589832 | tf_op jit(solution)/shard_map/ppermute | solution.py:206
  73.0 5.0 %collective-permute-start.10 = (bf16[4,96,256]{2,1,0:T(8,128)(2,1)S(1)}, bf16[4,96,256]{2,1,0:T(8,128)(2,1)S(1)}, u32[]{:S(2)}, u32[]{:S(2)}) collective-permute-start(bf16[4,96,256]{2,1,0:T(8,128)(2,1)S(1)} %collective-permute-done.8), channel_id=1, source_target_pairs={{384,352},{416,384},{448,416},{480,448},{0,480},{32,0},{64,32},{38... | collective-permute-start | bytes 589832 | tf_op jit(solution)/shard_map/ppermute | solution.py:206
  80.6 5.0 %collective-permute-start.12 = (bf16[4,96,256]{2,1,0:T(8,128)(2,1)S(1)}, bf16[4,96,256]{2,1,0:T(8,128)(2,1)S(1)}, u32[]{:S(2)}, u32[]{:S(2)}) collective-permute-start(bf16[4,96,256]{2,1,0:T(8,128)(2,1)S(1)} %collective-permute-done.10), channel_id=1, source_target_pairs={{352,320},{384,352},{416,384},{448,416},{480,448},{0,480},{32,0},{... | collective-permute-start | bytes 589832 | tf_op jit(solution)/shard_map/ppermute | solution.py:206
  86.5 2.6 %collective-permute-done.12 = bf16[4,96,256]{2,1,0:T(8,128)(2,1)S(1)} collective-permute-done((bf16[4,96,256]{2,1,0:T(8,128)(2,1)S(1)}, bf16[4,96,256]{2,1,0:T(8,128)(2,1)S(1)}, u32[]{:S(2)}, u32[]{:S(2)}) %collective-permute-start.12) | collective-permute-done | bytes 196640 | tf_op jit(solution)/shard_map/ppermute | solution.py:206
  89.1 5.0 %collective-permute-start.14 = (bf16[4,96,256]{2,1,0:T(8,128)(2,1)S(1)}, bf16[4,96,256]{2,1,0:T(8,128)(2,1)S(1)}, u32[]{:S(2)}, u32[]{:S(2)}) collective-permute-start(bf16[4,96,256]{2,1,0:T(8,128)(2,1)S(1)} %collective-permute-done.12), channel_id=1, source_target_pairs={{320,288},{352,320},{384,352},{416,384},{448,416},{480,448},{0,480... | collective-permute-start | bytes 589832 | tf_op jit(solution)/shard_map/ppermute | solution.py:206
  94.8 3.9 %collective-permute-done.14 = bf16[4,96,256]{2,1,0:T(8,128)(2,1)S(1)} collective-permute-done((bf16[4,96,256]{2,1,0:T(8,128)(2,1)S(1)}, bf16[4,96,256]{2,1,0:T(8,128)(2,1)S(1)}, u32[]{:S(2)}, u32[]{:S(2)}) %collective-permute-start.14) | collective-permute-done | bytes 196640 | tf_op jit(solution)/shard_map/ppermute | solution.py:206
  98.8 4.6 %shard_map.59 = (bf16[528,384]{1,0:T(8,128)(2,1)S(1)}, bf16[528,384]{1,0:T(8,128)(2,1)S(1)}, bf16[528,384]{1,0:T(8,128)(2,1)S(1)}) custom-call(s32[36]{0:T(128)S(1)} %copy-done.16, bf16[64,96,256]{2,1,0:T(8,128)(2,1)S(1)} %constant_dynamic-update-slice_fusion.kv_ref, bf16[528,384]{1,0:T(8,128)(2,1)S(1)} %collective-permute-done.16.rest_0_, ...), custom_call_target="tpu_custom_call" | custom-call | tf_op jit(solution)/shard_map/pallas_call | solution.py:234
  103.5 3.2 %collective-permute-start.19 = (bf16[528,384]{1,0:T(8,128)(2,1)S(1)}, bf16[528,384]{1,0:T(8,128)(2,1)S(1)}, u32[]{:S(2)}, u32[]{:S(2)}) collective-permute-start(bf16[528,384]{1,0:T(8,128)(2,1)S(1)} %get-tuple-element.17), channel_id=1, source_target_pairs={{0,16},{8,24},{16,0},{24,8},{1,17},{9,25},{17,1},{25,9},{2,18},{10... | collective-permute-start | bytes 1216520 | tf_op jit(solution)/shard_map/ppermute | solution.py:34
  106.6 2.8 %collective-permute-start.20 = (bf16[528,384]{1,0:T(8,128)(2,1)S(1)}, bf16[528,384]{1,0:T(8,128)(2,1)S(1)}, u32[]{:S(2)}, u32[]{:S(2)}) collective-permute-start(bf16[528,384]{1,0:T(8,128)(2,1)S(1)} %get-tuple-element.18), channel_id=1, source_target_pairs={{0,24},{8,0},{16,8},{24,16},{1,25},{9,1},{17,9},{25,17},{2,26},{10... | collective-permute-start | bytes 1216520 | tf_op jit(solution)/shard_map/ppermute | solution.py:34
  113.9 2.7 %collective-permute-done.20.p2 = bf16[528,384]{1,0:T(8,128)(2,1)S(1)} collective-permute-done((bf16[528,384]{1,0:T(8,128)(2,1)S(1)}, bf16[528,384]{1,0:T(8,128)(2,1)S(1)}, u32[]{:S(2)}, u32[]{:S(2)}) %collective-permute-start.20) | collective-permute-done | bytes 405536 | tf_op jit(solution)/shard_map/ppermute | solution.py:34
  116.6 7.0 %collective-permute-done.21.p3 = bf16[528,384]{1,0:T(8,128)(2,1)S(1)} collective-permute-done((bf16[528,384]{1,0:T(8,128)(2,1)S(1)}, bf16[528,384]{1,0:T(8,128)(2,1)S(1)}, u32[]{:S(2)}, u32[]{:S(2)}) %collective-permute-start.21) | collective-permute-done | bytes 405536 | tf_op jit(solution)/shard_map/ppermute | solution.py:34
  124.2 8.7 %collective-permute-start.22 = (bf16[512,384]{1,0:T(8,128)(2,1)S(1)}, bf16[512,384]{1,0:T(8,128)(2,1)S(1)}, u32[]{:S(2)}, u32[]{:S(2)}) collective-permute-start(bf16[512,384]{1,0:T(8,128)(2,1)S(1)} %shard_map.60.mine_ref), channel_id=1, source_target_pairs={{0,1},{1,0},{2,3},{3,2},{4,5},{5,4},{6,7},{7,6},{8,9},{9,8},{10,11... | collective-permute-start | bytes 1179656 | tf_op jit(solution)/shard_map/ppermute | solution.py:34
  135.1 3.5 %shard_map.55.w_ref = bf16[4,512,1024]{2,1,0:T(8,128)(2,1)S(1)} custom-call(s32[4]{0:T(128)S(1)} %fusion.2.cols_ref, bf16[512,4096]{1,0:T(8,128)(2,1)S(1)} %copy-done, bf16[512,4096]{1,0:T(8,128)(2,1)} %collective-permute-done.got_ref), custom_call_target="tpu_custom_call" | custom-call | tf_op jit(solution)/shard_map/pallas_call | solution.py:221
  140.4 4.7 %collective-permute-start.23 = (bf16[512,384]{1,0:T(8,128)(2,1)S(1)}, bf16[512,384]{1,0:T(8,128)(2,1)S(1)}, u32[]{:S(2)}, u32[]{:S(2)}) collective-permute-start(bf16[512,384]{1,0:T(8,128)(2,1)S(1)} %get-tuple-element.20), channel_id=1, source_target_pairs={{0,4},{2,6},{4,0},{6,2},{1,5},{3,7},{5,1},{7,3},{8,12},{10,14},{12... | collective-permute-start | bytes 1179656 | tf_op jit(solution)/shard_map/ppermute | solution.py:34
  147.3 4.3 %collective-permute-start.25 = (bf16[512,384]{1,0:T(8,128)(2,1)S(1)}, bf16[512,384]{1,0:T(8,128)(2,1)S(1)}, u32[]{:S(2)}, u32[]{:S(2)}) collective-permute-start(bf16[512,384]{1,0:T(8,128)(2,1)S(1)} %get-tuple-element.22), channel_id=1, source_target_pairs={{0,6},{2,0},{4,2},{6,4},{1,7},{3,1},{5,3},{7,5},{8,14},{10,8},{12,... | collective-permute-start | bytes 1179656 | tf_op jit(solution)/shard_map/ppermute | solution.py:34
  154.5 8.8 %collective-permute-done.24.g2 = bf16[512,384]{1,0:T(8,128)(2,1)S(1)} collective-permute-done((bf16[512,384]{1,0:T(8,128)(2,1)S(1)}, bf16[512,384]{1,0:T(8,128)(2,1)S(1)}, u32[]{:S(2)}, u32[]{:S(2)}) %collective-permute-start.24) | collective-permute-done | bytes 393248 | tf_op jit(solution)/shard_map/ppermute | solution.py:34
  (98 shorter events, 47.7 us)
Async XLA Ops:
  0.0 132.9 %collective-permute-start = (bf16[512,4096]{1,0:T(8,128)(2,1)}, bf16[512,4096]{1,0:T(8,128)(2,1)}, u32[]{:S(2)}, u32[]{:S(2)}) collective-permute-start(bf16[512,4096]{1,0:T(8,128)(2,1)} %mine_ref.1), channel_id=1, source_target_pairs={{0,1},{1,0},{2,3},{3,2},{4,5},{5,4},{6,7},{7,6},{8,9},{9,8},{10,11... | collective-permute-start | bytes 12582920 | tf_op jit(solution)/shard_map/ppermute | solution.py:34
  11.2 10.1 %all-to-all-start = ((bf16[4,96,256]{2,1,0:T(8,128)(2,1)}), bf16[4,96,256]{2,1,0:T(8,128)(2,1)}, u32[]{:S(2)}, u32[]{:S(2)}) async-start(bf16[4,96,256]{2,1,0:T(8,128)(2,1)} %shard_map.57), calls=%async_computation | async-start | bytes 393216 | tf_op jit(solution)/shard_map/all_to_all | solution.py:193
  21.4 16.9 %collective-permute-start.1 = (bf16[4,96,256]{2,1,0:T(8,128)(2,1)}, bf16[4,96,256]{2,1,0:T(8,128)(2,1)}, u32[]{:S(2)}, u32[]{:S(2)}) collective-permute-start(bf16[4,96,256]{2,1,0:T(8,128)(2,1)} %all-to-all-done), channel_id=1, source_target_pairs={{0,32},{32,64},{64,96},{96,128},{128,160},{160,192},{192,224},{224... | collective-permute-start | bytes 589832 | tf_op jit(solution)/shard_map/ppermute | solution.py:203
  29.5 18.0 %collective-permute-start.16 = (bf16[528,384]{1,0:T(8,128)(2,1)S(1)}, bf16[528,384]{1,0:T(8,128)(2,1)S(1)}, u32[]{:S(2)}, u32[]{:S(2)}) collective-permute-start(bf16[528,384]{1,0:T(8,128)(2,1)S(1)} %get-tuple-element.16.rest_0_), channel_id=1, source_target_pairs={{0,16},{8,24},{16,0},{24,8},{1,17},{9,25},{17,1},{25,9},{2,18},{10... | collective-permute-start | bytes 1216520 | tf_op jit(solution)/shard_map/ppermute | solution.py:34
  31.7 22.0 %collective-permute-start.17 = (bf16[528,384]{1,0:T(8,128)(2,1)S(1)}, bf16[528,384]{1,0:T(8,128)(2,1)S(1)}, u32[]{:S(2)}, u32[]{:S(2)}) collective-permute-start(bf16[528,384]{1,0:T(8,128)(2,1)S(1)} %get-tuple-element.16.rest_0_), channel_id=1, source_target_pairs={{0,8},{8,16},{16,24},{24,0},{1,9},{9,17},{17,25},{25,1},{2,10},{10... | collective-permute-start | bytes 1216520 | tf_op jit(solution)/shard_map/ppermute | solution.py:34
  34.8 19.7 %collective-permute-start.18 = (bf16[528,384]{1,0:T(8,128)(2,1)S(1)}, bf16[528,384]{1,0:T(8,128)(2,1)S(1)}, u32[]{:S(2)}, u32[]{:S(2)}) collective-permute-start(bf16[528,384]{1,0:T(8,128)(2,1)S(1)} %get-tuple-element.16.rest_0_), channel_id=1, source_target_pairs={{0,24},{8,0},{16,8},{24,16},{1,25},{9,1},{17,9},{25,17},{2,26},{10... | collective-permute-start | bytes 1216520 | tf_op jit(solution)/shard_map/ppermute | solution.py:34
  38.2 8.0 %collective-permute-start.2 = (bf16[4,96,256]{2,1,0:T(8,128)(2,1)}, bf16[4,96,256]{2,1,0:T(8,128)(2,1)}, u32[]{:S(2)}, u32[]{:S(2)}) collective-permute-start(bf16[4,96,256]{2,1,0:T(8,128)(2,1)} %all-to-all-done), channel_id=1, source_target_pairs={{0,480},{32,0},{64,32},{96,64},{128,96},{160,128},{192,160},{1,481... | collective-permute-start | bytes 589832 | tf_op jit(solution)/shard_map/ppermute | solution.py:206
  46.2 10.9 %collective-permute-start.3 = (bf16[4,96,256]{2,1,0:T(8,128)(2,1)}, bf16[4,96,256]{2,1,0:T(8,128)(2,1)}, u32[]{:S(2)}, u32[]{:S(2)}) collective-permute-start(bf16[4,96,256]{2,1,0:T(8,128)(2,1)} %collective-permute-done.1), channel_id=1, source_target_pairs={{32,64},{64,96},{96,128},{128,160},{160,192},{192,224},{224,256},{... | collective-permute-start | bytes 589832 | tf_op jit(solution)/shard_map/ppermute | solution.py:203
  47.5 10.4 %collective-permute-start.4 = (bf16[4,96,256]{2,1,0:T(8,128)(2,1)}, bf16[4,96,256]{2,1,0:T(8,128)(2,1)}, u32[]{:S(2)}, u32[]{:S(2)}) collective-permute-start(bf16[4,96,256]{2,1,0:T(8,128)(2,1)} %collective-permute-done.2), channel_id=1, source_target_pairs={{480,448},{0,480},{32,0},{64,32},{96,64},{128,96},{160,128},{481,4... | collective-permute-start | bytes 589832 | tf_op jit(solution)/shard_map/ppermute | solution.py:206
  57.9 7.5 %collective-permute-start.6 = (bf16[4,96,256]{2,1,0:T(8,128)(2,1)}, bf16[4,96,256]{2,1,0:T(8,128)(2,1)S(1)}, u32[]{:S(2)}, u32[]{:S(2)}) collective-permute-start(bf16[4,96,256]{2,1,0:T(8,128)(2,1)} %collective-permute-done.4), channel_id=1, source_target_pairs={{448,416},{480,448},{0,480},{32,0},{64,32},{96,64},{128,96},{449,4... | collective-permute-start | bytes 589832 | tf_op jit(solution)/shard_map/ppermute | solution.py:206
  65.5 7.5 %collective-permute-start.8 = (bf16[4,96,256]{2,1,0:T(8,128)(2,1)S(1)}, bf16[4,96,256]{2,1,0:T(8,128)(2,1)S(1)}, u32[]{:S(2)}, u32[]{:S(2)}) collective-permute-start(bf16[4,96,256]{2,1,0:T(8,128)(2,1)S(1)} %collective-permute-done.6), channel_id=1, source_target_pairs={{416,384},{448,416},{480,448},{0,480},{32,0},{64,32},{96,64},{417,... | collective-permute-start | bytes 589832 | tf_op jit(solution)/shard_map/ppermute | solution.py:206
  70.4 7.6 %collective-permute-start.9 = (bf16[4,96,256]{2,1,0:T(8,128)(2,1)S(1)}, bf16[4,96,256]{2,1,0:T(8,128)(2,1)S(1)}, u32[]{:S(2)}, u32[]{:S(2)}) collective-permute-start(bf16[4,96,256]{2,1,0:T(8,128)(2,1)S(1)} %collective-permute-done.7), channel_id=1, source_target_pairs={{128,160},{160,192},{192,224},{224,256},{256,288},{288,320},{320,3... | collective-permute-start | bytes 589832 | tf_op jit(solution)/shard_map/ppermute | solution.py:203
  73.0 7.6 %collective-permute-start.10 = (bf16[4,96,256]{2,1,0:T(8,128)(2,1)S(1)}, bf16[4,96,256]{2,1,0:T(8,128)(2,1)S(1)}, u32[]{:S(2)}, u32[]{:S(2)}) collective-permute-start(bf16[4,96,256]{2,1,0:T(8,128)(2,1)S(1)} %collective-permute-done.8), channel_id=1, source_target_pairs={{384,352},{416,384},{448,416},{480,448},{0,480},{32,0},{64,32},{38... | collective-permute-start | bytes 589832 | tf_op jit(solution)/shard_map/ppermute | solution.py:206
  78.1 7.6 %collective-permute-start.11 = (bf16[4,96,256]{2,1,0:T(8,128)(2,1)S(1)}, bf16[4,96,256]{2,1,0:T(8,128)(2,1)S(1)}, u32[]{:S(2)}, u32[]{:S(2)}) collective-permute-start(bf16[4,96,256]{2,1,0:T(8,128)(2,1)S(1)} %collective-permute-done.9), channel_id=1, source_target_pairs={{160,192},{192,224},{224,256},{256,288},{288,320},{320,352},{352,3... | collective-permute-start | bytes 589832 | tf_op jit(solution)/shard_map/ppermute | solution.py:203
  80.6 8.5 %collective-permute-start.12 = (bf16[4,96,256]{2,1,0:T(8,128)(2,1)S(1)}, bf16[4,96,256]{2,1,0:T(8,128)(2,1)S(1)}, u32[]{:S(2)}, u32[]{:S(2)}) collective-permute-start(bf16[4,96,256]{2,1,0:T(8,128)(2,1)S(1)} %collective-permute-done.10), channel_id=1, source_target_pairs={{352,320},{384,352},{416,384},{448,416},{480,448},{0,480},{32,0},{... | collective-permute-start | bytes 589832 | tf_op jit(solution)/shard_map/ppermute | solution.py:206
  85.7 8.5 %collective-permute-start.13 = (bf16[4,96,256]{2,1,0:T(8,128)(2,1)S(1)}, bf16[4,96,256]{2,1,0:T(8,128)(2,1)S(1)}, u32[]{:S(2)}, u32[]{:S(2)}) collective-permute-start(bf16[4,96,256]{2,1,0:T(8,128)(2,1)S(1)} %collective-permute-done.11), channel_id=1, source_target_pairs={{192,224},{224,256},{256,288},{288,320},{320,352},{352,384},{384,4... | collective-permute-start | bytes 589832 | tf_op jit(solution)/shard_map/ppermute | solution.py:203
  89.1 9.7 %collective-permute-start.14 = (bf16[4,96,256]{2,1,0:T(8,128)(2,1)S(1)}, bf16[4,96,256]{2,1,0:T(8,128)(2,1)S(1)}, u32[]{:S(2)}, u32[]{:S(2)}) collective-permute-start(bf16[4,96,256]{2,1,0:T(8,128)(2,1)S(1)} %collective-permute-done.12), channel_id=1, source_target_pairs={{320,288},{352,320},{384,352},{416,384},{448,416},{480,448},{0,480... | collective-permute-start | bytes 589832 | tf_op jit(solution)/shard_map/ppermute | solution.py:206
  103.5 10.4 %collective-permute-start.19 = (bf16[528,384]{1,0:T(8,128)(2,1)S(1)}, bf16[528,384]{1,0:T(8,128)(2,1)S(1)}, u32[]{:S(2)}, u32[]{:S(2)}) collective-permute-start(bf16[528,384]{1,0:T(8,128)(2,1)S(1)} %get-tuple-element.17), channel_id=1, source_target_pairs={{0,16},{8,24},{16,0},{24,8},{1,17},{9,25},{17,1},{25,9},{2,18},{10... | collective-permute-start | bytes 1216520 | tf_op jit(solution)/shard_map/ppermute | solution.py:34
  106.6 10.0 %collective-permute-start.20 = (bf16[528,384]{1,0:T(8,128)(2,1)S(1)}, bf16[528,384]{1,0:T(8,128)(2,1)S(1)}, u32[]{:S(2)}, u32[]{:S(2)}) collective-permute-start(bf16[528,384]{1,0:T(8,128)(2,1)S(1)} %get-tuple-element.18), channel_id=1, source_target_pairs={{0,24},{8,0},{16,8},{24,16},{1,25},{9,1},{17,9},{25,17},{2,26},{10... | collective-permute-start | bytes 1216520 | tf_op jit(solution)/shard_map/ppermute | solution.py:34
  109.4 14.2 %collective-permute-start.21 = (bf16[528,384]{1,0:T(8,128)(2,1)S(1)}, bf16[528,384]{1,0:T(8,128)(2,1)S(1)}, u32[]{:S(2)}, u32[]{:S(2)}) collective-permute-start(bf16[528,384]{1,0:T(8,128)(2,1)S(1)} %get-tuple-element.19), channel_id=1, source_target_pairs={{0,8},{8,16},{16,24},{24,0},{1,9},{9,17},{17,25},{25,1},{2,10},{10... | collective-permute-start | bytes 1216520 | tf_op jit(solution)/shard_map/ppermute | solution.py:34
  124.2 14.4 %collective-permute-start.22 = (bf16[512,384]{1,0:T(8,128)(2,1)S(1)}, bf16[512,384]{1,0:T(8,128)(2,1)S(1)}, u32[]{:S(2)}, u32[]{:S(2)}) collective-permute-start(bf16[512,384]{1,0:T(8,128)(2,1)S(1)} %shard_map.60.mine_ref), channel_id=1, source_target_pairs={{0,1},{1,0},{2,3},{3,2},{4,5},{5,4},{6,7},{7,6},{8,9},{9,8},{10,11... | collective-permute-start | bytes 1179656 | tf_op jit(solution)/shard_map/ppermute | solution.py:34
  140.4 14.1 %collective-permute-start.23 = (bf16[512,384]{1,0:T(8,128)(2,1)S(1)}, bf16[512,384]{1,0:T(8,128)(2,1)S(1)}, u32[]{:S(2)}, u32[]{:S(2)}) collective-permute-start(bf16[512,384]{1,0:T(8,128)(2,1)S(1)} %get-tuple-element.20), channel_id=1, source_target_pairs={{0,4},{2,6},{4,0},{6,2},{1,5},{3,7},{5,1},{7,3},{8,12},{10,14},{12... | collective-permute-start | bytes 1179656 | tf_op jit(solution)/shard_map/ppermute | solution.py:34
  145.1 18.2 %collective-permute-start.24 = (bf16[512,384]{1,0:T(8,128)(2,1)S(1)}, bf16[512,384]{1,0:T(8,128)(2,1)S(1)}, u32[]{:S(2)}, u32[]{:S(2)}) collective-permute-start(bf16[512,384]{1,0:T(8,128)(2,1)S(1)} %get-tuple-element.21), channel_id=1, source_target_pairs={{0,2},{2,4},{4,6},{6,0},{1,3},{3,5},{5,7},{7,1},{8,10},{10,12},{12... | collective-permute-start | bytes 1179656 | tf_op jit(solution)/shard_map/ppermute | solution.py:34
  147.3 16.0 %collective-permute-start.25 = (bf16[512,384]{1,0:T(8,128)(2,1)S(1)}, bf16[512,384]{1,0:T(8,128)(2,1)S(1)}, u32[]{:S(2)}, u32[]{:S(2)}) collective-permute-start(bf16[512,384]{1,0:T(8,128)(2,1)S(1)} %get-tuple-element.22), channel_id=1, source_target_pairs={{0,6},{2,0},{4,2},{6,4},{1,7},{3,1},{5,3},{7,5},{8,14},{10,8},{12,... | collective-permute-start | bytes 1179656 | tf_op jit(solution)/shard_map/ppermute | solution.py:34
  (20 other events, 253.5 us)

commit v4 on v3

--- a/solution.py
+++ b/solution.py
@@ -1,3 +1,4 @@
+import functools
 import math
 
 import jax
@@ -102,10 +103,8 @@
     o_ref[HALF:, :] = jnp.concatenate(rows, axis=0).astype(jnp.bfloat16)
 
 
-def slices_kernel(code_ref, kv_ref, *rest):
-    n = len(rest) // 2
-    for i in range(n):
-        slices_of(code_ref, kv_ref, rest[i], rest[n + i], i * HEADS * TOP)
+def slices_kernel(code_ref, kv_ref, q_ref, o_ref, *, base):
+    slices_of(code_ref, kv_ref, q_ref, o_ref, base)
 
 
 def merge_kernel(own_ref, lse_ref, p0, p1, p2, p3, out_ref):
@@ -156,9 +155,8 @@
     return out + jnp.dot(w_ref[s, :, HALF:], got_ref[...], preferred_element_type=jnp.float32)
 
 
-def pieces_kernel(w_ref, mine_ref, got_ref, *outs):
-    for s, out in zip((2, 1, 3), outs):
-        out[...] = piece_of(w_ref, s, mine_ref, got_ref).astype(jnp.bfloat16)
+def piece_kernel(w_ref, mine_ref, got_ref, out_ref, *, s):
+    out_ref[...] = piece_of(w_ref, s, mine_ref, got_ref).astype(jnp.bfloat16)
 
 
 def mine_kernel(w_ref, mine_ref, got_ref, out_ref):
@@ -188,7 +186,7 @@
     vmem = pl.BlockSpec(memory_space=pltpu.VMEM)
     smem = pl.BlockSpec(memory_space=pltpu.SMEM)
     packed = pallas(
-        4, pack_kernel, in_specs=[vmem] * 2, out_specs=vmem, out_shape=bf16(NY, SL, 2 * HD)
+        60, pack_kernel, in_specs=[vmem] * 2, out_specs=vmem, out_shape=bf16(NY, SL, 2 * HD)
     )(keys, values)
     row = lax.all_to_all(packed, "y", 0, 0)
     ids = block_ids.reshape(HEADS * TOP)
@@ -205,7 +203,6 @@
         if k < HOPS:
             m = lax.ppermute(m, "z", astern(k))
             kept.append(m)
-    kv = jnp.concatenate(kept, axis=0)
     w_got = send(out_weight, "core", 1)
     qx, own, own_lse = pallas(
         8,
@@ -231,33 +228,36 @@
             pltpu.SemaphoreType.DMA((NX,)),
         ],
     )(cols, out_weight, w_got)
-    parts = pallas(
-        12,
-        slices_kernel,
-        in_specs=[smem] + [vmem] * 4,
-        out_specs=[vmem] * 3,
-        out_shape=[bf16(EXT, TOK)] * 3,
-    )(codes, kv, *qs)
-    back = [send(o, "y", -s) for s, o in zip(order, parts)]
-    (home,) = pallas(
-        12,
-        slices_kernel,
-        in_specs=[smem] + [vmem] * 2,
-        out_specs=[vmem],
-        out_shape=[bf16(EXT, TOK)],
-    )(code, kv, qx)
+    kv = jnp.concatenate(kept, axis=0)
+
+    def attend(code, q, base):
+        return pallas(
+            12,
+            functools.partial(slices_kernel, base=base),
+            in_specs=[smem] + [vmem] * 2,
+            out_specs=vmem,
+            out_shape=bf16(EXT, TOK),
+        )(code, kv, q)
+
+    back = []
+    for i, s in enumerate(order):
+        part = attend(codes, qs[i], i * HEADS * TOP)
+        back.append(send(part, "y", -s))
+    home = attend(code, qx, 0)
     att = pallas(
         8, merge_kernel, in_specs=[vmem] * 6, out_specs=vmem, out_shape=bf16(HALF, TOK)
     )(own, own_lse, home, *back)
     att_got = send(att, "core", 1)
-    pieces = pallas(
-        16,
-        pieces_kernel,
-        in_specs=[vmem] * 3,
-        out_specs=[vmem] * 3,
-        out_shape=[bf16(HALF, TOK)] * 3,
-    )(w, att, att_got)
-    got = [send(p, "x", s) for s, p in zip(order, pieces)]
+    got = []
+    for s in order:
+        part = pallas(
+            12,
+            functools.partial(piece_kernel, s=s),
+            in_specs=[vmem] * 3,
+            out_specs=vmem,
+            out_shape=bf16(HALF, TOK),
+        )(w, att, att_got)
+        got.append(send(part, "x", s))
     mine = pallas(
         12, mine_kernel, in_specs=[vmem] * 3, out_specs=vmem, out_shape=f32(HALF, TOK)
     )(w, att, att_got)

time: 165 us -> 170 us (1.030)
  waiting for transfers between devices: 37.5 us -> 40.8 us
  Pallas kernels: 16.7 us -> 19.2 us
    ppermute x11, waiting for transfers between devices: 20.8 us -> 24 us  [send(): return lax.ppermute(a, axis, [(i, (i + s) % n) for i in range(n)])]
    pallas_call x4 -> x8, Pallas kernels: 9.09 us -> 11.6 us  [the longest x4 7.77 us: attend(): pallas(12, functools.partial(slices_kernel, base=base), in_specs=[smem] +...]
    unnamed x50 -> x48, local copies, waits for them, and re-layouts: 15.3 us -> 14.2 us
  transfers between devices with their start and end apart: 27 -> 27, of which waited for: 11 -> 10; matrix products, arithmetic and copies ran while one was open for 5% -> 4% of each run, Pallas kernels for 9% -> 10%
where the time goes in v4:
time: 170 us; the launch traced here: 168 us
  starting transfers between devices  92 us (54%)
  waiting for transfers between devices  40.8 us (24%)
  Pallas kernels  19.2 us (11%)
  local copies, waits for them, and re-layouts  15.1 us (9%)
    ppermute x11, starting transfers between devices, send(): return lax.ppermute(a, axis, [(i, (i + s) % n) for i in range(n)])  45.7 us
    ppermute x7, starting transfers between devices, steps(): m = lax.ppermute(m, 'z', astern(k))  34.8 us
    ppermute x11, waiting for transfers between devices, send(): return lax.ppermute(a, axis, [(i, (i + s) % n) for i in range(n)])  24 us
    unnamed x48, local copies, waits for them, and re-layouts  14.2 us
    ppermute x7, waiting for transfers between devices, steps(): m = lax.ppermute(m, 'z', astern(k))  11.5 us
    pallas_call x4, Pallas kernels, attend(): pallas(12, functools.partial(slices_kernel, base=base), in_specs=[smem] +...  7.77 us
    ppermute x8, starting transfers between devices, steps(): p = lax.ppermute(p, 'z', ahead(k))  7.57 us
    all_to_all x1, waiting for transfers between devices, steps(): row = lax.all_to_all(packed, 'y', 0, 0)  5.25 us
  transfers between devices with their start and end apart: 27, of which 10 were waited for; matrix products, arithmetic and copies ran while one was open for 4% of the time, Pallas kernels for 10%

profile of v4, /device:TPU:1, one launch (start us, length us, event | category | flops | bytes accessed | tf_op | source)
XLA Modules:
  0.0 168.4 jit_solution(2362852061795218834)
XLA Ops:
  0.0 8.7 %collective-permute-start = (bf16[512,4096]{1,0:T(8,128)(2,1)}, bf16[512,4096]{1,0:T(8,128)(2,1)}, u32[]{:S(2)}, u32[]{:S(2)}) collective-permute-start(bf16[512,4096]{1,0:T(8,128)(2,1)} %mine_ref.1), channel_id=1, source_target_pairs={{0,1},{1,0},{2,3},{3,2},{4,5},{5,4},{6,7},{7,6},{8,9},{9,8},{10,11... | collective-permute-start | bytes 12582920 | tf_op jit(solution)/shard_map/ppermute | solution.py:35
  10.4 4.0 %all-to-all-start = ((bf16[4,96,256]{2,1,0:T(8,128)(2,1)}), bf16[4,96,256]{2,1,0:T(8,128)(2,1)}, u32[]{:S(2)}, u32[]{:S(2)}) async-start(bf16[4,96,256]{2,1,0:T(8,128)(2,1)} %shard_map.57), calls=%async_computation | async-start | bytes 393216 | tf_op jit(solution)/shard_map/all_to_all | solution.py:191
  15.3 5.2 %all-to-all-done = bf16[4,96,256]{2,1,0:T(8,128)(2,1)} async-done(((bf16[4,96,256]{2,1,0:T(8,128)(2,1)}), bf16[4,96,256]{2,1,0:T(8,128)(2,1)}, u32[]{:S(2)}, u32[]{:S(2)}) %all-to-all-start) | async-done | bytes 196640 | tf_op jit(solution)/shard_map/all_to_all | solution.py:191
  25.3 2.0 %shard_map.56 = (bf16[528,384]{1,0:T(8,128)(2,1)S(1)}, bf16[512,384]{1,0:T(8,128)(2,1)S(1)}, f32[8,384]{1,0:T(8,128)S(1)}) custom-call(s32[12]{0:T(128)S(1)} %compare_select_fusion.19.code_ref, bf16[384,512]{1,0:T(8,128)(2,1)S(1)} %copy-done.9, bf16[384,128]{1,0:T(8,128)(2,1)S(1)} %copy-done.10, bf16[384,128]{1,0:T(8,128)(2,1)S(1)} %copy-done.11), custom_call_target="tpu_custom_call" | custom-call | tf_op jit(solution)/shard_map/pallas_call | solution.py:207
  28.7 2.2 %collective-permute-start.16 = (bf16[528,384]{1,0:T(8,128)(2,1)S(1)}, bf16[528,384]{1,0:T(8,128)(2,1)S(1)}, u32[]{:S(2)}, u32[]{:S(2)}) collective-permute-start(bf16[528,384]{1,0:T(8,128)(2,1)S(1)} %get-tuple-element.10.q_ref), channel_id=1, source_target_pairs={{0,16},{8,24},{16,0},{24,8},{1,17},{9,25},{17,1},{25,9},{2,18},{10... | collective-permute-start | bytes 1216520 | tf_op jit(solution)/shard_map/ppermute | solution.py:35
  30.9 3.1 %collective-permute-start.17 = (bf16[528,384]{1,0:T(8,128)(2,1)S(1)}, bf16[528,384]{1,0:T(8,128)(2,1)S(1)}, u32[]{:S(2)}, u32[]{:S(2)}) collective-permute-start(bf16[528,384]{1,0:T(8,128)(2,1)S(1)} %get-tuple-element.10.q_ref), channel_id=1, source_target_pairs={{0,8},{8,16},{16,24},{24,0},{1,9},{9,17},{17,25},{25,1},{2,10},{10... | collective-permute-start | bytes 1216520 | tf_op jit(solution)/shard_map/ppermute | solution.py:35
  34.0 3.4 %collective-permute-start.18 = (bf16[528,384]{1,0:T(8,128)(2,1)S(1)}, bf16[528,384]{1,0:T(8,128)(2,1)S(1)}, u32[]{:S(2)}, u32[]{:S(2)}) collective-permute-start(bf16[528,384]{1,0:T(8,128)(2,1)S(1)} %get-tuple-element.10.q_ref), channel_id=1, source_target_pairs={{0,24},{8,0},{16,8},{24,16},{1,25},{9,1},{17,9},{25,17},{2,26},{10... | collective-permute-start | bytes 1216520 | tf_op jit(solution)/shard_map/ppermute | solution.py:35
  37.4 5.0 %collective-permute-start.2 = (bf16[4,96,256]{2,1,0:T(8,128)(2,1)}, bf16[4,96,256]{2,1,0:T(8,128)(2,1)}, u32[]{:S(2)}, u32[]{:S(2)}) collective-permute-start(bf16[4,96,256]{2,1,0:T(8,128)(2,1)} %all-to-all-done), channel_id=1, source_target_pairs={{0,480},{32,0},{64,32},{96,64},{128,96},{160,128},{192,160},{1,481... | collective-permute-start | bytes 589832 | tf_op jit(solution)/shard_map/ppermute | solution.py:204
  46.7 5.2 %collective-permute-start.4 = (bf16[4,96,256]{2,1,0:T(8,128)(2,1)}, bf16[4,96,256]{2,1,0:T(8,128)(2,1)}, u32[]{:S(2)}, u32[]{:S(2)}) collective-permute-start(bf16[4,96,256]{2,1,0:T(8,128)(2,1)} %collective-permute-done.2), channel_id=1, source_target_pairs={{480,448},{0,480},{32,0},{64,32},{96,64},{128,96},{160,128},{481,4... | collective-permute-start | bytes 589832 | tf_op jit(solution)/shard_map/ppermute | solution.py:204
  57.3 4.6 %collective-permute-start.6 = (bf16[4,96,256]{2,1,0:T(8,128)(2,1)}, bf16[4,96,256]{2,1,0:T(8,128)(2,1)S(1)}, u32[]{:S(2)}, u32[]{:S(2)}) collective-permute-start(bf16[4,96,256]{2,1,0:T(8,128)(2,1)} %collective-permute-done.4), channel_id=1, source_target_pairs={{448,416},{480,448},{0,480},{32,0},{64,32},{96,64},{128,96},{449,4... | collective-permute-start | bytes 589832 | tf_op jit(solution)/shard_map/ppermute | solution.py:204
  64.8 4.9 %collective-permute-start.8 = (bf16[4,96,256]{2,1,0:T(8,128)(2,1)S(1)}, bf16[4,96,256]{2,1,0:T(8,128)(2,1)S(1)}, u32[]{:S(2)}, u32[]{:S(2)}) collective-permute-start(bf16[4,96,256]{2,1,0:T(8,128)(2,1)S(1)} %collective-permute-done.6), channel_id=1, source_target_pairs={{416,384},{448,416},{480,448},{0,480},{32,0},{64,32},{96,64},{417,... | collective-permute-start | bytes 589832 | tf_op jit(solution)/shard_map/ppermute | solution.py:204
  72.3 5.0 %collective-permute-start.10 = (bf16[4,96,256]{2,1,0:T(8,128)(2,1)S(1)}, bf16[4,96,256]{2,1,0:T(8,128)(2,1)S(1)}, u32[]{:S(2)}, u32[]{:S(2)}) collective-permute-start(bf16[4,96,256]{2,1,0:T(8,128)(2,1)S(1)} %collective-permute-done.8), channel_id=1, source_target_pairs={{384,352},{416,384},{448,416},{480,448},{0,480},{32,0},{64,32},{38... | collective-permute-start | bytes 589832 | tf_op jit(solution)/shard_map/ppermute | solution.py:204
  80.0 5.0 %collective-permute-start.12 = (bf16[4,96,256]{2,1,0:T(8,128)(2,1)S(1)}, bf16[4,96,256]{2,1,0:T(8,128)(2,1)S(1)}, u32[]{:S(2)}, u32[]{:S(2)}) collective-permute-start(bf16[4,96,256]{2,1,0:T(8,128)(2,1)S(1)} %collective-permute-done.10), channel_id=1, source_target_pairs={{352,320},{384,352},{416,384},{448,416},{480,448},{0,480},{32,0},{... | collective-permute-start | bytes 589832 | tf_op jit(solution)/shard_map/ppermute | solution.py:204
  85.9 2.6 %collective-permute-done.12 = bf16[4,96,256]{2,1,0:T(8,128)(2,1)S(1)} collective-permute-done((bf16[4,96,256]{2,1,0:T(8,128)(2,1)S(1)}, bf16[4,96,256]{2,1,0:T(8,128)(2,1)S(1)}, u32[]{:S(2)}, u32[]{:S(2)}) %collective-permute-start.12) | collective-permute-done | bytes 196640 | tf_op jit(solution)/shard_map/ppermute | solution.py:204
  88.4 5.0 %collective-permute-start.14 = (bf16[4,96,256]{2,1,0:T(8,128)(2,1)S(1)}, bf16[4,96,256]{2,1,0:T(8,128)(2,1)S(1)}, u32[]{:S(2)}, u32[]{:S(2)}) collective-permute-start(bf16[4,96,256]{2,1,0:T(8,128)(2,1)S(1)} %collective-permute-done.12), channel_id=1, source_target_pairs={{320,288},{352,320},{384,352},{416,384},{448,416},{480,448},{0,480... | collective-permute-start | bytes 589832 | tf_op jit(solution)/shard_map/ppermute | solution.py:204
  94.2 3.9 %collective-permute-done.14 = bf16[4,96,256]{2,1,0:T(8,128)(2,1)S(1)} collective-permute-done((bf16[4,96,256]{2,1,0:T(8,128)(2,1)S(1)}, bf16[4,96,256]{2,1,0:T(8,128)(2,1)S(1)}, u32[]{:S(2)}, u32[]{:S(2)}) %collective-permute-start.14) | collective-permute-done | bytes 196640 | tf_op jit(solution)/shard_map/ppermute | solution.py:204
  104.0 4.7 %collective-permute-start.20 = (bf16[528,384]{1,0:T(8,128)(2,1)S(1)}, bf16[528,384]{1,0:T(8,128)(2,1)S(1)}, u32[]{:S(2)}, u32[]{:S(2)}) collective-permute-start(bf16[528,384]{1,0:T(8,128)(2,1)S(1)} %shard_map.60), channel_id=1, source_target_pairs={{0,24},{8,0},{16,8},{24,16},{1,25},{9,1},{17,9},{25,17},{2,26},{10... | collective-permute-start | bytes 1216520 | tf_op jit(solution)/shard_map/ppermute | solution.py:35
  114.6 9.1 %collective-permute-done.19.p1 = bf16[528,384]{1,0:T(8,128)(2,1)S(1)} collective-permute-done((bf16[528,384]{1,0:T(8,128)(2,1)S(1)}, bf16[528,384]{1,0:T(8,128)(2,1)S(1)}, u32[]{:S(2)}, u32[]{:S(2)}) %collective-permute-start.19) | collective-permute-done | bytes 405536 | tf_op jit(solution)/shard_map/ppermute | solution.py:35
  124.2 9.7 %collective-permute-start.22 = (bf16[512,384]{1,0:T(8,128)(2,1)S(1)}, bf16[512,384]{1,0:T(8,128)(2,1)S(1)}, u32[]{:S(2)}, u32[]{:S(2)}) collective-permute-start(bf16[512,384]{1,0:T(8,128)(2,1)S(1)} %shard_map.62.mine_ref), channel_id=1, source_target_pairs={{0,1},{1,0},{2,3},{3,2},{4,5},{5,4},{6,7},{7,6},{8,9},{9,8},{10,11... | collective-permute-start | bytes 1179656 | tf_op jit(solution)/shard_map/ppermute | solution.py:35
  134.0 2.2 %copy-done = bf16[512,4096]{1,0:T(8,128)(2,1)S(1)} copy-done((bf16[512,4096]{1,0:T(8,128)(2,1)S(1)}, bf16[512,4096]{1,0:T(8,128)(2,1)}, u32[]{:S(2)}) %copy-start) | copy-done | bytes 4194328
  136.2 3.5 %shard_map.55.w_ref = bf16[4,512,1024]{2,1,0:T(8,128)(2,1)S(1)} custom-call(s32[4]{0:T(128)S(1)} %fusion.2.cols_ref, bf16[512,4096]{1,0:T(8,128)(2,1)S(1)} %copy-done, bf16[512,4096]{1,0:T(8,128)(2,1)} %collective-permute-done.got_ref), custom_call_target="tpu_custom_call" | custom-call | tf_op jit(solution)/shard_map/pallas_call | solution.py:218
  140.4 4.4 %collective-permute-start.25 = (bf16[512,384]{1,0:T(8,128)(2,1)S(1)}, bf16[512,384]{1,0:T(8,128)(2,1)S(1)}, u32[]{:S(2)}, u32[]{:S(2)}) collective-permute-start(bf16[512,384]{1,0:T(8,128)(2,1)S(1)} %shard_map.66), channel_id=1, source_target_pairs={{0,6},{2,0},{4,2},{6,4},{1,7},{3,1},{5,3},{7,5},{8,14},{10,8},{12,... | collective-permute-start | bytes 1179656 | tf_op jit(solution)/shard_map/ppermute | solution.py:35
  148.2 3.6 %collective-permute-start.23 = (bf16[512,384]{1,0:T(8,128)(2,1)S(1)}, bf16[512,384]{1,0:T(8,128)(2,1)S(1)}, u32[]{:S(2)}, u32[]{:S(2)}) collective-permute-start(bf16[512,384]{1,0:T(8,128)(2,1)S(1)} %shard_map.64), channel_id=1, source_target_pairs={{0,4},{2,6},{4,0},{6,2},{1,5},{3,7},{5,1},{7,3},{8,12},{10,14},{12... | collective-permute-start | bytes 1179656 | tf_op jit(solution)/shard_map/ppermute | solution.py:35
  153.3 14.2 %collective-permute-done.24.g2 = bf16[512,384]{1,0:T(8,128)(2,1)S(1)} collective-permute-done((bf16[512,384]{1,0:T(8,128)(2,1)S(1)}, bf16[512,384]{1,0:T(8,128)(2,1)S(1)}, u32[]{:S(2)}, u32[]{:S(2)}) %collective-permute-start.24) | collective-permute-done | bytes 393248 | tf_op jit(solution)/shard_map/ppermute | solution.py:35
  (100 shorter events, 46.4 us)
Async XLA Ops:
  0.0 134.0 %collective-permute-start = (bf16[512,4096]{1,0:T(8,128)(2,1)}, bf16[512,4096]{1,0:T(8,128)(2,1)}, u32[]{:S(2)}, u32[]{:S(2)}) collective-permute-start(bf16[512,4096]{1,0:T(8,128)(2,1)} %mine_ref.1), channel_id=1, source_target_pairs={{0,1},{1,0},{2,3},{3,2},{4,5},{5,4},{6,7},{7,6},{8,9},{9,8},{10,11... | collective-permute-start | bytes 12582920 | tf_op jit(solution)/shard_map/ppermute | solution.py:35
  10.4 10.1 %all-to-all-start = ((bf16[4,96,256]{2,1,0:T(8,128)(2,1)}), bf16[4,96,256]{2,1,0:T(8,128)(2,1)}, u32[]{:S(2)}, u32[]{:S(2)}) async-start(bf16[4,96,256]{2,1,0:T(8,128)(2,1)} %shard_map.57), calls=%async_computation | async-start | bytes 393216 | tf_op jit(solution)/shard_map/all_to_all | solution.py:191
  20.5 16.9 %collective-permute-start.1 = (bf16[4,96,256]{2,1,0:T(8,128)(2,1)}, bf16[4,96,256]{2,1,0:T(8,128)(2,1)}, u32[]{:S(2)}, u32[]{:S(2)}) collective-permute-start(bf16[4,96,256]{2,1,0:T(8,128)(2,1)} %all-to-all-done), channel_id=1, source_target_pairs={{0,32},{32,64},{64,96},{96,128},{128,160},{160,192},{192,224},{224... | collective-permute-start | bytes 589832 | tf_op jit(solution)/shard_map/ppermute | solution.py:201
  28.7 18.0 %collective-permute-start.16 = (bf16[528,384]{1,0:T(8,128)(2,1)S(1)}, bf16[528,384]{1,0:T(8,128)(2,1)S(1)}, u32[]{:S(2)}, u32[]{:S(2)}) collective-permute-start(bf16[528,384]{1,0:T(8,128)(2,1)S(1)} %get-tuple-element.10.q_ref), channel_id=1, source_target_pairs={{0,16},{8,24},{16,0},{24,8},{1,17},{9,25},{17,1},{25,9},{2,18},{10... | collective-permute-start | bytes 1216520 | tf_op jit(solution)/shard_map/ppermute | solution.py:35
  30.9 22.7 %collective-permute-start.17 = (bf16[528,384]{1,0:T(8,128)(2,1)S(1)}, bf16[528,384]{1,0:T(8,128)(2,1)S(1)}, u32[]{:S(2)}, u32[]{:S(2)}) collective-permute-start(bf16[528,384]{1,0:T(8,128)(2,1)S(1)} %get-tuple-element.10.q_ref), channel_id=1, source_target_pairs={{0,8},{8,16},{16,24},{24,0},{1,9},{9,17},{17,25},{25,1},{2,10},{10... | collective-permute-start | bytes 1216520 | tf_op jit(solution)/shard_map/ppermute | solution.py:35
  34.0 20.4 %collective-permute-start.18 = (bf16[528,384]{1,0:T(8,128)(2,1)S(1)}, bf16[528,384]{1,0:T(8,128)(2,1)S(1)}, u32[]{:S(2)}, u32[]{:S(2)}) collective-permute-start(bf16[528,384]{1,0:T(8,128)(2,1)S(1)} %get-tuple-element.10.q_ref), channel_id=1, source_target_pairs={{0,24},{8,0},{16,8},{24,16},{1,25},{9,1},{17,9},{25,17},{2,26},{10... | collective-permute-start | bytes 1216520 | tf_op jit(solution)/shard_map/ppermute | solution.py:35
  37.4 8.0 %collective-permute-start.2 = (bf16[4,96,256]{2,1,0:T(8,128)(2,1)}, bf16[4,96,256]{2,1,0:T(8,128)(2,1)}, u32[]{:S(2)}, u32[]{:S(2)}) collective-permute-start(bf16[4,96,256]{2,1,0:T(8,128)(2,1)} %all-to-all-done), channel_id=1, source_target_pairs={{0,480},{32,0},{64,32},{96,64},{128,96},{160,128},{192,160},{1,481... | collective-permute-start | bytes 589832 | tf_op jit(solution)/shard_map/ppermute | solution.py:204
  45.4 11.1 %collective-permute-start.3 = (bf16[4,96,256]{2,1,0:T(8,128)(2,1)}, bf16[4,96,256]{2,1,0:T(8,128)(2,1)}, u32[]{:S(2)}, u32[]{:S(2)}) collective-permute-start(bf16[4,96,256]{2,1,0:T(8,128)(2,1)} %collective-permute-done.1), channel_id=1, source_target_pairs={{32,64},{64,96},{96,128},{128,160},{160,192},{192,224},{224,256},{... | collective-permute-start | bytes 589832 | tf_op jit(solution)/shard_map/ppermute | solution.py:201
  46.7 10.6 %collective-permute-start.4 = (bf16[4,96,256]{2,1,0:T(8,128)(2,1)}, bf16[4,96,256]{2,1,0:T(8,128)(2,1)}, u32[]{:S(2)}, u32[]{:S(2)}) collective-permute-start(bf16[4,96,256]{2,1,0:T(8,128)(2,1)} %collective-permute-done.2), channel_id=1, source_target_pairs={{480,448},{0,480},{32,0},{64,32},{96,64},{128,96},{160,128},{481,4... | collective-permute-start | bytes 589832 | tf_op jit(solution)/shard_map/ppermute | solution.py:204
  57.3 7.5 %collective-permute-start.6 = (bf16[4,96,256]{2,1,0:T(8,128)(2,1)}, bf16[4,96,256]{2,1,0:T(8,128)(2,1)S(1)}, u32[]{:S(2)}, u32[]{:S(2)}) collective-permute-start(bf16[4,96,256]{2,1,0:T(8,128)(2,1)} %collective-permute-done.4), channel_id=1, source_target_pairs={{448,416},{480,448},{0,480},{32,0},{64,32},{96,64},{128,96},{449,4... | collective-permute-start | bytes 589832 | tf_op jit(solution)/shard_map/ppermute | solution.py:204
  64.8 7.5 %collective-permute-start.8 = (bf16[4,96,256]{2,1,0:T(8,128)(2,1)S(1)}, bf16[4,96,256]{2,1,0:T(8,128)(2,1)S(1)}, u32[]{:S(2)}, u32[]{:S(2)}) collective-permute-start(bf16[4,96,256]{2,1,0:T(8,128)(2,1)S(1)} %collective-permute-done.6), channel_id=1, source_target_pairs={{416,384},{448,416},{480,448},{0,480},{32,0},{64,32},{96,64},{417,... | collective-permute-start | bytes 589832 | tf_op jit(solution)/shard_map/ppermute | solution.py:204
  69.8 7.6 %collective-permute-start.9 = (bf16[4,96,256]{2,1,0:T(8,128)(2,1)S(1)}, bf16[4,96,256]{2,1,0:T(8,128)(2,1)S(1)}, u32[]{:S(2)}, u32[]{:S(2)}) collective-permute-start(bf16[4,96,256]{2,1,0:T(8,128)(2,1)S(1)} %collective-permute-done.7), channel_id=1, source_target_pairs={{128,160},{160,192},{192,224},{224,256},{256,288},{288,320},{320,3... | collective-permute-start | bytes 589832 | tf_op jit(solution)/shard_map/ppermute | solution.py:201
  72.3 7.6 %collective-permute-start.10 = (bf16[4,96,256]{2,1,0:T(8,128)(2,1)S(1)}, bf16[4,96,256]{2,1,0:T(8,128)(2,1)S(1)}, u32[]{:S(2)}, u32[]{:S(2)}) collective-permute-start(bf16[4,96,256]{2,1,0:T(8,128)(2,1)S(1)} %collective-permute-done.8), channel_id=1, source_target_pairs={{384,352},{416,384},{448,416},{480,448},{0,480},{32,0},{64,32},{38... | collective-permute-start | bytes 589832 | tf_op jit(solution)/shard_map/ppermute | solution.py:204
  77.4 7.6 %collective-permute-start.11 = (bf16[4,96,256]{2,1,0:T(8,128)(2,1)S(1)}, bf16[4,96,256]{2,1,0:T(8,128)(2,1)S(1)}, u32[]{:S(2)}, u32[]{:S(2)}) collective-permute-start(bf16[4,96,256]{2,1,0:T(8,128)(2,1)S(1)} %collective-permute-done.9), channel_id=1, source_target_pairs={{160,192},{192,224},{224,256},{256,288},{288,320},{320,352},{352,3... | collective-permute-start | bytes 589832 | tf_op jit(solution)/shard_map/ppermute | solution.py:201
  80.0 8.5 %collective-permute-start.12 = (bf16[4,96,256]{2,1,0:T(8,128)(2,1)S(1)}, bf16[4,96,256]{2,1,0:T(8,128)(2,1)S(1)}, u32[]{:S(2)}, u32[]{:S(2)}) collective-permute-start(bf16[4,96,256]{2,1,0:T(8,128)(2,1)S(1)} %collective-permute-done.10), channel_id=1, source_target_pairs={{352,320},{384,352},{416,384},{448,416},{480,448},{0,480},{32,0},{... | collective-permute-start | bytes 589832 | tf_op jit(solution)/shard_map/ppermute | solution.py:204
  85.0 8.4 %collective-permute-start.13 = (bf16[4,96,256]{2,1,0:T(8,128)(2,1)S(1)}, bf16[4,96,256]{2,1,0:T(8,128)(2,1)S(1)}, u32[]{:S(2)}, u32[]{:S(2)}) collective-permute-start(bf16[4,96,256]{2,1,0:T(8,128)(2,1)S(1)} %collective-permute-done.11), channel_id=1, source_target_pairs={{192,224},{224,256},{256,288},{288,320},{320,352},{352,384},{384,4... | collective-permute-start | bytes 589832 | tf_op jit(solution)/shard_map/ppermute | solution.py:201
  88.4 9.7 %collective-permute-start.14 = (bf16[4,96,256]{2,1,0:T(8,128)(2,1)S(1)}, bf16[4,96,256]{2,1,0:T(8,128)(2,1)S(1)}, u32[]{:S(2)}, u32[]{:S(2)}) collective-permute-start(bf16[4,96,256]{2,1,0:T(8,128)(2,1)S(1)} %collective-permute-done.12), channel_id=1, source_target_pairs={{320,288},{352,320},{384,352},{416,384},{448,416},{480,448},{0,480... | collective-permute-start | bytes 589832 | tf_op jit(solution)/shard_map/ppermute | solution.py:204
  100.1 14.5 %collective-permute-start.21 = (bf16[528,384]{1,0:T(8,128)(2,1)S(1)}, bf16[528,384]{1,0:T(8,128)(2,1)S(1)}, u32[]{:S(2)}, u32[]{:S(2)}) collective-permute-start(bf16[528,384]{1,0:T(8,128)(2,1)S(1)} %shard_map.61), channel_id=1, source_target_pairs={{0,8},{8,16},{16,24},{24,0},{1,9},{9,17},{17,25},{25,1},{2,10},{10... | collective-permute-start | bytes 1216520 | tf_op jit(solution)/shard_map/ppermute | solution.py:35
  104.0 10.6 %collective-permute-start.20 = (bf16[528,384]{1,0:T(8,128)(2,1)S(1)}, bf16[528,384]{1,0:T(8,128)(2,1)S(1)}, u32[]{:S(2)}, u32[]{:S(2)}) collective-permute-start(bf16[528,384]{1,0:T(8,128)(2,1)S(1)} %shard_map.60), channel_id=1, source_target_pairs={{0,24},{8,0},{16,8},{24,16},{1,25},{9,1},{17,9},{25,17},{2,26},{10... | collective-permute-start | bytes 1216520 | tf_op jit(solution)/shard_map/ppermute | solution.py:35
  110.7 13.0 %collective-permute-start.19 = (bf16[528,384]{1,0:T(8,128)(2,1)S(1)}, bf16[528,384]{1,0:T(8,128)(2,1)S(1)}, u32[]{:S(2)}, u32[]{:S(2)}) collective-permute-start(bf16[528,384]{1,0:T(8,128)(2,1)S(1)} %shard_map.59), channel_id=1, source_target_pairs={{0,16},{8,24},{16,0},{24,8},{1,17},{9,25},{17,1},{25,9},{2,18},{10... | collective-permute-start | bytes 1216520 | tf_op jit(solution)/shard_map/ppermute | solution.py:35
  124.2 15.5 %collective-permute-start.22 = (bf16[512,384]{1,0:T(8,128)(2,1)S(1)}, bf16[512,384]{1,0:T(8,128)(2,1)S(1)}, u32[]{:S(2)}, u32[]{:S(2)}) collective-permute-start(bf16[512,384]{1,0:T(8,128)(2,1)S(1)} %shard_map.62.mine_ref), channel_id=1, source_target_pairs={{0,1},{1,0},{2,3},{3,2},{4,5},{5,4},{6,7},{7,6},{8,9},{9,8},{10,11... | collective-permute-start | bytes 1179656 | tf_op jit(solution)/shard_map/ppermute | solution.py:35
  140.4 12.8 %collective-permute-start.25 = (bf16[512,384]{1,0:T(8,128)(2,1)S(1)}, bf16[512,384]{1,0:T(8,128)(2,1)S(1)}, u32[]{:S(2)}, u32[]{:S(2)}) collective-permute-start(bf16[512,384]{1,0:T(8,128)(2,1)S(1)} %shard_map.66), channel_id=1, source_target_pairs={{0,6},{2,0},{4,2},{6,4},{1,7},{3,1},{5,3},{7,5},{8,14},{10,8},{12,... | collective-permute-start | bytes 1179656 | tf_op jit(solution)/shard_map/ppermute | solution.py:35
  145.5 21.9 %collective-permute-start.24 = (bf16[512,384]{1,0:T(8,128)(2,1)S(1)}, bf16[512,384]{1,0:T(8,128)(2,1)S(1)}, u32[]{:S(2)}, u32[]{:S(2)}) collective-permute-start(bf16[512,384]{1,0:T(8,128)(2,1)S(1)} %shard_map.65), channel_id=1, source_target_pairs={{0,2},{2,4},{4,6},{6,0},{1,3},{3,5},{5,7},{7,1},{8,10},{10,12},{12... | collective-permute-start | bytes 1179656 | tf_op jit(solution)/shard_map/ppermute | solution.py:35
  148.2 19.3 %collective-permute-start.23 = (bf16[512,384]{1,0:T(8,128)(2,1)S(1)}, bf16[512,384]{1,0:T(8,128)(2,1)S(1)}, u32[]{:S(2)}, u32[]{:S(2)}) collective-permute-start(bf16[512,384]{1,0:T(8,128)(2,1)S(1)} %shard_map.64), channel_id=1, source_target_pairs={{0,4},{2,6},{4,0},{6,2},{1,5},{3,7},{5,1},{7,3},{8,12},{10,14},{12... | collective-permute-start | bytes 1179656 | tf_op jit(solution)/shard_map/ppermute | solution.py:35
  (19 other events, 149.8 us)

commit v5 on v4

--- a/solution.py
+++ b/solution.py
@@ -53,7 +53,21 @@
         out_ref[y, :, HD:] = v_ref[y * SL : (y + 1) * SL, :]
 
 
-def own_kernel(code_ref, q_ref, k_ref, v_ref, qx_ref, o_ref, lse_ref):
+def query_kernel(code_ref, q_ref, out_ref):
+    lane = lax.broadcasted_iota(jnp.int32, (16, TOK), 1)
+    codes = jnp.zeros((16, TOK), jnp.float32)
+    for i in range(HEADS * TOP):
+        codes = jnp.where(lane == i, code_ref[i].astype(jnp.float32), codes)
+    codes = codes.astype(jnp.bfloat16)
+    for h in range(HEADS):
+        q = q_ref[:, h * HD : (h + 1) * HD].T
+        for y in range(NY):
+            out_ref[y, h * HD : (h + 1) * HD, :] = q
+    for y in range(NY):
+        out_ref[y, HALF:, :] = codes
+
+
+def own_kernel(q_ref, k_ref, v_ref, o_ref, lse_ref):
     keep = lax.broadcasted_iota(jnp.int32, (TOK, TOK), 0) <= lax.broadcasted_iota(
         jnp.int32, (TOK, TOK), 1
     )
@@ -62,7 +76,6 @@
     rows = []
     for h in range(HEADS):
         q = q_ref[:, h * HD : (h + 1) * HD].T
-        qx_ref[h * HD : (h + 1) * HD, :] = q
         s = jnp.dot(k, q, preferred_element_type=jnp.float32)
         s = jnp.where(keep, s * COEF, DEAD)
         top = jnp.max(s, axis=0, keepdims=True)
@@ -72,14 +85,16 @@
         o_ref[h * HD : (h + 1) * HD, :] = o.astype(jnp.bfloat16)
         rows.append(top + jnp.log2(total))
     lse_ref[...] = jnp.concatenate(rows + rows, axis=0)
-    lane = lax.broadcasted_iota(jnp.int32, (16, TOK), 1)
-    codes = jnp.zeros((16, TOK), jnp.float32)
-    for i in range(HEADS * TOP):
-        codes = jnp.where(lane == i, code_ref[i].astype(jnp.float32), codes)
-    qx_ref[HALF:, :] = codes.astype(jnp.bfloat16)
-
-
-def slices_of(code_ref, kv_ref, q_ref, o_ref, base):
+
+
+def first_kernel(row_ref, out_ref, sem):
+    copy = pltpu.make_async_copy(row_ref, out_ref.at[pl.ds(0, NY)], sem.at[0])
+    copy.start()
+    copy.wait()
+
+
+def slices_kernel(home_ref, code_ref, kv_ref, q_ref, o_ref, *, s):
+    base = home_ref[s] * HEADS * TOP
     rows = []
     for h in range(HEADS):
         codes = [code_ref[base + h * TOP + j] for j in range(TOP)]
@@ -87,11 +102,11 @@
         bias = [jnp.where(c < NONE, 0.0, DEAD).astype(jnp.float32) for c in codes]
         k = jnp.concatenate([t[:, :HD] for t in picked], axis=0)
         v = jnp.concatenate([t[:, HD:] for t in picked], axis=0)
-        s = jnp.dot(k, q_ref[h * HD : (h + 1) * HD, :], preferred_element_type=jnp.float32)
-        s = [s[j * SL : (j + 1) * SL] * COEF + bias[j] for j in range(TOP)]
-        s = jnp.concatenate(s, axis=0)
-        top = jnp.max(s, axis=0, keepdims=True)
-        p = jnp.exp2(s - top)
+        t = jnp.dot(k, q_ref[h * HD : (h + 1) * HD, :], preferred_element_type=jnp.float32)
+        t = [t[j * SL : (j + 1) * SL] * COEF + bias[j] for j in range(TOP)]
+        t = jnp.concatenate(t, axis=0)
+        top = jnp.max(t, axis=0, keepdims=True)
+        p = jnp.exp2(t - top)
         total = jnp.sum(p, axis=0, keepdims=True)
         o = tn(v, p.astype(jnp.bfloat16)) * (1.0 / total)
         o_ref[h * HD : (h + 1) * HD, :] = o.astype(jnp.bfloat16)
@@ -101,10 +116,6 @@
         rows += [hi, mid, lse - hi - mid]
     rows += [jnp.zeros((4, TOK), jnp.float32)]
     o_ref[HALF:, :] = jnp.concatenate(rows, axis=0).astype(jnp.bfloat16)
-
-
-def slices_kernel(code_ref, kv_ref, q_ref, o_ref, *, base):
-    slices_of(code_ref, kv_ref, q_ref, o_ref, base)
 
 
 def merge_kernel(own_ref, lse_ref, p0, p1, p2, p3, out_ref):
@@ -195,25 +206,40 @@
     for d, place in enumerate(SLOTS):
         slot = jnp.where(offset == d, place, slot)
     code = jnp.where(ids < z * NY + y, slot * NY + ids % NY, NONE)
-    kept = [row]
+    anyw = pl.BlockSpec(memory_space=pl.ANY)
+    kv = pallas(
+        2,
+        first_kernel,
+        in_specs=[anyw],
+        out_specs=anyw,
+        out_shape=bf16(NZ * NY, SL, 2 * HD),
+        scratch_shapes=[pltpu.SemaphoreType.DMA((1,))],
+    )(row)
+
+    def put(kv, a, at):
+        return lax.dynamic_update_slice(kv, a, (at * NY, 0, 0))
+
     p = m = row
     for k in range(1, HOPS + 1):
         p = lax.ppermute(p, "z", ahead(k))
-        kept.append(p)
+        kv = put(kv, p, 2 * k - 1)
         if k < HOPS:
             m = lax.ppermute(m, "z", astern(k))
-            kept.append(m)
-    w_got = send(out_weight, "core", 1)
-    qx, own, own_lse = pallas(
+            kv = put(kv, m, 2 * k)
+    qx = pallas(
+        60, query_kernel, in_specs=[smem, vmem], out_specs=vmem, out_shape=bf16(NY, EXT, TOK)
+    )(code, queries)
+    qs = lax.all_to_all(qx, "y", 0, 0)
+    own, own_lse = pallas(
         8,
         own_kernel,
-        in_specs=[smem] + [vmem] * 3,
-        out_specs=[vmem] * 3,
-        out_shape=[bf16(EXT, TOK), bf16(HALF, TOK), f32(2 * HEADS, TOK)],
-    )(code, queries, keys, values)
+        in_specs=[vmem] * 3,
+        out_specs=[vmem] * 2,
+        out_shape=[bf16(HALF, TOK), f32(2 * HEADS, TOK)],
+    )(queries, keys, values)
+    w_got = send(out_weight, "core", 1)
+    codes = qs[:, HALF, : HEADS * TOP].astype(jnp.int32).reshape(-1)
     order = (2, 1, 3)
-    qs = [send(qx, "y", s) for s in order]
-    codes = jnp.stack([a[HALF, : HEADS * TOP] for a in qs], axis=0).astype(jnp.int32).reshape(-1)
     cols = (x + jnp.arange(NX, dtype=jnp.int32)) % NX * 2 + core
     w = pallas(
         12,
@@ -228,22 +254,20 @@
             pltpu.SemaphoreType.DMA((NX,)),
         ],
     )(cols, out_weight, w_got)
-    kv = jnp.concatenate(kept, axis=0)
-
-    def attend(code, q, base):
+    homes = (y - jnp.arange(NY, dtype=jnp.int32)) % NY
+
+    def attend(s):
+        q = lax.dynamic_index_in_dim(qs, homes[s], keepdims=False)
         return pallas(
             12,
-            functools.partial(slices_kernel, base=base),
-            in_specs=[smem] + [vmem] * 2,
+            functools.partial(slices_kernel, s=s),
+            in_specs=[smem] * 2 + [vmem] * 2,
             out_specs=vmem,
             out_shape=bf16(EXT, TOK),
-        )(code, kv, q)
-
-    back = []
-    for i, s in enumerate(order):
-        part = attend(codes, qs[i], i * HEADS * TOP)
-        back.append(send(part, "y", -s))
-    home = attend(code, qx, 0)
+        )(homes, codes, kv, q)
+
+    back = [send(attend(s), "y", -s) for s in order]
+    home = attend(0)
     att = pallas(
         8, merge_kernel, in_specs=[vmem] * 6, out_specs=vmem, out_shape=bf16(HALF, TOK)
     )(own, own_lse, home, *back)

time: 170 us -> 160 us (0.941)
  the two profiles are of different devices: /device:TPU:1 before, /device:TPU:384 now
where the time goes in v5:
time: 160 us; the launch traced here: 159 us
  starting transfers between devices  71.4 us (45%)
  waiting for transfers between devices  48.2 us (30%)
  Pallas kernels  21.3 us (13%)
  local copies, waits for them, and re-layouts  8.35 us (5%)
  between operations  8.09 us (5%)
    ppermute x8, waiting for transfers between devices, steps(): p = lax.ppermute(p, 'z', ahead(k))  26.8 us
    ppermute x8, starting transfers between devices, send(): return lax.ppermute(a, axis, [(i, (i + s) % n) for i in range(n)])  26.5 us
    ppermute x7, starting transfers between devices, steps(): m = lax.ppermute(m, 'z', astern(k))  18.8 us
    ppermute x8, waiting for transfers between devices, send(): return lax.ppermute(a, axis, [(i, (i + s) % n) for i in range(n)])  18.5 us
    ppermute x8, starting transfers between devices, steps(): p = lax.ppermute(p, 'z', ahead(k))  17.3 us
    pallas_call x4, Pallas kernels, attend(): pallas(12, functools.partial(slices_kernel, s=s), in_specs=[smem] * 2 + [...  7.8 us
    all_to_all x1, starting transfers between devices, steps(): row = lax.all_to_all(packed, 'y', 0, 0)  4.46 us
    all_to_all x1, starting transfers between devices, steps(): qs = lax.all_to_all(qx, 'y', 0, 0)  4.35 us
  transfers between devices with their start and end apart: 25, of which 10 were waited for; matrix products, arithmetic and copies ran while one was open for 5% of the time, Pallas kernels for 12%

profile of v5, /device:TPU:384, one launch (start us, length us, event | category | flops | bytes accessed | tf_op | source)
XLA Modules:
  0.0 158.6 jit_solution(13484480510640640682)
XLA Ops:
  3.6 4.5 %all-to-all-start.1 = ((bf16[4,96,256]{2,1,0:T(8,128)(2,1)}), bf16[4,96,256]{2,1,0:T(8,128)(2,1)S(1)}, u32[]{:S(2)}, u32[]{:S(2)}) async-start(bf16[4,96,256]{2,1,0:T(8,128)(2,1)} %shard_map.58), calls=%async_computation.1 | async-start | bytes 393216 | tf_op jit(solution)/shard_map/all_to_all | solution.py:202
  9.5 2.4 %shard_map.57 = bf16[4,528,384]{2,1,0:T(8,128)(2,1)} custom-call(s32[12]{0:T(128)} %compare_select_fusion.21.code_ref, bf16[384,512]{1,0:T(8,128)(2,1)} %q_ref.3), custom_call_target="tpu_custom_call" | custom-call | tf_op jit(solution)/shard_map/pallas_call | solution.py:229
  11.8 2.8 %all-to-all-done.1.row_ref = bf16[4,96,256]{2,1,0:T(8,128)(2,1)S(1)} async-done(((bf16[4,96,256]{2,1,0:T(8,128)(2,1)}), bf16[4,96,256]{2,1,0:T(8,128)(2,1)S(1)}, u32[]{:S(2)}, u32[]{:S(2)}) %all-to-all-start.1) | async-done | bytes 196640 | tf_op jit(solution)/shard_map/all_to_all | solution.py:202
  14.7 4.3 %all-to-all-start = ((bf16[4,528,384]{2,1,0:T(8,128)(2,1)}), bf16[4,528,384]{2,1,0:T(8,128)(2,1)}, u32[]{:S(2)}, u32[]{:S(2)}) async-start(bf16[4,528,384]{2,1,0:T(8,128)(2,1)} %shard_map.57), calls=%async_computation | async-start | bytes 3244032 | tf_op jit(solution)/shard_map/all_to_all | solution.py:232
  19.0 2.9 %collective-permute-start.1 = (bf16[4,96,256]{2,1,0:T(8,128)(2,1)S(1)}, bf16[4,96,256]{2,1,0:T(8,128)(2,1)}, u32[]{:S(2)}, u32[]{:S(2)}) collective-permute-start(bf16[4,96,256]{2,1,0:T(8,128)(2,1)S(1)} %all-to-all-done.1.row_ref), channel_id=1, source_target_pairs={{0,32},{32,64},{64,96},{96,128},{128,160},{160,192},{192,224},{224... | collective-permute-start | bytes 589832 | tf_op jit(solution)/shard_map/ppermute | solution.py:224
  31.1 2.9 %collective-permute-start.3 = (bf16[4,96,256]{2,1,0:T(8,128)(2,1)}, bf16[4,96,256]{2,1,0:T(8,128)(2,1)S(1)}, u32[]{:S(2)}, u32[]{:S(2)}) collective-permute-start(bf16[4,96,256]{2,1,0:T(8,128)(2,1)} %collective-permute-done.1), channel_id=1, source_target_pairs={{32,64},{64,96},{96,128},{128,160},{160,192},{192,224},{224,256},{... | collective-permute-start | bytes 589832 | tf_op jit(solution)/shard_map/ppermute | solution.py:224
  35.7 4.4 %collective-permute-done.3 = bf16[4,96,256]{2,1,0:T(8,128)(2,1)S(1)} collective-permute-done((bf16[4,96,256]{2,1,0:T(8,128)(2,1)}, bf16[4,96,256]{2,1,0:T(8,128)(2,1)S(1)}, u32[]{:S(2)}, u32[]{:S(2)}) %collective-permute-start.3) | collective-permute-done | bytes 196640 | tf_op jit(solution)/shard_map/ppermute | solution.py:224
  42.8 6.1 %collective-permute-done.5 = bf16[4,96,256]{2,1,0:T(8,128)(2,1)S(1)} collective-permute-done((bf16[4,96,256]{2,1,0:T(8,128)(2,1)S(1)}, bf16[4,96,256]{2,1,0:T(8,128)(2,1)S(1)}, u32[]{:S(2)}, u32[]{:S(2)}) %collective-permute-start.5) | collective-permute-done | bytes 196640 | tf_op jit(solution)/shard_map/ppermute | solution.py:224
  52.2 5.5 %collective-permute-done.7 = bf16[4,96,256]{2,1,0:T(8,128)(2,1)S(1)} collective-permute-done((bf16[4,96,256]{2,1,0:T(8,128)(2,1)S(1)}, bf16[4,96,256]{2,1,0:T(8,128)(2,1)S(1)}, u32[]{:S(2)}, u32[]{:S(2)}) %collective-permute-start.7) | collective-permute-done | bytes 196640 | tf_op jit(solution)/shard_map/ppermute | solution.py:224
  59.6 5.1 %collective-permute-start.10 = (bf16[4,96,256]{2,1,0:T(8,128)(2,1)S(1)}, bf16[4,96,256]{2,1,0:T(8,128)(2,1)}, u32[]{:S(2)}, u32[]{:S(2)}) collective-permute-start(bf16[4,96,256]{2,1,0:T(8,128)(2,1)S(1)} %collective-permute-done.8), channel_id=1, source_target_pairs={{384,352},{416,384},{448,416},{480,448},{0,480},{32,0},{64,32},{38... | collective-permute-start | bytes 589832 | tf_op jit(solution)/shard_map/ppermute | solution.py:227
  68.3 5.2 %collective-permute-start.12 = (bf16[4,96,256]{2,1,0:T(8,128)(2,1)}, bf16[4,96,256]{2,1,0:T(8,128)(2,1)S(1)}, u32[]{:S(2)}, u32[]{:S(2)}) collective-permute-start(bf16[4,96,256]{2,1,0:T(8,128)(2,1)} %collective-permute-done.10), channel_id=1, source_target_pairs={{352,320},{384,352},{416,384},{448,416},{480,448},{0,480},{32,0},{... | collective-permute-start | bytes 589832 | tf_op jit(solution)/shard_map/ppermute | solution.py:227
  78.9 5.1 %collective-permute-start.14 = (bf16[4,96,256]{2,1,0:T(8,128)(2,1)S(1)}, bf16[4,96,256]{2,1,0:T(8,128)(2,1)S(1)}, u32[]{:S(2)}, u32[]{:S(2)}) collective-permute-start(bf16[4,96,256]{2,1,0:T(8,128)(2,1)S(1)} %collective-permute-done.12), channel_id=1, source_target_pairs={{320,288},{352,320},{384,352},{416,384},{448,416},{480,448},{0,480... | collective-permute-start | bytes 589832 | tf_op jit(solution)/shard_map/ppermute | solution.py:227
  85.0 2.4 %collective-permute-done.13 = bf16[4,96,256]{2,1,0:T(8,128)(2,1)S(1)} collective-permute-done((bf16[4,96,256]{2,1,0:T(8,128)(2,1)}, bf16[4,96,256]{2,1,0:T(8,128)(2,1)S(1)}, u32[]{:S(2)}, u32[]{:S(2)}) %collective-permute-start.13) | collective-permute-done | bytes 196640 | tf_op jit(solution)/shard_map/ppermute | solution.py:224
  89.3 6.8 %collective-permute-done.15 = bf16[4,96,256]{2,1,0:T(8,128)(2,1)S(1)} collective-permute-done((bf16[4,96,256]{2,1,0:T(8,128)(2,1)S(1)}, bf16[4,96,256]{2,1,0:T(8,128)(2,1)S(1)}, u32[]{:S(2)}, u32[]{:S(2)}) %collective-permute-start.15) | collective-permute-done | bytes 196640 | tf_op jit(solution)/shard_map/ppermute | solution.py:224
  98.1 4.5 %collective-permute-start.18 = (bf16[528,384]{1,0:T(8,128)(2,1)S(1)}, bf16[528,384]{1,0:T(8,128)(2,1)S(1)}, u32[]{:S(2)}, u32[]{:S(2)}) collective-permute-start(bf16[528,384]{1,0:T(8,128)(2,1)S(1)} %shard_map.63), channel_id=1, source_target_pairs={{0,8},{8,16},{16,24},{24,0},{1,9},{9,17},{17,25},{25,1},{2,10},{10... | collective-permute-start | bytes 1216520 | tf_op jit(solution)/shard_map/ppermute | solution.py:35
  104.6 2.8 %collective-permute-start.17 = (bf16[528,384]{1,0:T(8,128)(2,1)S(1)}, bf16[528,384]{1,0:T(8,128)(2,1)S(1)}, u32[]{:S(2)}, u32[]{:S(2)}) collective-permute-start(bf16[528,384]{1,0:T(8,128)(2,1)S(1)} %shard_map.62), channel_id=1, source_target_pairs={{0,24},{8,0},{16,8},{24,16},{1,25},{9,1},{17,9},{25,17},{2,26},{10... | collective-permute-start | bytes 1216520 | tf_op jit(solution)/shard_map/ppermute | solution.py:35
  107.4 2.0 %shard_map.61 = bf16[528,384]{1,0:T(8,128)(2,1)S(1)} custom-call(s32[4]{0:T(128)S(1)} %and_select_fusion.3.home_ref, s32[48]{0:T(128)S(1)} %reshape.8.code_ref, bf16[64,96,256]{2,1,0:T(8,128)(2,1)S(1)} %constant_dynamic-update-slice_fusion.kv_ref, bf16[528,384]{1,0:T(8,128)(2,1)S(1)} %get-tuple-element.11.q_ref), custom_call_target="tpu_custom_call" | custom-call | tf_op jit(solution)/shard_map/pallas_call | solution.py:261
  109.3 4.6 %collective-permute-start.16 = (bf16[528,384]{1,0:T(8,128)(2,1)S(1)}, bf16[528,384]{1,0:T(8,128)(2,1)S(1)}, u32[]{:S(2)}, u32[]{:S(2)}) collective-permute-start(bf16[528,384]{1,0:T(8,128)(2,1)S(1)} %shard_map.61), channel_id=1, source_target_pairs={{0,16},{8,24},{16,0},{24,8},{1,17},{9,25},{17,1},{25,9},{2,18},{10... | collective-permute-start | bytes 1216520 | tf_op jit(solution)/shard_map/ppermute | solution.py:35
  117.4 3.3 %collective-permute-done.16.p1 = bf16[528,384]{1,0:T(8,128)(2,1)S(1)} collective-permute-done((bf16[528,384]{1,0:T(8,128)(2,1)S(1)}, bf16[528,384]{1,0:T(8,128)(2,1)S(1)}, u32[]{:S(2)}, u32[]{:S(2)}) %collective-permute-start.16) | collective-permute-done | bytes 405536 | tf_op jit(solution)/shard_map/ppermute | solution.py:35
  123.1 2.2 %copy-done = bf16[512,4096]{1,0:T(8,128)(2,1)S(1)} copy-done((bf16[512,4096]{1,0:T(8,128)(2,1)S(1)}, bf16[512,4096]{1,0:T(8,128)(2,1)}, u32[]{:S(2)}) %copy-start) | copy-done | bytes 4194328
  125.3 3.5 %shard_map.55.w_ref = bf16[4,512,1024]{2,1,0:T(8,128)(2,1)S(1)} custom-call(s32[4]{0:T(128)S(1)} %fusion.3.cols_ref, bf16[512,4096]{1,0:T(8,128)(2,1)S(1)} %copy-done, bf16[512,4096]{1,0:T(8,128)(2,1)} %collective-permute-done.got_ref), custom_call_target="tpu_custom_call" | custom-call | tf_op jit(solution)/shard_map/pallas_call | solution.py:244
  129.5 4.7 %collective-permute-start.22 = (bf16[512,384]{1,0:T(8,128)(2,1)S(1)}, bf16[512,384]{1,0:T(8,128)(2,1)S(1)}, u32[]{:S(2)}, u32[]{:S(2)}) collective-permute-start(bf16[512,384]{1,0:T(8,128)(2,1)S(1)} %shard_map.68), channel_id=1, source_target_pairs={{0,6},{2,0},{4,2},{6,4},{1,7},{3,1},{5,3},{7,5},{8,14},{10,8},{12,... | collective-permute-start | bytes 1179656 | tf_op jit(solution)/shard_map/ppermute | solution.py:35
  137.6 4.2 %collective-permute-start.20 = (bf16[512,384]{1,0:T(8,128)(2,1)S(1)}, bf16[512,384]{1,0:T(8,128)(2,1)S(1)}, u32[]{:S(2)}, u32[]{:S(2)}) collective-permute-start(bf16[512,384]{1,0:T(8,128)(2,1)S(1)} %shard_map.66), channel_id=1, source_target_pairs={{0,4},{2,6},{4,0},{6,2},{1,5},{3,7},{5,1},{7,3},{8,12},{10,14},{12... | collective-permute-start | bytes 1179656 | tf_op jit(solution)/shard_map/ppermute | solution.py:35
  143.3 14.4 %collective-permute-done.21.g2 = bf16[512,384]{1,0:T(8,128)(2,1)S(1)} collective-permute-done((bf16[512,384]{1,0:T(8,128)(2,1)S(1)}, bf16[512,384]{1,0:T(8,128)(2,1)S(1)}, u32[]{:S(2)}, u32[]{:S(2)}) %collective-permute-start.21) | collective-permute-done | bytes 393248 | tf_op jit(solution)/shard_map/ppermute | solution.py:35
  (73 shorter events, 43.9 us)
Async XLA Ops:
  0.0 123.1 %collective-permute-start = (bf16[512,4096]{1,0:T(8,128)(2,1)}, bf16[512,4096]{1,0:T(8,128)(2,1)}, u32[]{:S(2)}, u32[]{:S(2)}) collective-permute-start(bf16[512,4096]{1,0:T(8,128)(2,1)} %mine_ref.1), channel_id=1, source_target_pairs={{0,1},{1,0},{2,3},{3,2},{4,5},{5,4},{6,7},{7,6},{8,9},{9,8},{10,11... | collective-permute-start | bytes 12582920 | tf_op jit(solution)/shard_map/ppermute | solution.py:35
  3.6 11.1 %all-to-all-start.1 = ((bf16[4,96,256]{2,1,0:T(8,128)(2,1)}), bf16[4,96,256]{2,1,0:T(8,128)(2,1)S(1)}, u32[]{:S(2)}, u32[]{:S(2)}) async-start(bf16[4,96,256]{2,1,0:T(8,128)(2,1)} %shard_map.58), calls=%async_computation.1 | async-start | bytes 393216 | tf_op jit(solution)/shard_map/all_to_all | solution.py:202
  14.7 59.9 %all-to-all-start = ((bf16[4,528,384]{2,1,0:T(8,128)(2,1)}), bf16[4,528,384]{2,1,0:T(8,128)(2,1)}, u32[]{:S(2)}, u32[]{:S(2)}) async-start(bf16[4,528,384]{2,1,0:T(8,128)(2,1)} %shard_map.57), calls=%async_computation | async-start | bytes 3244032 | tf_op jit(solution)/shard_map/all_to_all | solution.py:232
  19.0 12.1 %collective-permute-start.1 = (bf16[4,96,256]{2,1,0:T(8,128)(2,1)S(1)}, bf16[4,96,256]{2,1,0:T(8,128)(2,1)}, u32[]{:S(2)}, u32[]{:S(2)}) collective-permute-start(bf16[4,96,256]{2,1,0:T(8,128)(2,1)S(1)} %all-to-all-done.1.row_ref), channel_id=1, source_target_pairs={{0,32},{32,64},{64,96},{96,128},{128,160},{160,192},{192,224},{224... | collective-permute-start | bytes 589832 | tf_op jit(solution)/shard_map/ppermute | solution.py:224
  22.0 12.1 %collective-permute-start.2 = (bf16[4,96,256]{2,1,0:T(8,128)(2,1)S(1)}, bf16[4,96,256]{2,1,0:T(8,128)(2,1)S(1)}, u32[]{:S(2)}, u32[]{:S(2)}) collective-permute-start(bf16[4,96,256]{2,1,0:T(8,128)(2,1)S(1)} %all-to-all-done.1.row_ref), channel_id=1, source_target_pairs={{0,480},{32,0},{64,32},{96,64},{128,96},{160,128},{192,160},{1,481... | collective-permute-start | bytes 589832 | tf_op jit(solution)/shard_map/ppermute | solution.py:227
  31.1 9.0 %collective-permute-start.3 = (bf16[4,96,256]{2,1,0:T(8,128)(2,1)}, bf16[4,96,256]{2,1,0:T(8,128)(2,1)S(1)}, u32[]{:S(2)}, u32[]{:S(2)}) collective-permute-start(bf16[4,96,256]{2,1,0:T(8,128)(2,1)} %collective-permute-done.1), channel_id=1, source_target_pairs={{32,64},{64,96},{96,128},{128,160},{160,192},{192,224},{224,256},{... | collective-permute-start | bytes 589832 | tf_op jit(solution)/shard_map/ppermute | solution.py:224
  34.1 8.0 %collective-permute-start.4 = (bf16[4,96,256]{2,1,0:T(8,128)(2,1)S(1)}, bf16[4,96,256]{2,1,0:T(8,128)(2,1)S(1)}, u32[]{:S(2)}, u32[]{:S(2)}) collective-permute-start(bf16[4,96,256]{2,1,0:T(8,128)(2,1)S(1)} %collective-permute-done.2), channel_id=1, source_target_pairs={{480,448},{0,480},{32,0},{64,32},{96,64},{128,96},{160,128},{481,4... | collective-permute-start | bytes 589832 | tf_op jit(solution)/shard_map/ppermute | solution.py:227
  40.1 8.8 %collective-permute-start.5 = (bf16[4,96,256]{2,1,0:T(8,128)(2,1)S(1)}, bf16[4,96,256]{2,1,0:T(8,128)(2,1)S(1)}, u32[]{:S(2)}, u32[]{:S(2)}) collective-permute-start(bf16[4,96,256]{2,1,0:T(8,128)(2,1)S(1)} %collective-permute-done.3), channel_id=1, source_target_pairs={{64,96},{96,128},{128,160},{160,192},{192,224},{224,256},{256,288}... | collective-permute-start | bytes 589832 | tf_op jit(solution)/shard_map/ppermute | solution.py:224
  42.0 8.8 %collective-permute-start.6 = (bf16[4,96,256]{2,1,0:T(8,128)(2,1)S(1)}, bf16[4,96,256]{2,1,0:T(8,128)(2,1)S(1)}, u32[]{:S(2)}, u32[]{:S(2)}) collective-permute-start(bf16[4,96,256]{2,1,0:T(8,128)(2,1)S(1)} %collective-permute-done.4), channel_id=1, source_target_pairs={{448,416},{480,448},{0,480},{32,0},{64,32},{96,64},{128,96},{449,4... | collective-permute-start | bytes 589832 | tf_op jit(solution)/shard_map/ppermute | solution.py:227
  48.9 8.8 %collective-permute-start.7 = (bf16[4,96,256]{2,1,0:T(8,128)(2,1)S(1)}, bf16[4,96,256]{2,1,0:T(8,128)(2,1)S(1)}, u32[]{:S(2)}, u32[]{:S(2)}) collective-permute-start(bf16[4,96,256]{2,1,0:T(8,128)(2,1)S(1)} %collective-permute-done.5), channel_id=1, source_target_pairs={{96,128},{128,160},{160,192},{192,224},{224,256},{256,288},{288,32... | collective-permute-start | bytes 589832 | tf_op jit(solution)/shard_map/ppermute | solution.py:224
  50.8 8.8 %collective-permute-start.8 = (bf16[4,96,256]{2,1,0:T(8,128)(2,1)S(1)}, bf16[4,96,256]{2,1,0:T(8,128)(2,1)S(1)}, u32[]{:S(2)}, u32[]{:S(2)}) collective-permute-start(bf16[4,96,256]{2,1,0:T(8,128)(2,1)S(1)} %collective-permute-done.6), channel_id=1, source_target_pairs={{416,384},{448,416},{480,448},{0,480},{32,0},{64,32},{96,64},{417,... | collective-permute-start | bytes 589832 | tf_op jit(solution)/shard_map/ppermute | solution.py:227
  57.6 8.8 %collective-permute-start.9 = (bf16[4,96,256]{2,1,0:T(8,128)(2,1)S(1)}, bf16[4,96,256]{2,1,0:T(8,128)(2,1)S(1)}, u32[]{:S(2)}, u32[]{:S(2)}) collective-permute-start(bf16[4,96,256]{2,1,0:T(8,128)(2,1)S(1)} %collective-permute-done.7), channel_id=1, source_target_pairs={{128,160},{160,192},{192,224},{224,256},{256,288},{288,320},{320,3... | collective-permute-start | bytes 589832 | tf_op jit(solution)/shard_map/ppermute | solution.py:224
  59.6 8.8 %collective-permute-start.10 = (bf16[4,96,256]{2,1,0:T(8,128)(2,1)S(1)}, bf16[4,96,256]{2,1,0:T(8,128)(2,1)}, u32[]{:S(2)}, u32[]{:S(2)}) collective-permute-start(bf16[4,96,256]{2,1,0:T(8,128)(2,1)S(1)} %collective-permute-done.8), channel_id=1, source_target_pairs={{384,352},{416,384},{448,416},{480,448},{0,480},{32,0},{64,32},{38... | collective-permute-start | bytes 589832 | tf_op jit(solution)/shard_map/ppermute | solution.py:227
  66.4 10.5 %collective-permute-start.11 = (bf16[4,96,256]{2,1,0:T(8,128)(2,1)S(1)}, bf16[4,96,256]{2,1,0:T(8,128)(2,1)}, u32[]{:S(2)}, u32[]{:S(2)}) collective-permute-start(bf16[4,96,256]{2,1,0:T(8,128)(2,1)S(1)} %collective-permute-done.9), channel_id=1, source_target_pairs={{160,192},{192,224},{224,256},{256,288},{288,320},{320,352},{352,3... | collective-permute-start | bytes 589832 | tf_op jit(solution)/shard_map/ppermute | solution.py:224
  68.3 10.5 %collective-permute-start.12 = (bf16[4,96,256]{2,1,0:T(8,128)(2,1)}, bf16[4,96,256]{2,1,0:T(8,128)(2,1)S(1)}, u32[]{:S(2)}, u32[]{:S(2)}) collective-permute-start(bf16[4,96,256]{2,1,0:T(8,128)(2,1)} %collective-permute-done.10), channel_id=1, source_target_pairs={{352,320},{384,352},{416,384},{448,416},{480,448},{0,480},{32,0},{... | collective-permute-start | bytes 589832 | tf_op jit(solution)/shard_map/ppermute | solution.py:227
  76.9 10.4 %collective-permute-start.13 = (bf16[4,96,256]{2,1,0:T(8,128)(2,1)}, bf16[4,96,256]{2,1,0:T(8,128)(2,1)S(1)}, u32[]{:S(2)}, u32[]{:S(2)}) collective-permute-start(bf16[4,96,256]{2,1,0:T(8,128)(2,1)} %collective-permute-done.11), channel_id=1, source_target_pairs={{192,224},{224,256},{256,288},{288,320},{320,352},{352,384},{384,4... | collective-permute-start | bytes 589832 | tf_op jit(solution)/shard_map/ppermute | solution.py:224
  78.9 10.4 %collective-permute-start.14 = (bf16[4,96,256]{2,1,0:T(8,128)(2,1)S(1)}, bf16[4,96,256]{2,1,0:T(8,128)(2,1)S(1)}, u32[]{:S(2)}, u32[]{:S(2)}) collective-permute-start(bf16[4,96,256]{2,1,0:T(8,128)(2,1)S(1)} %collective-permute-done.12), channel_id=1, source_target_pairs={{320,288},{352,320},{384,352},{416,384},{448,416},{480,448},{0,480... | collective-permute-start | bytes 589832 | tf_op jit(solution)/shard_map/ppermute | solution.py:227
  87.3 8.8 %collective-permute-start.15 = (bf16[4,96,256]{2,1,0:T(8,128)(2,1)S(1)}, bf16[4,96,256]{2,1,0:T(8,128)(2,1)S(1)}, u32[]{:S(2)}, u32[]{:S(2)}) collective-permute-start(bf16[4,96,256]{2,1,0:T(8,128)(2,1)S(1)} %collective-permute-done.13), channel_id=1, source_target_pairs={{224,256},{256,288},{288,320},{320,352},{352,384},{384,416},{416,4... | collective-permute-start | bytes 589832 | tf_op jit(solution)/shard_map/ppermute | solution.py:224
  98.1 19.3 %collective-permute-start.18 = (bf16[528,384]{1,0:T(8,128)(2,1)S(1)}, bf16[528,384]{1,0:T(8,128)(2,1)S(1)}, u32[]{:S(2)}, u32[]{:S(2)}) collective-permute-start(bf16[528,384]{1,0:T(8,128)(2,1)S(1)} %shard_map.63), channel_id=1, source_target_pairs={{0,8},{8,16},{16,24},{24,0},{1,9},{9,17},{17,25},{25,1},{2,10},{10... | collective-permute-start | bytes 1216520 | tf_op jit(solution)/shard_map/ppermute | solution.py:35
  104.6 12.7 %collective-permute-start.17 = (bf16[528,384]{1,0:T(8,128)(2,1)S(1)}, bf16[528,384]{1,0:T(8,128)(2,1)S(1)}, u32[]{:S(2)}, u32[]{:S(2)}) collective-permute-start(bf16[528,384]{1,0:T(8,128)(2,1)S(1)} %shard_map.62), channel_id=1, source_target_pairs={{0,24},{8,0},{16,8},{24,16},{1,25},{9,1},{17,9},{25,17},{2,26},{10... | collective-permute-start | bytes 1216520 | tf_op jit(solution)/shard_map/ppermute | solution.py:35
  109.3 11.3 %collective-permute-start.16 = (bf16[528,384]{1,0:T(8,128)(2,1)S(1)}, bf16[528,384]{1,0:T(8,128)(2,1)S(1)}, u32[]{:S(2)}, u32[]{:S(2)}) collective-permute-start(bf16[528,384]{1,0:T(8,128)(2,1)S(1)} %shard_map.61), channel_id=1, source_target_pairs={{0,16},{8,24},{16,0},{24,8},{1,17},{9,25},{17,1},{25,9},{2,18},{10... | collective-permute-start | bytes 1216520 | tf_op jit(solution)/shard_map/ppermute | solution.py:35
  129.5 13.7 %collective-permute-start.22 = (bf16[512,384]{1,0:T(8,128)(2,1)S(1)}, bf16[512,384]{1,0:T(8,128)(2,1)S(1)}, u32[]{:S(2)}, u32[]{:S(2)}) collective-permute-start(bf16[512,384]{1,0:T(8,128)(2,1)S(1)} %shard_map.68), channel_id=1, source_target_pairs={{0,6},{2,0},{4,2},{6,4},{1,7},{3,1},{5,3},{7,5},{8,14},{10,8},{12,... | collective-permute-start | bytes 1179656 | tf_op jit(solution)/shard_map/ppermute | solution.py:35
  134.9 22.8 %collective-permute-start.21 = (bf16[512,384]{1,0:T(8,128)(2,1)S(1)}, bf16[512,384]{1,0:T(8,128)(2,1)S(1)}, u32[]{:S(2)}, u32[]{:S(2)}) collective-permute-start(bf16[512,384]{1,0:T(8,128)(2,1)S(1)} %shard_map.67), channel_id=1, source_target_pairs={{0,2},{2,4},{4,6},{6,0},{1,3},{3,5},{5,7},{7,1},{8,10},{10,12},{12... | collective-permute-start | bytes 1179656 | tf_op jit(solution)/shard_map/ppermute | solution.py:35
  137.6 20.1 %collective-permute-start.20 = (bf16[512,384]{1,0:T(8,128)(2,1)S(1)}, bf16[512,384]{1,0:T(8,128)(2,1)S(1)}, u32[]{:S(2)}, u32[]{:S(2)}) collective-permute-start(bf16[512,384]{1,0:T(8,128)(2,1)S(1)} %shard_map.66), channel_id=1, source_target_pairs={{0,4},{2,6},{4,0},{6,2},{1,5},{3,7},{5,1},{7,3},{8,12},{10,14},{12... | collective-permute-start | bytes 1179656 | tf_op jit(solution)/shard_map/ppermute | solution.py:35
  (5 other events, 43.8 us)

commit v6 on v5

--- a/solution.py
+++ b/solution.py
@@ -93,8 +93,13 @@
     copy.wait()
 
 
-def slices_kernel(home_ref, code_ref, kv_ref, q_ref, o_ref, *, s):
-    base = home_ref[s] * HEADS * TOP
+def slices_kernel(home_ref, code_ref, kv_ref, q_ref, *outs, shifts):
+    for s, o_ref in zip(shifts, outs):
+        slices_of(home_ref[s], code_ref, kv_ref, q_ref, o_ref)
+
+
+def slices_of(home, code_ref, kv_ref, q_ref, o_ref):
+    base = home * HEADS * TOP
     rows = []
     for h in range(HEADS):
         codes = [code_ref[base + h * TOP + j] for j in range(TOP)]
@@ -102,7 +107,7 @@
         bias = [jnp.where(c < NONE, 0.0, DEAD).astype(jnp.float32) for c in codes]
         k = jnp.concatenate([t[:, :HD] for t in picked], axis=0)
         v = jnp.concatenate([t[:, HD:] for t in picked], axis=0)
-        t = jnp.dot(k, q_ref[h * HD : (h + 1) * HD, :], preferred_element_type=jnp.float32)
+        t = jnp.dot(k, q_ref[home, h * HD : (h + 1) * HD, :], preferred_element_type=jnp.float32)
         t = [t[j * SL : (j + 1) * SL] * COEF + bias[j] for j in range(TOP)]
         t = jnp.concatenate(t, axis=0)
         top = jnp.max(t, axis=0, keepdims=True)
@@ -256,18 +261,18 @@
     )(cols, out_weight, w_got)
     homes = (y - jnp.arange(NY, dtype=jnp.int32)) % NY
 
-    def attend(s):
-        q = lax.dynamic_index_in_dim(qs, homes[s], keepdims=False)
+    def attend(shifts):
         return pallas(
             12,
-            functools.partial(slices_kernel, s=s),
+            functools.partial(slices_kernel, shifts=shifts),
             in_specs=[smem] * 2 + [vmem] * 2,
-            out_specs=vmem,
-            out_shape=bf16(EXT, TOK),
-        )(homes, codes, kv, q)
-
-    back = [send(attend(s), "y", -s) for s in order]
-    home = attend(0)
+            out_specs=[vmem] * len(shifts),
+            out_shape=[bf16(EXT, TOK)] * len(shifts),
+        )(homes, codes, kv, qs)
+
+    parts = attend(order)
+    back = [send(part, "y", -s) for s, part in zip(order, parts)]
+    (home,) = attend((0,))
     att = pallas(
         8, merge_kernel, in_specs=[vmem] * 6, out_specs=vmem, out_shape=bf16(HALF, TOK)
     )(own, own_lse, home, *back)

time: 160 us -> 155 us (0.969)
  the two profiles are of different devices: /device:TPU:384 before, /device:TPU:256 now
where the time goes in v6:
time: 155 us; the launch traced here: 154 us
  waiting for transfers between devices  65.4 us (42%)
  starting transfers between devices  58.5 us (38%)
  Pallas kernels  21.8 us (14%)
  local copies, waits for them, and re-layouts  6.14 us (4%)
    ppermute x8, waiting for transfers between devices, steps(): p = lax.ppermute(p, 'z', ahead(k))  40.4 us
    ppermute x8, starting transfers between devices, send(): return lax.ppermute(a, axis, [(i, (i + s) % n) for i in range(n)])  27 us
    ppermute x8, waiting for transfers between devices, send(): return lax.ppermute(a, axis, [(i, (i + s) % n) for i in range(n)])  19.1 us
    ppermute x8, starting transfers between devices, steps(): p = lax.ppermute(p, 'z', ahead(k))  17.3 us
    pallas_call x2, Pallas kernels, attend(): pallas(12, functools.partial(slices_kernel, shifts=shifts), in_specs=[sme...  8.39 us
    all_to_all x1, waiting for transfers between devices, steps(): row = lax.all_to_all(packed, 'y', 0, 0)  5.78 us
    ppermute x7, starting transfers between devices, steps(): m = lax.ppermute(m, 'z', astern(k))  5.4 us
    all_to_all x1, starting transfers between devices, steps(): row = lax.all_to_all(packed, 'y', 0, 0)  4.46 us
  transfers between devices with their start and end apart: 25, of which 11 were waited for; matrix products, arithmetic and copies ran while one was open for 3% of the time, Pallas kernels for 13%

profile of v6, /device:TPU:256, one launch (start us, length us, event | category | flops | bytes accessed | tf_op | source)
XLA Modules:
  0.0 153.7 jit_solution(936372804572726583)
XLA Ops:
  3.6 4.5 %all-to-all-start.1 = ((bf16[4,96,256]{2,1,0:T(8,128)(2,1)}), bf16[4,96,256]{2,1,0:T(8,128)(2,1)S(1)}, u32[]{:S(2)}, u32[]{:S(2)}) async-start(bf16[4,96,256]{2,1,0:T(8,128)(2,1)} %shard_map.58), calls=%async_computation.1 | async-start | bytes 393216 | tf_op jit(solution)/shard_map/all_to_all | solution.py:207
  8.9 5.8 %all-to-all-done.1.row_ref = bf16[4,96,256]{2,1,0:T(8,128)(2,1)S(1)} async-done(((bf16[4,96,256]{2,1,0:T(8,128)(2,1)}), bf16[4,96,256]{2,1,0:T(8,128)(2,1)S(1)}, u32[]{:S(2)}, u32[]{:S(2)}) %all-to-all-start.1) | async-done | bytes 196640 | tf_op jit(solution)/shard_map/all_to_all | solution.py:207
  14.7 2.9 %collective-permute-start.1 = (bf16[4,96,256]{2,1,0:T(8,128)(2,1)S(1)}, bf16[4,96,256]{2,1,0:T(8,128)(2,1)}, u32[]{:S(2)}, u32[]{:S(2)}) collective-permute-start(bf16[4,96,256]{2,1,0:T(8,128)(2,1)S(1)} %all-to-all-done.1.row_ref), channel_id=1, source_target_pairs={{0,32},{32,64},{64,96},{96,128},{128,160},{160,192},{192,224},{224... | collective-permute-start | bytes 589832 | tf_op jit(solution)/shard_map/ppermute | solution.py:229
  18.8 2.4 %shard_map.57 = bf16[4,528,384]{2,1,0:T(8,128)(2,1)} custom-call(s32[12]{0:T(128)} %compare_select_fusion.21.code_ref, bf16[384,512]{1,0:T(8,128)(2,1)} %q_ref.3), custom_call_target="tpu_custom_call" | custom-call | tf_op jit(solution)/shard_map/pallas_call | solution.py:234
  21.2 4.4 %all-to-all-start = ((bf16[4,528,384]{2,1,0:T(8,128)(2,1)}), bf16[4,528,384]{2,1,0:T(8,128)(2,1)}, u32[]{:S(2)}, u32[]{:S(2)}) async-start(bf16[4,528,384]{2,1,0:T(8,128)(2,1)} %shard_map.57), calls=%async_computation | async-start | bytes 3244032 | tf_op jit(solution)/shard_map/all_to_all | solution.py:237
  25.8 2.9 %collective-permute-start.3 = (bf16[4,96,256]{2,1,0:T(8,128)(2,1)}, bf16[4,96,256]{2,1,0:T(8,128)(2,1)S(1)}, u32[]{:S(2)}, u32[]{:S(2)}) collective-permute-start(bf16[4,96,256]{2,1,0:T(8,128)(2,1)} %collective-permute-done.1), channel_id=1, source_target_pairs={{32,64},{64,96},{96,128},{128,160},{160,192},{192,224},{224,256},{... | collective-permute-start | bytes 589832 | tf_op jit(solution)/shard_map/ppermute | solution.py:229
  30.4 4.4 %collective-permute-done.3 = bf16[4,96,256]{2,1,0:T(8,128)(2,1)S(1)} collective-permute-done((bf16[4,96,256]{2,1,0:T(8,128)(2,1)}, bf16[4,96,256]{2,1,0:T(8,128)(2,1)S(1)}, u32[]{:S(2)}, u32[]{:S(2)}) %collective-permute-start.3) | collective-permute-done | bytes 196640 | tf_op jit(solution)/shard_map/ppermute | solution.py:229
  37.5 6.1 %collective-permute-done.5 = bf16[4,96,256]{2,1,0:T(8,128)(2,1)S(1)} collective-permute-done((bf16[4,96,256]{2,1,0:T(8,128)(2,1)S(1)}, bf16[4,96,256]{2,1,0:T(8,128)(2,1)S(1)}, u32[]{:S(2)}, u32[]{:S(2)}) %collective-permute-start.5) | collective-permute-done | bytes 196640 | tf_op jit(solution)/shard_map/ppermute | solution.py:229
  46.2 6.1 %collective-permute-done.7 = bf16[4,96,256]{2,1,0:T(8,128)(2,1)S(1)} collective-permute-done((bf16[4,96,256]{2,1,0:T(8,128)(2,1)S(1)}, bf16[4,96,256]{2,1,0:T(8,128)(2,1)S(1)}, u32[]{:S(2)}, u32[]{:S(2)}) %collective-permute-start.7) | collective-permute-done | bytes 196640 | tf_op jit(solution)/shard_map/ppermute | solution.py:229
  55.7 5.4 %collective-permute-done.9 = bf16[4,96,256]{2,1,0:T(8,128)(2,1)S(1)} collective-permute-done((bf16[4,96,256]{2,1,0:T(8,128)(2,1)S(1)}, bf16[4,96,256]{2,1,0:T(8,128)(2,1)S(1)}, u32[]{:S(2)}, u32[]{:S(2)}) %collective-permute-start.9) | collective-permute-done | bytes 196640 | tf_op jit(solution)/shard_map/ppermute | solution.py:229
  65.5 4.6 %collective-permute-done.11 = bf16[4,96,256]{2,1,0:T(8,128)(2,1)} collective-permute-done((bf16[4,96,256]{2,1,0:T(8,128)(2,1)S(1)}, bf16[4,96,256]{2,1,0:T(8,128)(2,1)}, u32[]{:S(2)}, u32[]{:S(2)}) %collective-permute-start.11) | collective-permute-done | bytes 196640 | tf_op jit(solution)/shard_map/ppermute | solution.py:229
  73.8 7.0 %collective-permute-done.13 = bf16[4,96,256]{2,1,0:T(8,128)(2,1)S(1)} collective-permute-done((bf16[4,96,256]{2,1,0:T(8,128)(2,1)}, bf16[4,96,256]{2,1,0:T(8,128)(2,1)S(1)}, u32[]{:S(2)}, u32[]{:S(2)}) %collective-permute-start.13) | collective-permute-done | bytes 196640 | tf_op jit(solution)/shard_map/ppermute | solution.py:229
  82.7 6.8 %collective-permute-done.15 = bf16[4,96,256]{2,1,0:T(8,128)(2,1)S(1)} collective-permute-done((bf16[4,96,256]{2,1,0:T(8,128)(2,1)S(1)}, bf16[4,96,256]{2,1,0:T(8,128)(2,1)S(1)}, u32[]{:S(2)}, u32[]{:S(2)}) %collective-permute-start.15) | collective-permute-done | bytes 196640 | tf_op jit(solution)/shard_map/ppermute | solution.py:229
  89.5 5.5 %shard_map.61 = (bf16[528,384]{1,0:T(8,128)(2,1)S(1)}, bf16[528,384]{1,0:T(8,128)(2,1)S(1)}, bf16[528,384]{1,0:T(8,128)(2,1)S(1)}) custom-call(s32[4]{0:T(128)S(1)} %and_select_fusion.3.home_ref, s32[48]{0:T(128)S(1)} %reshape.8.code_ref, bf16[64,96,256]{2,1,0:T(8,128)(2,1)S(1)} %constant_dynamic-update-slice_fusion.kv_ref, ...), custom_call_target="tpu_custom_call" | custom-call | tf_op jit(solution)/shard_map/pallas_call | solution.py:265
  95.1 6.5 %collective-permute-start.16 = (bf16[528,384]{1,0:T(8,128)(2,1)S(1)}, bf16[528,384]{1,0:T(8,128)(2,1)S(1)}, u32[]{:S(2)}, u32[]{:S(2)}) collective-permute-start(bf16[528,384]{1,0:T(8,128)(2,1)S(1)} %get-tuple-element.12), channel_id=1, source_target_pairs={{0,16},{8,24},{16,0},{24,8},{1,17},{9,25},{17,1},{25,9},{2,18},{10... | collective-permute-start | bytes 1216520 | tf_op jit(solution)/shard_map/ppermute | solution.py:35
  101.6 3.1 %collective-permute-start.17 = (bf16[528,384]{1,0:T(8,128)(2,1)S(1)}, bf16[528,384]{1,0:T(8,128)(2,1)S(1)}, u32[]{:S(2)}, u32[]{:S(2)}) collective-permute-start(bf16[528,384]{1,0:T(8,128)(2,1)S(1)} %get-tuple-element.13), channel_id=1, source_target_pairs={{0,24},{8,0},{16,8},{24,16},{1,25},{9,1},{17,9},{25,17},{2,26},{10... | collective-permute-start | bytes 1216520 | tf_op jit(solution)/shard_map/ppermute | solution.py:35
  104.7 2.8 %collective-permute-start.18 = (bf16[528,384]{1,0:T(8,128)(2,1)S(1)}, bf16[528,384]{1,0:T(8,128)(2,1)S(1)}, u32[]{:S(2)}, u32[]{:S(2)}) collective-permute-start(bf16[528,384]{1,0:T(8,128)(2,1)S(1)} %get-tuple-element.14), channel_id=1, source_target_pairs={{0,8},{8,16},{16,24},{24,0},{1,9},{9,17},{17,25},{25,1},{2,10},{10... | collective-permute-start | bytes 1216520 | tf_op jit(solution)/shard_map/ppermute | solution.py:35
  108.9 2.8 %shard_map.60.p0 = bf16[528,384]{1,0:T(8,128)(2,1)S(1)} custom-call(s32[4]{0:T(128)S(1)} %and_select_fusion.3.home_ref, s32[48]{0:T(128)S(1)} %reshape.8.code_ref, bf16[64,96,256]{2,1,0:T(8,128)(2,1)S(1)} %constant_dynamic-update-slice_fusion.kv_ref, bf16[4,528,384]{2,1,0:T(8,128)(2,1)} %all-to-all-done.q_ref), custom_call_target="tpu_custom_call" | custom-call | tf_op jit(solution)/shard_map/pallas_call | solution.py:265
  111.8 3.9 %collective-permute-done.18.p3 = bf16[528,384]{1,0:T(8,128)(2,1)S(1)} collective-permute-done((bf16[528,384]{1,0:T(8,128)(2,1)S(1)}, bf16[528,384]{1,0:T(8,128)(2,1)S(1)}, u32[]{:S(2)}, u32[]{:S(2)}) %collective-permute-start.18) | collective-permute-done | bytes 405536 | tf_op jit(solution)/shard_map/ppermute | solution.py:35
  118.2 2.2 %copy-done = bf16[512,4096]{1,0:T(8,128)(2,1)S(1)} copy-done((bf16[512,4096]{1,0:T(8,128)(2,1)S(1)}, bf16[512,4096]{1,0:T(8,128)(2,1)}, u32[]{:S(2)}) %copy-start) | copy-done | bytes 4194328
  120.3 3.5 %shard_map.55.w_ref = bf16[4,512,1024]{2,1,0:T(8,128)(2,1)S(1)} custom-call(s32[4]{0:T(128)S(1)} %fusion.3.cols_ref, bf16[512,4096]{1,0:T(8,128)(2,1)S(1)} %copy-done, bf16[512,4096]{1,0:T(8,128)(2,1)} %collective-permute-done.got_ref), custom_call_target="tpu_custom_call" | custom-call | tf_op jit(solution)/shard_map/pallas_call | solution.py:249
  124.6 4.7 %collective-permute-start.22 = (bf16[512,384]{1,0:T(8,128)(2,1)S(1)}, bf16[512,384]{1,0:T(8,128)(2,1)S(1)}, u32[]{:S(2)}, u32[]{:S(2)}) collective-permute-start(bf16[512,384]{1,0:T(8,128)(2,1)S(1)} %shard_map.66), channel_id=1, source_target_pairs={{0,6},{2,0},{4,2},{6,4},{1,7},{3,1},{5,3},{7,5},{8,14},{10,8},{12,... | collective-permute-start | bytes 1179656 | tf_op jit(solution)/shard_map/ppermute | solution.py:35
  132.6 4.2 %collective-permute-start.20 = (bf16[512,384]{1,0:T(8,128)(2,1)S(1)}, bf16[512,384]{1,0:T(8,128)(2,1)S(1)}, u32[]{:S(2)}, u32[]{:S(2)}) collective-permute-start(bf16[512,384]{1,0:T(8,128)(2,1)S(1)} %shard_map.64), channel_id=1, source_target_pairs={{0,4},{2,6},{4,0},{6,2},{1,5},{3,7},{5,1},{7,3},{8,12},{10,14},{12... | collective-permute-start | bytes 1179656 | tf_op jit(solution)/shard_map/ppermute | solution.py:35
  138.3 14.4 %collective-permute-done.21.g2 = bf16[512,384]{1,0:T(8,128)(2,1)S(1)} collective-permute-done((bf16[512,384]{1,0:T(8,128)(2,1)S(1)}, bf16[512,384]{1,0:T(8,128)(2,1)S(1)}, u32[]{:S(2)}, u32[]{:S(2)}) %collective-permute-start.21) | collective-permute-done | bytes 393248 | tf_op jit(solution)/shard_map/ppermute | solution.py:35
  (69 shorter events, 36.3 us)
Async XLA Ops:
  0.0 118.1 %collective-permute-start = (bf16[512,4096]{1,0:T(8,128)(2,1)}, bf16[512,4096]{1,0:T(8,128)(2,1)}, u32[]{:S(2)}, u32[]{:S(2)}) collective-permute-start(bf16[512,4096]{1,0:T(8,128)(2,1)} %mine_ref.1), channel_id=1, source_target_pairs={{0,1},{1,0},{2,3},{3,2},{4,5},{5,4},{6,7},{7,6},{8,9},{9,8},{10,11... | collective-permute-start | bytes 12582920 | tf_op jit(solution)/shard_map/ppermute | solution.py:35
  3.6 11.1 %all-to-all-start.1 = ((bf16[4,96,256]{2,1,0:T(8,128)(2,1)}), bf16[4,96,256]{2,1,0:T(8,128)(2,1)S(1)}, u32[]{:S(2)}, u32[]{:S(2)}) async-start(bf16[4,96,256]{2,1,0:T(8,128)(2,1)} %shard_map.58), calls=%async_computation.1 | async-start | bytes 393216 | tf_op jit(solution)/shard_map/all_to_all | solution.py:207
  14.7 11.2 %collective-permute-start.1 = (bf16[4,96,256]{2,1,0:T(8,128)(2,1)S(1)}, bf16[4,96,256]{2,1,0:T(8,128)(2,1)}, u32[]{:S(2)}, u32[]{:S(2)}) collective-permute-start(bf16[4,96,256]{2,1,0:T(8,128)(2,1)S(1)} %all-to-all-done.1.row_ref), channel_id=1, source_target_pairs={{0,32},{32,64},{64,96},{96,128},{128,160},{160,192},{192,224},{224... | collective-permute-start | bytes 589832 | tf_op jit(solution)/shard_map/ppermute | solution.py:229
  17.6 11.2 %collective-permute-start.2 = (bf16[4,96,256]{2,1,0:T(8,128)(2,1)S(1)}, bf16[4,96,256]{2,1,0:T(8,128)(2,1)S(1)}, u32[]{:S(2)}, u32[]{:S(2)}) collective-permute-start(bf16[4,96,256]{2,1,0:T(8,128)(2,1)S(1)} %all-to-all-done.1.row_ref), channel_id=1, source_target_pairs={{0,480},{32,0},{64,32},{96,64},{128,96},{160,128},{192,160},{1,481... | collective-permute-start | bytes 589832 | tf_op jit(solution)/shard_map/ppermute | solution.py:232
  21.2 43.5 %all-to-all-start = ((bf16[4,528,384]{2,1,0:T(8,128)(2,1)}), bf16[4,528,384]{2,1,0:T(8,128)(2,1)}, u32[]{:S(2)}, u32[]{:S(2)}) async-start(bf16[4,528,384]{2,1,0:T(8,128)(2,1)} %shard_map.57), calls=%async_computation | async-start | bytes 3244032 | tf_op jit(solution)/shard_map/all_to_all | solution.py:237
  25.8 9.0 %collective-permute-start.3 = (bf16[4,96,256]{2,1,0:T(8,128)(2,1)}, bf16[4,96,256]{2,1,0:T(8,128)(2,1)S(1)}, u32[]{:S(2)}, u32[]{:S(2)}) collective-permute-start(bf16[4,96,256]{2,1,0:T(8,128)(2,1)} %collective-permute-done.1), channel_id=1, source_target_pairs={{32,64},{64,96},{96,128},{128,160},{160,192},{192,224},{224,256},{... | collective-permute-start | bytes 589832 | tf_op jit(solution)/shard_map/ppermute | solution.py:229
  28.8 8.0 %collective-permute-start.4 = (bf16[4,96,256]{2,1,0:T(8,128)(2,1)S(1)}, bf16[4,96,256]{2,1,0:T(8,128)(2,1)S(1)}, u32[]{:S(2)}, u32[]{:S(2)}) collective-permute-start(bf16[4,96,256]{2,1,0:T(8,128)(2,1)S(1)} %collective-permute-done.2), channel_id=1, source_target_pairs={{480,448},{0,480},{32,0},{64,32},{96,64},{128,96},{160,128},{481,4... | collective-permute-start | bytes 589832 | tf_op jit(solution)/shard_map/ppermute | solution.py:232
  34.8 8.8 %collective-permute-start.5 = (bf16[4,96,256]{2,1,0:T(8,128)(2,1)S(1)}, bf16[4,96,256]{2,1,0:T(8,128)(2,1)S(1)}, u32[]{:S(2)}, u32[]{:S(2)}) collective-permute-start(bf16[4,96,256]{2,1,0:T(8,128)(2,1)S(1)} %collective-permute-done.3), channel_id=1, source_target_pairs={{64,96},{96,128},{128,160},{160,192},{192,224},{224,256},{256,288}... | collective-permute-start | bytes 589832 | tf_op jit(solution)/shard_map/ppermute | solution.py:229
  36.8 8.8 %collective-permute-start.6 = (bf16[4,96,256]{2,1,0:T(8,128)(2,1)S(1)}, bf16[4,96,256]{2,1,0:T(8,128)(2,1)S(1)}, u32[]{:S(2)}, u32[]{:S(2)}) collective-permute-start(bf16[4,96,256]{2,1,0:T(8,128)(2,1)S(1)} %collective-permute-done.4), channel_id=1, source_target_pairs={{448,416},{480,448},{0,480},{32,0},{64,32},{96,64},{128,96},{449,4... | collective-permute-start | bytes 589832 | tf_op jit(solution)/shard_map/ppermute | solution.py:232
  43.6 8.8 %collective-permute-start.7 = (bf16[4,96,256]{2,1,0:T(8,128)(2,1)S(1)}, bf16[4,96,256]{2,1,0:T(8,128)(2,1)S(1)}, u32[]{:S(2)}, u32[]{:S(2)}) collective-permute-start(bf16[4,96,256]{2,1,0:T(8,128)(2,1)S(1)} %collective-permute-done.5), channel_id=1, source_target_pairs={{96,128},{128,160},{160,192},{192,224},{224,256},{256,288},{288,32... | collective-permute-start | bytes 589832 | tf_op jit(solution)/shard_map/ppermute | solution.py:229
  45.5 8.8 %collective-permute-start.8 = (bf16[4,96,256]{2,1,0:T(8,128)(2,1)S(1)}, bf16[4,96,256]{2,1,0:T(8,128)(2,1)S(1)}, u32[]{:S(2)}, u32[]{:S(2)}) collective-permute-start(bf16[4,96,256]{2,1,0:T(8,128)(2,1)S(1)} %collective-permute-done.6), channel_id=1, source_target_pairs={{416,384},{448,416},{480,448},{0,480},{32,0},{64,32},{96,64},{417,... | collective-permute-start | bytes 589832 | tf_op jit(solution)/shard_map/ppermute | solution.py:232
  52.4 8.8 %collective-permute-start.9 = (bf16[4,96,256]{2,1,0:T(8,128)(2,1)S(1)}, bf16[4,96,256]{2,1,0:T(8,128)(2,1)S(1)}, u32[]{:S(2)}, u32[]{:S(2)}) collective-permute-start(bf16[4,96,256]{2,1,0:T(8,128)(2,1)S(1)} %collective-permute-done.7), channel_id=1, source_target_pairs={{128,160},{160,192},{192,224},{224,256},{256,288},{288,320},{320,3... | collective-permute-start | bytes 589832 | tf_op jit(solution)/shard_map/ppermute | solution.py:229
  54.3 8.8 %collective-permute-start.10 = (bf16[4,96,256]{2,1,0:T(8,128)(2,1)S(1)}, bf16[4,96,256]{2,1,0:T(8,128)(2,1)}, u32[]{:S(2)}, u32[]{:S(2)}) collective-permute-start(bf16[4,96,256]{2,1,0:T(8,128)(2,1)S(1)} %collective-permute-done.8), channel_id=1, source_target_pairs={{384,352},{416,384},{448,416},{480,448},{0,480},{32,0},{64,32},{38... | collective-permute-start | bytes 589832 | tf_op jit(solution)/shard_map/ppermute | solution.py:232
  61.1 9.0 %collective-permute-start.11 = (bf16[4,96,256]{2,1,0:T(8,128)(2,1)S(1)}, bf16[4,96,256]{2,1,0:T(8,128)(2,1)}, u32[]{:S(2)}, u32[]{:S(2)}) collective-permute-start(bf16[4,96,256]{2,1,0:T(8,128)(2,1)S(1)} %collective-permute-done.9), channel_id=1, source_target_pairs={{160,192},{192,224},{224,256},{256,288},{288,320},{320,352},{352,3... | collective-permute-start | bytes 589832 | tf_op jit(solution)/shard_map/ppermute | solution.py:229
  63.0 9.0 %collective-permute-start.12 = (bf16[4,96,256]{2,1,0:T(8,128)(2,1)}, bf16[4,96,256]{2,1,0:T(8,128)(2,1)S(1)}, u32[]{:S(2)}, u32[]{:S(2)}) collective-permute-start(bf16[4,96,256]{2,1,0:T(8,128)(2,1)} %collective-permute-done.10), channel_id=1, source_target_pairs={{352,320},{384,352},{416,384},{448,416},{480,448},{0,480},{32,0},{... | collective-permute-start | bytes 589832 | tf_op jit(solution)/shard_map/ppermute | solution.py:232
  70.1 10.6 %collective-permute-start.13 = (bf16[4,96,256]{2,1,0:T(8,128)(2,1)}, bf16[4,96,256]{2,1,0:T(8,128)(2,1)S(1)}, u32[]{:S(2)}, u32[]{:S(2)}) collective-permute-start(bf16[4,96,256]{2,1,0:T(8,128)(2,1)} %collective-permute-done.11), channel_id=1, source_target_pairs={{192,224},{224,256},{256,288},{288,320},{320,352},{352,384},{384,4... | collective-permute-start | bytes 589832 | tf_op jit(solution)/shard_map/ppermute | solution.py:229
  72.1 10.6 %collective-permute-start.14 = (bf16[4,96,256]{2,1,0:T(8,128)(2,1)S(1)}, bf16[4,96,256]{2,1,0:T(8,128)(2,1)S(1)}, u32[]{:S(2)}, u32[]{:S(2)}) collective-permute-start(bf16[4,96,256]{2,1,0:T(8,128)(2,1)S(1)} %collective-permute-done.12), channel_id=1, source_target_pairs={{320,288},{352,320},{384,352},{416,384},{448,416},{480,448},{0,480... | collective-permute-start | bytes 589832 | tf_op jit(solution)/shard_map/ppermute | solution.py:232
  80.7 8.8 %collective-permute-start.15 = (bf16[4,96,256]{2,1,0:T(8,128)(2,1)S(1)}, bf16[4,96,256]{2,1,0:T(8,128)(2,1)S(1)}, u32[]{:S(2)}, u32[]{:S(2)}) collective-permute-start(bf16[4,96,256]{2,1,0:T(8,128)(2,1)S(1)} %collective-permute-done.13), channel_id=1, source_target_pairs={{224,256},{256,288},{288,320},{320,352},{352,384},{384,416},{416,4... | collective-permute-start | bytes 589832 | tf_op jit(solution)/shard_map/ppermute | solution.py:229
  95.1 16.7 %collective-permute-start.16 = (bf16[528,384]{1,0:T(8,128)(2,1)S(1)}, bf16[528,384]{1,0:T(8,128)(2,1)S(1)}, u32[]{:S(2)}, u32[]{:S(2)}) collective-permute-start(bf16[528,384]{1,0:T(8,128)(2,1)S(1)} %get-tuple-element.12), channel_id=1, source_target_pairs={{0,16},{8,24},{16,0},{24,8},{1,17},{9,25},{17,1},{25,9},{2,18},{10... | collective-permute-start | bytes 1216520 | tf_op jit(solution)/shard_map/ppermute | solution.py:35
  101.6 10.2 %collective-permute-start.17 = (bf16[528,384]{1,0:T(8,128)(2,1)S(1)}, bf16[528,384]{1,0:T(8,128)(2,1)S(1)}, u32[]{:S(2)}, u32[]{:S(2)}) collective-permute-start(bf16[528,384]{1,0:T(8,128)(2,1)S(1)} %get-tuple-element.13), channel_id=1, source_target_pairs={{0,24},{8,0},{16,8},{24,16},{1,25},{9,1},{17,9},{25,17},{2,26},{10... | collective-permute-start | bytes 1216520 | tf_op jit(solution)/shard_map/ppermute | solution.py:35
  104.7 11.0 %collective-permute-start.18 = (bf16[528,384]{1,0:T(8,128)(2,1)S(1)}, bf16[528,384]{1,0:T(8,128)(2,1)S(1)}, u32[]{:S(2)}, u32[]{:S(2)}) collective-permute-start(bf16[528,384]{1,0:T(8,128)(2,1)S(1)} %get-tuple-element.14), channel_id=1, source_target_pairs={{0,8},{8,16},{16,24},{24,0},{1,9},{9,17},{17,25},{25,1},{2,10},{10... | collective-permute-start | bytes 1216520 | tf_op jit(solution)/shard_map/ppermute | solution.py:35
  124.6 13.7 %collective-permute-start.22 = (bf16[512,384]{1,0:T(8,128)(2,1)S(1)}, bf16[512,384]{1,0:T(8,128)(2,1)S(1)}, u32[]{:S(2)}, u32[]{:S(2)}) collective-permute-start(bf16[512,384]{1,0:T(8,128)(2,1)S(1)} %shard_map.66), channel_id=1, source_target_pairs={{0,6},{2,0},{4,2},{6,4},{1,7},{3,1},{5,3},{7,5},{8,14},{10,8},{12,... | collective-permute-start | bytes 1179656 | tf_op jit(solution)/shard_map/ppermute | solution.py:35
  130.0 22.8 %collective-permute-start.21 = (bf16[512,384]{1,0:T(8,128)(2,1)S(1)}, bf16[512,384]{1,0:T(8,128)(2,1)S(1)}, u32[]{:S(2)}, u32[]{:S(2)}) collective-permute-start(bf16[512,384]{1,0:T(8,128)(2,1)S(1)} %shard_map.65), channel_id=1, source_target_pairs={{0,2},{2,4},{4,6},{6,0},{1,3},{3,5},{5,7},{7,1},{8,10},{10,12},{12... | collective-permute-start | bytes 1179656 | tf_op jit(solution)/shard_map/ppermute | solution.py:35
  132.6 20.1 %collective-permute-start.20 = (bf16[512,384]{1,0:T(8,128)(2,1)S(1)}, bf16[512,384]{1,0:T(8,128)(2,1)S(1)}, u32[]{:S(2)}, u32[]{:S(2)}) collective-permute-start(bf16[512,384]{1,0:T(8,128)(2,1)S(1)} %shard_map.64), channel_id=1, source_target_pairs={{0,4},{2,6},{4,0},{6,2},{1,5},{3,7},{5,1},{7,3},{8,12},{10,14},{12... | collective-permute-start | bytes 1179656 | tf_op jit(solution)/shard_map/ppermute | solution.py:35
  (5 other events, 111.1 us)

commit v7 on v4

--- a/solution.py
+++ b/solution.py
@@ -53,7 +53,17 @@
         out_ref[y, :, HD:] = v_ref[y * SL : (y + 1) * SL, :]
 
 
-def own_kernel(code_ref, q_ref, k_ref, v_ref, qx_ref, o_ref, lse_ref):
+def query_kernel(code_ref, q_ref, qx_ref):
+    for h in range(HEADS):
+        qx_ref[h * HD : (h + 1) * HD, :] = q_ref[:, h * HD : (h + 1) * HD].T
+    lane = lax.broadcasted_iota(jnp.int32, (16, TOK), 1)
+    codes = jnp.zeros((16, TOK), jnp.float32)
+    for i in range(HEADS * TOP):
+        codes = jnp.where(lane == i, code_ref[i].astype(jnp.float32), codes)
+    qx_ref[HALF:, :] = codes.astype(jnp.bfloat16)
+
+
+def own_kernel(q_ref, k_ref, v_ref, o_ref, lse_ref):
     keep = lax.broadcasted_iota(jnp.int32, (TOK, TOK), 0) <= lax.broadcasted_iota(
         jnp.int32, (TOK, TOK), 1
     )
@@ -61,8 +71,7 @@
     v = v_ref[...]
     rows = []
     for h in range(HEADS):
-        q = q_ref[:, h * HD : (h + 1) * HD].T
-        qx_ref[h * HD : (h + 1) * HD, :] = q
+        q = q_ref[h * HD : (h + 1) * HD, :]
         s = jnp.dot(k, q, preferred_element_type=jnp.float32)
         s = jnp.where(keep, s * COEF, DEAD)
         top = jnp.max(s, axis=0, keepdims=True)
@@ -72,11 +81,6 @@
         o_ref[h * HD : (h + 1) * HD, :] = o.astype(jnp.bfloat16)
         rows.append(top + jnp.log2(total))
     lse_ref[...] = jnp.concatenate(rows + rows, axis=0)
-    lane = lax.broadcasted_iota(jnp.int32, (16, TOK), 1)
-    codes = jnp.zeros((16, TOK), jnp.float32)
-    for i in range(HEADS * TOP):
-        codes = jnp.where(lane == i, code_ref[i].astype(jnp.float32), codes)
-    qx_ref[HALF:, :] = codes.astype(jnp.bfloat16)
 
 
 def slices_of(code_ref, kv_ref, q_ref, o_ref, base):
@@ -103,8 +107,10 @@
     o_ref[HALF:, :] = jnp.concatenate(rows, axis=0).astype(jnp.bfloat16)
 
 
-def slices_kernel(code_ref, kv_ref, q_ref, o_ref, *, base):
-    slices_of(code_ref, kv_ref, q_ref, o_ref, base)
+def slices_kernel(code_ref, kv_ref, *rest):
+    n = len(rest) // 2
+    for i in range(n):
+        slices_of(code_ref, kv_ref, rest[i], rest[n + i], i * HEADS * TOP)
 
 
 def merge_kernel(own_ref, lse_ref, p0, p1, p2, p3, out_ref):
@@ -204,13 +210,16 @@
             m = lax.ppermute(m, "z", astern(k))
             kept.append(m)
     w_got = send(out_weight, "core", 1)
-    qx, own, own_lse = pallas(
+    qx = pallas(
+        8, query_kernel, in_specs=[smem, vmem], out_specs=vmem, out_shape=bf16(EXT, TOK)
+    )(code, queries)
+    own, own_lse = pallas(
         8,
         own_kernel,
-        in_specs=[smem] + [vmem] * 3,
-        out_specs=[vmem] * 3,
-        out_shape=[bf16(EXT, TOK), bf16(HALF, TOK), f32(2 * HEADS, TOK)],
-    )(code, queries, keys, values)
+        in_specs=[vmem] * 3,
+        out_specs=[vmem] * 2,
+        out_shape=[bf16(HALF, TOK), f32(2 * HEADS, TOK)],
+    )(qx, keys, values)
     order = (2, 1, 3)
     qs = [send(qx, "y", s) for s in order]
     codes = jnp.stack([a[HALF, : HEADS * TOP] for a in qs], axis=0).astype(jnp.int32).reshape(-1)
@@ -230,20 +239,18 @@
     )(cols, out_weight, w_got)
     kv = jnp.concatenate(kept, axis=0)
 
-    def attend(code, q, base):
+    def attend(code, *qs):
         return pallas(
             12,
-            functools.partial(slices_kernel, base=base),
-            in_specs=[smem] + [vmem] * 2,
-            out_specs=vmem,
-            out_shape=bf16(EXT, TOK),
-        )(code, kv, q)
-
-    back = []
-    for i, s in enumerate(order):
-        part = attend(codes, qs[i], i * HEADS * TOP)
-        back.append(send(part, "y", -s))
-    home = attend(code, qx, 0)
+            slices_kernel,
+            in_specs=[smem] + [vmem] * (1 + len(qs)),
+            out_specs=[vmem] * len(qs),
+            out_shape=[bf16(EXT, TOK)] * len(qs),
+        )(code, kv, *qs)
+
+    parts = attend(codes, *qs)
+    back = [send(part, "y", -s) for s, part in zip(order, parts)]
+    (home,) = attend(code, qx)
     att = pallas(
         8, merge_kernel, in_specs=[vmem] * 6, out_specs=vmem, out_shape=bf16(HALF, TOK)
     )(own, own_lse, home, *back)

time: 170 us -> 164 us (0.965)
  local copies, waits for them, and re-layouts: 15.1 us -> 12.5 us
    unnamed x48 -> x38, local copies, waits for them, and re-layouts: 14.2 us -> 11.2 us
    pallas_call x5 -> x4, Pallas kernels: 9.79 us -> 8.64 us  [the longest x2 6.58 us: attend(): pallas(12, slices_kernel, in_specs=[smem] + [vmem] * (1 + len(qs)), out_s...]
  transfers between devices with their start and end apart: 27 -> 27, of which waited for: 10 -> 11; matrix products, arithmetic and copies ran while one was open for 4% -> 5% of each run, Pallas kernels for 10% -> 10%
where the time goes in v7:
time: 164 us; the launch traced here: 163 us
  starting transfers between devices  90.9 us (55%)
  waiting for transfers between devices  40 us (24%)
  Pallas kernels  18 us (11%)
  local copies, waits for them, and re-layouts  12.5 us (8%)
    ppermute x11, starting transfers between devices, send(): return lax.ppermute(a, axis, [(i, (i + s) % n) for i in range(n)])  44.5 us
    ppermute x7, starting transfers between devices, steps(): m = lax.ppermute(m, 'z', astern(k))  34.8 us
    ppermute x11, waiting for transfers between devices, send(): return lax.ppermute(a, axis, [(i, (i + s) % n) for i in range(n)])  23.3 us
    ppermute x7, waiting for transfers between devices, steps(): m = lax.ppermute(m, 'z', astern(k))  11.5 us
    unnamed x38, local copies, waits for them, and re-layouts  11.2 us
    ppermute x8, starting transfers between devices, steps(): p = lax.ppermute(p, 'z', ahead(k))  7.61 us
    pallas_call x2, Pallas kernels, attend(): pallas(12, slices_kernel, in_specs=[smem] + [vmem] * (1 + len(qs)), out_s...  6.58 us
    all_to_all x1, waiting for transfers between devices, steps(): row = lax.all_to_all(packed, 'y', 0, 0)  5.25 us
  transfers between devices with their start and end apart: 27, of which 11 were waited for; matrix products, arithmetic and copies ran while one was open for 5% of the time, Pallas kernels for 10%

profile of v7, /device:TPU:1, one launch (start us, length us, event | category | flops | bytes accessed | tf_op | source)
XLA Modules:
  0.0 162.7 jit_solution(16488571733174190368)
XLA Ops:
  0.0 8.7 %collective-permute-start = (bf16[512,4096]{1,0:T(8,128)(2,1)}, bf16[512,4096]{1,0:T(8,128)(2,1)}, u32[]{:S(2)}, u32[]{:S(2)}) collective-permute-start(bf16[512,4096]{1,0:T(8,128)(2,1)} %mine_ref.1), channel_id=1, source_target_pairs={{0,1},{1,0},{2,3},{3,2},{4,5},{5,4},{6,7},{7,6},{8,9},{9,8},{10,11... | collective-permute-start | bytes 12582920 | tf_op jit(solution)/shard_map/ppermute | solution.py:35
  10.4 4.0 %all-to-all-start = ((bf16[4,96,256]{2,1,0:T(8,128)(2,1)}), bf16[4,96,256]{2,1,0:T(8,128)(2,1)}, u32[]{:S(2)}, u32[]{:S(2)}) async-start(bf16[4,96,256]{2,1,0:T(8,128)(2,1)} %shard_map.58), calls=%async_computation | async-start | bytes 393216 | tf_op jit(solution)/shard_map/all_to_all | solution.py:197
  15.3 5.2 %all-to-all-done = bf16[4,96,256]{2,1,0:T(8,128)(2,1)} async-done(((bf16[4,96,256]{2,1,0:T(8,128)(2,1)}), bf16[4,96,256]{2,1,0:T(8,128)(2,1)}, u32[]{:S(2)}, u32[]{:S(2)}) %all-to-all-start) | async-done | bytes 196640 | tf_op jit(solution)/shard_map/all_to_all | solution.py:197
  26.4 3.1 %collective-permute-start.17 = (bf16[528,384]{1,0:T(8,128)(2,1)S(1)}, bf16[528,384]{1,0:T(8,128)(2,1)S(1)}, u32[]{:S(2)}, u32[]{:S(2)}) collective-permute-start(bf16[528,384]{1,0:T(8,128)(2,1)S(1)} %shard_map.56.q_ref.rest_0_), channel_id=1, source_target_pairs={{0,8},{8,16},{16,24},{24,0},{1,9},{9,17},{17,25},{25,1},{2,10},{10... | collective-permute-start | bytes 1216520 | tf_op jit(solution)/shard_map/ppermute | solution.py:35
  29.5 3.4 %collective-permute-start.18 = (bf16[528,384]{1,0:T(8,128)(2,1)S(1)}, bf16[528,384]{1,0:T(8,128)(2,1)S(1)}, u32[]{:S(2)}, u32[]{:S(2)}) collective-permute-start(bf16[528,384]{1,0:T(8,128)(2,1)S(1)} %shard_map.56.q_ref.rest_0_), channel_id=1, source_target_pairs={{0,24},{8,0},{16,8},{24,16},{1,25},{9,1},{17,9},{25,17},{2,26},{10... | collective-permute-start | bytes 1216520 | tf_op jit(solution)/shard_map/ppermute | solution.py:35
  32.9 5.0 %collective-permute-start.2 = (bf16[4,96,256]{2,1,0:T(8,128)(2,1)}, bf16[4,96,256]{2,1,0:T(8,128)(2,1)}, u32[]{:S(2)}, u32[]{:S(2)}) collective-permute-start(bf16[4,96,256]{2,1,0:T(8,128)(2,1)} %all-to-all-done), channel_id=1, source_target_pairs={{0,480},{32,0},{64,32},{96,64},{128,96},{160,128},{192,160},{1,481... | collective-permute-start | bytes 589832 | tf_op jit(solution)/shard_map/ppermute | solution.py:210
  42.2 5.2 %collective-permute-start.4 = (bf16[4,96,256]{2,1,0:T(8,128)(2,1)}, bf16[4,96,256]{2,1,0:T(8,128)(2,1)}, u32[]{:S(2)}, u32[]{:S(2)}) collective-permute-start(bf16[4,96,256]{2,1,0:T(8,128)(2,1)} %collective-permute-done.2), channel_id=1, source_target_pairs={{480,448},{0,480},{32,0},{64,32},{96,64},{128,96},{160,128},{481,4... | collective-permute-start | bytes 589832 | tf_op jit(solution)/shard_map/ppermute | solution.py:210
  53.4 4.6 %collective-permute-start.6 = (bf16[4,96,256]{2,1,0:T(8,128)(2,1)}, bf16[4,96,256]{2,1,0:T(8,128)(2,1)S(1)}, u32[]{:S(2)}, u32[]{:S(2)}) collective-permute-start(bf16[4,96,256]{2,1,0:T(8,128)(2,1)} %collective-permute-done.4), channel_id=1, source_target_pairs={{448,416},{480,448},{0,480},{32,0},{64,32},{96,64},{128,96},{449,4... | collective-permute-start | bytes 589832 | tf_op jit(solution)/shard_map/ppermute | solution.py:210
  60.9 4.9 %collective-permute-start.8 = (bf16[4,96,256]{2,1,0:T(8,128)(2,1)S(1)}, bf16[4,96,256]{2,1,0:T(8,128)(2,1)S(1)}, u32[]{:S(2)}, u32[]{:S(2)}) collective-permute-start(bf16[4,96,256]{2,1,0:T(8,128)(2,1)S(1)} %collective-permute-done.6), channel_id=1, source_target_pairs={{416,384},{448,416},{480,448},{0,480},{32,0},{64,32},{96,64},{417,... | collective-permute-start | bytes 589832 | tf_op jit(solution)/shard_map/ppermute | solution.py:210
  68.4 5.0 %collective-permute-start.10 = (bf16[4,96,256]{2,1,0:T(8,128)(2,1)S(1)}, bf16[4,96,256]{2,1,0:T(8,128)(2,1)S(1)}, u32[]{:S(2)}, u32[]{:S(2)}) collective-permute-start(bf16[4,96,256]{2,1,0:T(8,128)(2,1)S(1)} %collective-permute-done.8), channel_id=1, source_target_pairs={{384,352},{416,384},{448,416},{480,448},{0,480},{32,0},{64,32},{38... | collective-permute-start | bytes 589832 | tf_op jit(solution)/shard_map/ppermute | solution.py:210
  76.1 5.0 %collective-permute-start.12 = (bf16[4,96,256]{2,1,0:T(8,128)(2,1)S(1)}, bf16[4,96,256]{2,1,0:T(8,128)(2,1)S(1)}, u32[]{:S(2)}, u32[]{:S(2)}) collective-permute-start(bf16[4,96,256]{2,1,0:T(8,128)(2,1)S(1)} %collective-permute-done.10), channel_id=1, source_target_pairs={{352,320},{384,352},{416,384},{448,416},{480,448},{0,480},{32,0},{... | collective-permute-start | bytes 589832 | tf_op jit(solution)/shard_map/ppermute | solution.py:210
  82.0 2.5 %collective-permute-done.12 = bf16[4,96,256]{2,1,0:T(8,128)(2,1)S(1)} collective-permute-done((bf16[4,96,256]{2,1,0:T(8,128)(2,1)S(1)}, bf16[4,96,256]{2,1,0:T(8,128)(2,1)S(1)}, u32[]{:S(2)}, u32[]{:S(2)}) %collective-permute-start.12) | collective-permute-done | bytes 196640 | tf_op jit(solution)/shard_map/ppermute | solution.py:210
  84.5 5.0 %collective-permute-start.14 = (bf16[4,96,256]{2,1,0:T(8,128)(2,1)S(1)}, bf16[4,96,256]{2,1,0:T(8,128)(2,1)S(1)}, u32[]{:S(2)}, u32[]{:S(2)}) collective-permute-start(bf16[4,96,256]{2,1,0:T(8,128)(2,1)S(1)} %collective-permute-done.12), channel_id=1, source_target_pairs={{320,288},{352,320},{384,352},{416,384},{448,416},{480,448},{0,480... | collective-permute-start | bytes 589832 | tf_op jit(solution)/shard_map/ppermute | solution.py:210
  90.3 3.9 %collective-permute-done.14 = bf16[4,96,256]{2,1,0:T(8,128)(2,1)S(1)} collective-permute-done((bf16[4,96,256]{2,1,0:T(8,128)(2,1)S(1)}, bf16[4,96,256]{2,1,0:T(8,128)(2,1)S(1)}, u32[]{:S(2)}, u32[]{:S(2)}) %collective-permute-start.14) | collective-permute-done | bytes 196640 | tf_op jit(solution)/shard_map/ppermute | solution.py:210
  94.3 4.6 %shard_map.60 = (bf16[528,384]{1,0:T(8,128)(2,1)S(1)}, bf16[528,384]{1,0:T(8,128)(2,1)S(1)}, bf16[528,384]{1,0:T(8,128)(2,1)S(1)}) custom-call(s32[36]{0:T(128)S(1)} %copy-done.10, bf16[64,96,256]{2,1,0:T(8,128)(2,1)S(1)} %constant_dynamic-update-slice_fusion.kv_ref, bf16[528,384]{1,0:T(8,128)(2,1)S(1)} %copy-done.2, bf16[528,384]{1,0:T(8,128)(2,1)S(1)} %copy-done.4, ...), custom_call_target="tpu_custom_call" | custom-call | tf_op jit(solution)/shard_map/pallas_call | solution.py:243
  98.9 3.2 %collective-permute-start.19 = (bf16[528,384]{1,0:T(8,128)(2,1)S(1)}, bf16[528,384]{1,0:T(8,128)(2,1)S(1)}, u32[]{:S(2)}, u32[]{:S(2)}) collective-permute-start(bf16[528,384]{1,0:T(8,128)(2,1)S(1)} %get-tuple-element.12), channel_id=1, source_target_pairs={{0,16},{8,24},{16,0},{24,8},{1,17},{9,25},{17,1},{25,9},{2,18},{10... | collective-permute-start | bytes 1216520 | tf_op jit(solution)/shard_map/ppermute | solution.py:35
  102.1 2.8 %collective-permute-start.20 = (bf16[528,384]{1,0:T(8,128)(2,1)S(1)}, bf16[528,384]{1,0:T(8,128)(2,1)S(1)}, u32[]{:S(2)}, u32[]{:S(2)}) collective-permute-start(bf16[528,384]{1,0:T(8,128)(2,1)S(1)} %get-tuple-element.13), channel_id=1, source_target_pairs={{0,24},{8,0},{16,8},{24,16},{1,25},{9,1},{17,9},{25,17},{2,26},{10... | collective-permute-start | bytes 1216520 | tf_op jit(solution)/shard_map/ppermute | solution.py:35
  104.9 2.5 %collective-permute-start.21 = (bf16[528,384]{1,0:T(8,128)(2,1)S(1)}, bf16[528,384]{1,0:T(8,128)(2,1)S(1)}, u32[]{:S(2)}, u32[]{:S(2)}) collective-permute-start(bf16[528,384]{1,0:T(8,128)(2,1)S(1)} %get-tuple-element.14), channel_id=1, source_target_pairs={{0,8},{8,16},{16,24},{24,0},{1,9},{9,17},{17,25},{25,1},{2,10},{10... | collective-permute-start | bytes 1216520 | tf_op jit(solution)/shard_map/ppermute | solution.py:35
  112.1 7.0 %collective-permute-done.21.p3 = bf16[528,384]{1,0:T(8,128)(2,1)S(1)} collective-permute-done((bf16[528,384]{1,0:T(8,128)(2,1)S(1)}, bf16[528,384]{1,0:T(8,128)(2,1)S(1)}, u32[]{:S(2)}, u32[]{:S(2)}) %collective-permute-start.21) | collective-permute-done | bytes 405536 | tf_op jit(solution)/shard_map/ppermute | solution.py:35
  119.6 8.7 %collective-permute-start.22 = (bf16[512,384]{1,0:T(8,128)(2,1)S(1)}, bf16[512,384]{1,0:T(8,128)(2,1)S(1)}, u32[]{:S(2)}, u32[]{:S(2)}) collective-permute-start(bf16[512,384]{1,0:T(8,128)(2,1)S(1)} %shard_map.61.mine_ref), channel_id=1, source_target_pairs={{0,1},{1,0},{2,3},{3,2},{4,5},{5,4},{6,7},{7,6},{8,9},{9,8},{10,11... | collective-permute-start | bytes 1179656 | tf_op jit(solution)/shard_map/ppermute | solution.py:35
  130.5 3.5 %shard_map.55.w_ref = bf16[4,512,1024]{2,1,0:T(8,128)(2,1)S(1)} custom-call(s32[4]{0:T(128)S(1)} %fusion.2.cols_ref, bf16[512,4096]{1,0:T(8,128)(2,1)S(1)} %copy-done, bf16[512,4096]{1,0:T(8,128)(2,1)} %collective-permute-done.got_ref), custom_call_target="tpu_custom_call" | custom-call | tf_op jit(solution)/shard_map/pallas_call | solution.py:227
  134.8 4.4 %collective-permute-start.25 = (bf16[512,384]{1,0:T(8,128)(2,1)S(1)}, bf16[512,384]{1,0:T(8,128)(2,1)S(1)}, u32[]{:S(2)}, u32[]{:S(2)}) collective-permute-start(bf16[512,384]{1,0:T(8,128)(2,1)S(1)} %shard_map.65), channel_id=1, source_target_pairs={{0,6},{2,0},{4,2},{6,4},{1,7},{3,1},{5,3},{7,5},{8,14},{10,8},{12,... | collective-permute-start | bytes 1179656 | tf_op jit(solution)/shard_map/ppermute | solution.py:35
  142.5 3.6 %collective-permute-start.23 = (bf16[512,384]{1,0:T(8,128)(2,1)S(1)}, bf16[512,384]{1,0:T(8,128)(2,1)S(1)}, u32[]{:S(2)}, u32[]{:S(2)}) collective-permute-start(bf16[512,384]{1,0:T(8,128)(2,1)S(1)} %shard_map.63), channel_id=1, source_target_pairs={{0,4},{2,6},{4,0},{6,2},{1,5},{3,7},{5,1},{7,3},{8,12},{10,14},{12... | collective-permute-start | bytes 1179656 | tf_op jit(solution)/shard_map/ppermute | solution.py:35
  147.6 14.2 %collective-permute-done.24.g2 = bf16[512,384]{1,0:T(8,128)(2,1)S(1)} collective-permute-done((bf16[512,384]{1,0:T(8,128)(2,1)S(1)}, bf16[512,384]{1,0:T(8,128)(2,1)S(1)}, u32[]{:S(2)}, u32[]{:S(2)}) %collective-permute-start.24) | collective-permute-done | bytes 393248 | tf_op jit(solution)/shard_map/ppermute | solution.py:35
  (89 shorter events, 42.0 us)
Async XLA Ops:
  0.0 128.3 %collective-permute-start = (bf16[512,4096]{1,0:T(8,128)(2,1)}, bf16[512,4096]{1,0:T(8,128)(2,1)}, u32[]{:S(2)}, u32[]{:S(2)}) collective-permute-start(bf16[512,4096]{1,0:T(8,128)(2,1)} %mine_ref.1), channel_id=1, source_target_pairs={{0,1},{1,0},{2,3},{3,2},{4,5},{5,4},{6,7},{7,6},{8,9},{9,8},{10,11... | collective-permute-start | bytes 12582920 | tf_op jit(solution)/shard_map/ppermute | solution.py:35
  10.4 10.1 %all-to-all-start = ((bf16[4,96,256]{2,1,0:T(8,128)(2,1)}), bf16[4,96,256]{2,1,0:T(8,128)(2,1)}, u32[]{:S(2)}, u32[]{:S(2)}) async-start(bf16[4,96,256]{2,1,0:T(8,128)(2,1)} %shard_map.58), calls=%async_computation | async-start | bytes 393216 | tf_op jit(solution)/shard_map/all_to_all | solution.py:197
  20.5 12.4 %collective-permute-start.1 = (bf16[4,96,256]{2,1,0:T(8,128)(2,1)}, bf16[4,96,256]{2,1,0:T(8,128)(2,1)}, u32[]{:S(2)}, u32[]{:S(2)}) collective-permute-start(bf16[4,96,256]{2,1,0:T(8,128)(2,1)} %all-to-all-done), channel_id=1, source_target_pairs={{0,32},{32,64},{64,96},{96,128},{128,160},{160,192},{192,224},{224... | collective-permute-start | bytes 589832 | tf_op jit(solution)/shard_map/ppermute | solution.py:207
  24.2 18.0 %collective-permute-start.16 = (bf16[528,384]{1,0:T(8,128)(2,1)S(1)}, bf16[528,384]{1,0:T(8,128)(2,1)S(1)}, u32[]{:S(2)}, u32[]{:S(2)}) collective-permute-start(bf16[528,384]{1,0:T(8,128)(2,1)S(1)} %shard_map.56.q_ref.rest_0_), channel_id=1, source_target_pairs={{0,16},{8,24},{16,0},{24,8},{1,17},{9,25},{17,1},{25,9},{2,18},{10... | collective-permute-start | bytes 1216520 | tf_op jit(solution)/shard_map/ppermute | solution.py:35
  26.4 22.7 %collective-permute-start.17 = (bf16[528,384]{1,0:T(8,128)(2,1)S(1)}, bf16[528,384]{1,0:T(8,128)(2,1)S(1)}, u32[]{:S(2)}, u32[]{:S(2)}) collective-permute-start(bf16[528,384]{1,0:T(8,128)(2,1)S(1)} %shard_map.56.q_ref.rest_0_), channel_id=1, source_target_pairs={{0,8},{8,16},{16,24},{24,0},{1,9},{9,17},{17,25},{25,1},{2,10},{10... | collective-permute-start | bytes 1216520 | tf_op jit(solution)/shard_map/ppermute | solution.py:35
  29.5 20.4 %collective-permute-start.18 = (bf16[528,384]{1,0:T(8,128)(2,1)S(1)}, bf16[528,384]{1,0:T(8,128)(2,1)S(1)}, u32[]{:S(2)}, u32[]{:S(2)}) collective-permute-start(bf16[528,384]{1,0:T(8,128)(2,1)S(1)} %shard_map.56.q_ref.rest_0_), channel_id=1, source_target_pairs={{0,24},{8,0},{16,8},{24,16},{1,25},{9,1},{17,9},{25,17},{2,26},{10... | collective-permute-start | bytes 1216520 | tf_op jit(solution)/shard_map/ppermute | solution.py:35
  32.9 7.9 %collective-permute-start.2 = (bf16[4,96,256]{2,1,0:T(8,128)(2,1)}, bf16[4,96,256]{2,1,0:T(8,128)(2,1)}, u32[]{:S(2)}, u32[]{:S(2)}) collective-permute-start(bf16[4,96,256]{2,1,0:T(8,128)(2,1)} %all-to-all-done), channel_id=1, source_target_pairs={{0,480},{32,0},{64,32},{96,64},{128,96},{160,128},{192,160},{1,481... | collective-permute-start | bytes 589832 | tf_op jit(solution)/shard_map/ppermute | solution.py:210
  40.9 11.7 %collective-permute-start.3 = (bf16[4,96,256]{2,1,0:T(8,128)(2,1)}, bf16[4,96,256]{2,1,0:T(8,128)(2,1)}, u32[]{:S(2)}, u32[]{:S(2)}) collective-permute-start(bf16[4,96,256]{2,1,0:T(8,128)(2,1)} %collective-permute-done.1), channel_id=1, source_target_pairs={{32,64},{64,96},{96,128},{128,160},{160,192},{192,224},{224,256},{... | collective-permute-start | bytes 589832 | tf_op jit(solution)/shard_map/ppermute | solution.py:207
  42.2 11.2 %collective-permute-start.4 = (bf16[4,96,256]{2,1,0:T(8,128)(2,1)}, bf16[4,96,256]{2,1,0:T(8,128)(2,1)}, u32[]{:S(2)}, u32[]{:S(2)}) collective-permute-start(bf16[4,96,256]{2,1,0:T(8,128)(2,1)} %collective-permute-done.2), channel_id=1, source_target_pairs={{480,448},{0,480},{32,0},{64,32},{96,64},{128,96},{160,128},{481,4... | collective-permute-start | bytes 589832 | tf_op jit(solution)/shard_map/ppermute | solution.py:210
  53.4 7.5 %collective-permute-start.6 = (bf16[4,96,256]{2,1,0:T(8,128)(2,1)}, bf16[4,96,256]{2,1,0:T(8,128)(2,1)S(1)}, u32[]{:S(2)}, u32[]{:S(2)}) collective-permute-start(bf16[4,96,256]{2,1,0:T(8,128)(2,1)} %collective-permute-done.4), channel_id=1, source_target_pairs={{448,416},{480,448},{0,480},{32,0},{64,32},{96,64},{128,96},{449,4... | collective-permute-start | bytes 589832 | tf_op jit(solution)/shard_map/ppermute | solution.py:210
  60.9 7.5 %collective-permute-start.8 = (bf16[4,96,256]{2,1,0:T(8,128)(2,1)S(1)}, bf16[4,96,256]{2,1,0:T(8,128)(2,1)S(1)}, u32[]{:S(2)}, u32[]{:S(2)}) collective-permute-start(bf16[4,96,256]{2,1,0:T(8,128)(2,1)S(1)} %collective-permute-done.6), channel_id=1, source_target_pairs={{416,384},{448,416},{480,448},{0,480},{32,0},{64,32},{96,64},{417,... | collective-permute-start | bytes 589832 | tf_op jit(solution)/shard_map/ppermute | solution.py:210
  65.9 7.6 %collective-permute-start.9 = (bf16[4,96,256]{2,1,0:T(8,128)(2,1)S(1)}, bf16[4,96,256]{2,1,0:T(8,128)(2,1)S(1)}, u32[]{:S(2)}, u32[]{:S(2)}) collective-permute-start(bf16[4,96,256]{2,1,0:T(8,128)(2,1)S(1)} %collective-permute-done.7), channel_id=1, source_target_pairs={{128,160},{160,192},{192,224},{224,256},{256,288},{288,320},{320,3... | collective-permute-start | bytes 589832 | tf_op jit(solution)/shard_map/ppermute | solution.py:207
  68.4 7.6 %collective-permute-start.10 = (bf16[4,96,256]{2,1,0:T(8,128)(2,1)S(1)}, bf16[4,96,256]{2,1,0:T(8,128)(2,1)S(1)}, u32[]{:S(2)}, u32[]{:S(2)}) collective-permute-start(bf16[4,96,256]{2,1,0:T(8,128)(2,1)S(1)} %collective-permute-done.8), channel_id=1, source_target_pairs={{384,352},{416,384},{448,416},{480,448},{0,480},{32,0},{64,32},{38... | collective-permute-start | bytes 589832 | tf_op jit(solution)/shard_map/ppermute | solution.py:210
  73.5 7.6 %collective-permute-start.11 = (bf16[4,96,256]{2,1,0:T(8,128)(2,1)S(1)}, bf16[4,96,256]{2,1,0:T(8,128)(2,1)S(1)}, u32[]{:S(2)}, u32[]{:S(2)}) collective-permute-start(bf16[4,96,256]{2,1,0:T(8,128)(2,1)S(1)} %collective-permute-done.9), channel_id=1, source_target_pairs={{160,192},{192,224},{224,256},{256,288},{288,320},{320,352},{352,3... | collective-permute-start | bytes 589832 | tf_op jit(solution)/shard_map/ppermute | solution.py:207
  76.1 8.5 %collective-permute-start.12 = (bf16[4,96,256]{2,1,0:T(8,128)(2,1)S(1)}, bf16[4,96,256]{2,1,0:T(8,128)(2,1)S(1)}, u32[]{:S(2)}, u32[]{:S(2)}) collective-permute-start(bf16[4,96,256]{2,1,0:T(8,128)(2,1)S(1)} %collective-permute-done.10), channel_id=1, source_target_pairs={{352,320},{384,352},{416,384},{448,416},{480,448},{0,480},{32,0},{... | collective-permute-start | bytes 589832 | tf_op jit(solution)/shard_map/ppermute | solution.py:210
  81.2 8.4 %collective-permute-start.13 = (bf16[4,96,256]{2,1,0:T(8,128)(2,1)S(1)}, bf16[4,96,256]{2,1,0:T(8,128)(2,1)S(1)}, u32[]{:S(2)}, u32[]{:S(2)}) collective-permute-start(bf16[4,96,256]{2,1,0:T(8,128)(2,1)S(1)} %collective-permute-done.11), channel_id=1, source_target_pairs={{192,224},{224,256},{256,288},{288,320},{320,352},{352,384},{384,4... | collective-permute-start | bytes 589832 | tf_op jit(solution)/shard_map/ppermute | solution.py:207
  84.5 9.7 %collective-permute-start.14 = (bf16[4,96,256]{2,1,0:T(8,128)(2,1)S(1)}, bf16[4,96,256]{2,1,0:T(8,128)(2,1)S(1)}, u32[]{:S(2)}, u32[]{:S(2)}) collective-permute-start(bf16[4,96,256]{2,1,0:T(8,128)(2,1)S(1)} %collective-permute-done.12), channel_id=1, source_target_pairs={{320,288},{352,320},{384,352},{416,384},{448,416},{480,448},{0,480... | collective-permute-start | bytes 589832 | tf_op jit(solution)/shard_map/ppermute | solution.py:210
  98.9 11.8 %collective-permute-start.19 = (bf16[528,384]{1,0:T(8,128)(2,1)S(1)}, bf16[528,384]{1,0:T(8,128)(2,1)S(1)}, u32[]{:S(2)}, u32[]{:S(2)}) collective-permute-start(bf16[528,384]{1,0:T(8,128)(2,1)S(1)} %get-tuple-element.12), channel_id=1, source_target_pairs={{0,16},{8,24},{16,0},{24,8},{1,17},{9,25},{17,1},{25,9},{2,18},{10... | collective-permute-start | bytes 1216520 | tf_op jit(solution)/shard_map/ppermute | solution.py:35
  102.1 10.0 %collective-permute-start.20 = (bf16[528,384]{1,0:T(8,128)(2,1)S(1)}, bf16[528,384]{1,0:T(8,128)(2,1)S(1)}, u32[]{:S(2)}, u32[]{:S(2)}) collective-permute-start(bf16[528,384]{1,0:T(8,128)(2,1)S(1)} %get-tuple-element.13), channel_id=1, source_target_pairs={{0,24},{8,0},{16,8},{24,16},{1,25},{9,1},{17,9},{25,17},{2,26},{10... | collective-permute-start | bytes 1216520 | tf_op jit(solution)/shard_map/ppermute | solution.py:35
  104.9 14.2 %collective-permute-start.21 = (bf16[528,384]{1,0:T(8,128)(2,1)S(1)}, bf16[528,384]{1,0:T(8,128)(2,1)S(1)}, u32[]{:S(2)}, u32[]{:S(2)}) collective-permute-start(bf16[528,384]{1,0:T(8,128)(2,1)S(1)} %get-tuple-element.14), channel_id=1, source_target_pairs={{0,8},{8,16},{16,24},{24,0},{1,9},{9,17},{17,25},{25,1},{2,10},{10... | collective-permute-start | bytes 1216520 | tf_op jit(solution)/shard_map/ppermute | solution.py:35
  119.6 14.4 %collective-permute-start.22 = (bf16[512,384]{1,0:T(8,128)(2,1)S(1)}, bf16[512,384]{1,0:T(8,128)(2,1)S(1)}, u32[]{:S(2)}, u32[]{:S(2)}) collective-permute-start(bf16[512,384]{1,0:T(8,128)(2,1)S(1)} %shard_map.61.mine_ref), channel_id=1, source_target_pairs={{0,1},{1,0},{2,3},{3,2},{4,5},{5,4},{6,7},{7,6},{8,9},{9,8},{10,11... | collective-permute-start | bytes 1179656 | tf_op jit(solution)/shard_map/ppermute | solution.py:35
  134.8 12.8 %collective-permute-start.25 = (bf16[512,384]{1,0:T(8,128)(2,1)S(1)}, bf16[512,384]{1,0:T(8,128)(2,1)S(1)}, u32[]{:S(2)}, u32[]{:S(2)}) collective-permute-start(bf16[512,384]{1,0:T(8,128)(2,1)S(1)} %shard_map.65), channel_id=1, source_target_pairs={{0,6},{2,0},{4,2},{6,4},{1,7},{3,1},{5,3},{7,5},{8,14},{10,8},{12,... | collective-permute-start | bytes 1179656 | tf_op jit(solution)/shard_map/ppermute | solution.py:35
  139.9 21.9 %collective-permute-start.24 = (bf16[512,384]{1,0:T(8,128)(2,1)S(1)}, bf16[512,384]{1,0:T(8,128)(2,1)S(1)}, u32[]{:S(2)}, u32[]{:S(2)}) collective-permute-start(bf16[512,384]{1,0:T(8,128)(2,1)S(1)} %shard_map.64), channel_id=1, source_target_pairs={{0,2},{2,4},{4,6},{6,0},{1,3},{3,5},{5,7},{7,1},{8,10},{10,12},{12... | collective-permute-start | bytes 1179656 | tf_op jit(solution)/shard_map/ppermute | solution.py:35
  142.5 19.3 %collective-permute-start.23 = (bf16[512,384]{1,0:T(8,128)(2,1)S(1)}, bf16[512,384]{1,0:T(8,128)(2,1)S(1)}, u32[]{:S(2)}, u32[]{:S(2)}) collective-permute-start(bf16[512,384]{1,0:T(8,128)(2,1)S(1)} %shard_map.63), channel_id=1, source_target_pairs={{0,4},{2,6},{4,0},{6,2},{1,5},{3,7},{5,1},{7,3},{8,12},{10,14},{12... | collective-permute-start | bytes 1179656 | tf_op jit(solution)/shard_map/ppermute | solution.py:35
  (14 other events, 242.6 us)

commit v8 on v7

--- a/solution.py
+++ b/solution.py
@@ -136,37 +136,34 @@
         out_ref[span, :] = (acc * (1.0 / total)).astype(jnp.bfloat16)
 
 
-def turn_kernel(cols_ref, mine_ref, got_ref, out_ref, blocks, turned, sems, out_sems):
+def turn_kernel(cols_ref, src_ref, out_ref, blocks, turned, sems, out_sems):
     loads = []
     for s in range(NX):
         cols = pl.ds(pl.multiple_of(cols_ref[s] * HALF, HALF), HALF)
-        for i, src in enumerate((mine_ref, got_ref)):
-            at = 2 * s + i
-            loads.append(pltpu.make_async_copy(src.at[:, cols], blocks.at[at], sems.at[at]))
+        loads.append(pltpu.make_async_copy(src_ref.at[:, cols], blocks.at[s], sems.at[s]))
     for load in loads:
         load.start()
     stores = []
     for s in range(NX):
-        for i in range(2):
-            loads[2 * s + i].wait()
-            turned[s, :, i * HALF : (i + 1) * HALF] = blocks[2 * s + i].T
+        loads[s].wait()
+        turned[s] = blocks[s].T
         stores.append(pltpu.make_async_copy(turned.at[s], out_ref.at[s], out_sems.at[s]))
         stores[s].start()
     for store in stores:
         store.wait()
 
 
-def piece_of(w_ref, s, mine_ref, got_ref):
-    out = jnp.dot(w_ref[s, :, :HALF], mine_ref[...], preferred_element_type=jnp.float32)
-    return out + jnp.dot(w_ref[s, :, HALF:], got_ref[...], preferred_element_type=jnp.float32)
-
-
-def piece_kernel(w_ref, mine_ref, got_ref, out_ref, *, s):
-    out_ref[...] = piece_of(w_ref, s, mine_ref, got_ref).astype(jnp.bfloat16)
-
-
-def mine_kernel(w_ref, mine_ref, got_ref, out_ref):
-    out_ref[...] = piece_of(w_ref, 0, mine_ref, got_ref)
+def piece_of(w_mine, w_got, s, mine_ref, got_ref):
+    out = jnp.dot(w_mine[s], mine_ref[...], preferred_element_type=jnp.float32)
+    return out + jnp.dot(w_got[s], got_ref[...], preferred_element_type=jnp.float32)
+
+
+def piece_kernel(w_mine, w_got, mine_ref, got_ref, out_ref, *, s):
+    out_ref[...] = piece_of(w_mine, w_got, s, mine_ref, got_ref).astype(jnp.bfloat16)
+
+
+def mine_kernel(w_mine, w_got, mine_ref, got_ref, out_ref):
+    out_ref[...] = piece_of(w_mine, w_got, 0, mine_ref, got_ref)
 
 
 def sum_kernel(mine_ref, g1, g2, g3, out_ref):
@@ -224,19 +221,24 @@
     qs = [send(qx, "y", s) for s in order]
     codes = jnp.stack([a[HALF, : HEADS * TOP] for a in qs], axis=0).astype(jnp.int32).reshape(-1)
     cols = (x + jnp.arange(NX, dtype=jnp.int32)) % NX * 2 + core
-    w = pallas(
-        12,
-        turn_kernel,
-        in_specs=[smem] + [pl.BlockSpec(memory_space=pltpu.HBM)] * 2,
-        out_specs=pl.BlockSpec(memory_space=pltpu.HBM),
-        out_shape=bf16(NX, HALF, 2 * HALF),
-        scratch_shapes=[
-            pltpu.VMEM((2 * NX, HALF, HALF), jnp.bfloat16),
-            pltpu.VMEM((NX, HALF, 2 * HALF), jnp.bfloat16),
-            pltpu.SemaphoreType.DMA((2 * NX,)),
-            pltpu.SemaphoreType.DMA((NX,)),
-        ],
-    )(cols, out_weight, w_got)
+    hbm = pl.BlockSpec(memory_space=pltpu.HBM)
+
+    def turn(src):
+        return pallas(
+            8,
+            turn_kernel,
+            in_specs=[smem, hbm],
+            out_specs=hbm,
+            out_shape=bf16(NX, HALF, HALF),
+            scratch_shapes=[
+                pltpu.VMEM((NX, HALF, HALF), jnp.bfloat16),
+                pltpu.VMEM((NX, HALF, HALF), jnp.bfloat16),
+                pltpu.SemaphoreType.DMA((NX,)),
+                pltpu.SemaphoreType.DMA((NX,)),
+            ],
+        )(cols, src)
+
+    wt = (turn(out_weight), turn(w_got))
     kv = jnp.concatenate(kept, axis=0)
 
     def attend(code, *qs):
@@ -260,14 +262,14 @@
         part = pallas(
             12,
             functools.partial(piece_kernel, s=s),
-            in_specs=[vmem] * 3,
+            in_specs=[vmem] * 4,
             out_specs=vmem,
             out_shape=bf16(HALF, TOK),
-        )(w, att, att_got)
+        )(*wt, att, att_got)
         got.append(send(part, "x", s))
     mine = pallas(
-        12, mine_kernel, in_specs=[vmem] * 3, out_specs=vmem, out_shape=f32(HALF, TOK)
-    )(w, att, att_got)
+        12, mine_kernel, in_specs=[vmem] * 4, out_specs=vmem, out_shape=f32(HALF, TOK)
+    )(*wt, att, att_got)
     return pallas(
         8, sum_kernel, in_specs=[vmem] * 4, out_specs=vmem, out_shape=bf16(HALF, TOK)
     )(mine, *got)

time: 164 us -> 165 us (level)
    pallas_call x5 -> x6, Pallas kernels: 6.32 us -> 7.24 us  [the longest x2 4.42 us: turn(): pallas(8, turn_kernel, in_specs=[smem, hbm], out_specs=hbm, out_shape=bf1...]
  transfers between devices with their start and end apart: 27 -> 27, of which waited for: 11 -> 11; matrix products, arithmetic and copies ran while one was open for 5% -> 5% of each run, Pallas kernels for 10% -> 11%
where the time goes in v8:
time: 165 us; the launch traced here: 164 us
  starting transfers between devices  90.9 us (55%)
  waiting for transfers between devices  40 us (24%)
  Pallas kernels  19 us (12%)
  local copies, waits for them, and re-layouts  12.5 us (8%)
    ppermute x11, starting transfers between devices, send(): return lax.ppermute(a, axis, [(i, (i + s) % n) for i in range(n)])  44.5 us
    ppermute x7, starting transfers between devices, steps(): m = lax.ppermute(m, 'z', astern(k))  34.8 us
    ppermute x11, waiting for transfers between devices, send(): return lax.ppermute(a, axis, [(i, (i + s) % n) for i in range(n)])  23.3 us
    ppermute x7, waiting for transfers between devices, steps(): m = lax.ppermute(m, 'z', astern(k))  11.5 us
    unnamed x38, local copies, waits for them, and re-layouts  11.2 us
    ppermute x8, starting transfers between devices, steps(): p = lax.ppermute(p, 'z', ahead(k))  7.61 us
    pallas_call x2, Pallas kernels, attend(): pallas(12, slices_kernel, in_specs=[smem] + [vmem] * (1 + len(qs)), out_s...  6.58 us
    all_to_all x1, waiting for transfers between devices, steps(): row = lax.all_to_all(packed, 'y', 0, 0)  5.25 us
  transfers between devices with their start and end apart: 27, of which 11 were waited for; matrix products, arithmetic and copies ran while one was open for 5% of the time, Pallas kernels for 11%

profile of v8, /device:TPU:1, one launch (start us, length us, event | category | flops | bytes accessed | tf_op | source)
XLA Modules:
  0.0 163.6 jit_solution(5231662392583766944)
XLA Ops:
  0.0 8.7 %collective-permute-start = (bf16[512,4096]{1,0:T(8,128)(2,1)}, bf16[512,4096]{1,0:T(8,128)(2,1)}, u32[]{:S(2)}, u32[]{:S(2)}) collective-permute-start(bf16[512,4096]{1,0:T(8,128)(2,1)} %src_ref.1), channel_id=1, source_target_pairs={{0,1},{1,0},{2,3},{3,2},{4,5},{5,4},{6,7},{7,6},{8,9},{9,8},{10,11... | collective-permute-start | bytes 12582920 | tf_op jit(solution)/shard_map/ppermute | solution.py:35
  10.4 4.0 %all-to-all-start = ((bf16[4,96,256]{2,1,0:T(8,128)(2,1)}), bf16[4,96,256]{2,1,0:T(8,128)(2,1)}, u32[]{:S(2)}, u32[]{:S(2)}) async-start(bf16[4,96,256]{2,1,0:T(8,128)(2,1)} %shard_map.59), calls=%async_computation | async-start | bytes 393216 | tf_op jit(solution)/shard_map/all_to_all | solution.py:194
  15.3 5.2 %all-to-all-done = bf16[4,96,256]{2,1,0:T(8,128)(2,1)} async-done(((bf16[4,96,256]{2,1,0:T(8,128)(2,1)}), bf16[4,96,256]{2,1,0:T(8,128)(2,1)}, u32[]{:S(2)}, u32[]{:S(2)}) %all-to-all-start) | async-done | bytes 196640 | tf_op jit(solution)/shard_map/all_to_all | solution.py:194
  26.4 3.1 %collective-permute-start.17 = (bf16[528,384]{1,0:T(8,128)(2,1)S(1)}, bf16[528,384]{1,0:T(8,128)(2,1)S(1)}, u32[]{:S(2)}, u32[]{:S(2)}) collective-permute-start(bf16[528,384]{1,0:T(8,128)(2,1)S(1)} %shard_map.57.q_ref.rest_0_), channel_id=1, source_target_pairs={{0,8},{8,16},{16,24},{24,0},{1,9},{9,17},{17,25},{25,1},{2,10},{10... | collective-permute-start | bytes 1216520 | tf_op jit(solution)/shard_map/ppermute | solution.py:35
  29.5 3.4 %collective-permute-start.18 = (bf16[528,384]{1,0:T(8,128)(2,1)S(1)}, bf16[528,384]{1,0:T(8,128)(2,1)S(1)}, u32[]{:S(2)}, u32[]{:S(2)}) collective-permute-start(bf16[528,384]{1,0:T(8,128)(2,1)S(1)} %shard_map.57.q_ref.rest_0_), channel_id=1, source_target_pairs={{0,24},{8,0},{16,8},{24,16},{1,25},{9,1},{17,9},{25,17},{2,26},{10... | collective-permute-start | bytes 1216520 | tf_op jit(solution)/shard_map/ppermute | solution.py:35
  32.9 5.0 %collective-permute-start.2 = (bf16[4,96,256]{2,1,0:T(8,128)(2,1)}, bf16[4,96,256]{2,1,0:T(8,128)(2,1)}, u32[]{:S(2)}, u32[]{:S(2)}) collective-permute-start(bf16[4,96,256]{2,1,0:T(8,128)(2,1)} %all-to-all-done), channel_id=1, source_target_pairs={{0,480},{32,0},{64,32},{96,64},{128,96},{160,128},{192,160},{1,481... | collective-permute-start | bytes 589832 | tf_op jit(solution)/shard_map/ppermute | solution.py:207
  42.2 5.2 %collective-permute-start.4 = (bf16[4,96,256]{2,1,0:T(8,128)(2,1)}, bf16[4,96,256]{2,1,0:T(8,128)(2,1)}, u32[]{:S(2)}, u32[]{:S(2)}) collective-permute-start(bf16[4,96,256]{2,1,0:T(8,128)(2,1)} %collective-permute-done.2), channel_id=1, source_target_pairs={{480,448},{0,480},{32,0},{64,32},{96,64},{128,96},{160,128},{481,4... | collective-permute-start | bytes 589832 | tf_op jit(solution)/shard_map/ppermute | solution.py:207
  53.4 4.6 %collective-permute-start.6 = (bf16[4,96,256]{2,1,0:T(8,128)(2,1)}, bf16[4,96,256]{2,1,0:T(8,128)(2,1)S(1)}, u32[]{:S(2)}, u32[]{:S(2)}) collective-permute-start(bf16[4,96,256]{2,1,0:T(8,128)(2,1)} %collective-permute-done.4), channel_id=1, source_target_pairs={{448,416},{480,448},{0,480},{32,0},{64,32},{96,64},{128,96},{449,4... | collective-permute-start | bytes 589832 | tf_op jit(solution)/shard_map/ppermute | solution.py:207
  60.9 4.9 %collective-permute-start.8 = (bf16[4,96,256]{2,1,0:T(8,128)(2,1)S(1)}, bf16[4,96,256]{2,1,0:T(8,128)(2,1)S(1)}, u32[]{:S(2)}, u32[]{:S(2)}) collective-permute-start(bf16[4,96,256]{2,1,0:T(8,128)(2,1)S(1)} %collective-permute-done.6), channel_id=1, source_target_pairs={{416,384},{448,416},{480,448},{0,480},{32,0},{64,32},{96,64},{417,... | collective-permute-start | bytes 589832 | tf_op jit(solution)/shard_map/ppermute | solution.py:207
  68.4 5.0 %collective-permute-start.10 = (bf16[4,96,256]{2,1,0:T(8,128)(2,1)S(1)}, bf16[4,96,256]{2,1,0:T(8,128)(2,1)S(1)}, u32[]{:S(2)}, u32[]{:S(2)}) collective-permute-start(bf16[4,96,256]{2,1,0:T(8,128)(2,1)S(1)} %collective-permute-done.8), channel_id=1, source_target_pairs={{384,352},{416,384},{448,416},{480,448},{0,480},{32,0},{64,32},{38... | collective-permute-start | bytes 589832 | tf_op jit(solution)/shard_map/ppermute | solution.py:207
  76.1 5.0 %collective-permute-start.12 = (bf16[4,96,256]{2,1,0:T(8,128)(2,1)S(1)}, bf16[4,96,256]{2,1,0:T(8,128)(2,1)S(1)}, u32[]{:S(2)}, u32[]{:S(2)}) collective-permute-start(bf16[4,96,256]{2,1,0:T(8,128)(2,1)S(1)} %collective-permute-done.10), channel_id=1, source_target_pairs={{352,320},{384,352},{416,384},{448,416},{480,448},{0,480},{32,0},{... | collective-permute-start | bytes 589832 | tf_op jit(solution)/shard_map/ppermute | solution.py:207
  82.0 2.5 %collective-permute-done.12 = bf16[4,96,256]{2,1,0:T(8,128)(2,1)S(1)} collective-permute-done((bf16[4,96,256]{2,1,0:T(8,128)(2,1)S(1)}, bf16[4,96,256]{2,1,0:T(8,128)(2,1)S(1)}, u32[]{:S(2)}, u32[]{:S(2)}) %collective-permute-start.12) | collective-permute-done | bytes 196640 | tf_op jit(solution)/shard_map/ppermute | solution.py:207
  84.5 5.0 %collective-permute-start.14 = (bf16[4,96,256]{2,1,0:T(8,128)(2,1)S(1)}, bf16[4,96,256]{2,1,0:T(8,128)(2,1)S(1)}, u32[]{:S(2)}, u32[]{:S(2)}) collective-permute-start(bf16[4,96,256]{2,1,0:T(8,128)(2,1)S(1)} %collective-permute-done.12), channel_id=1, source_target_pairs={{320,288},{352,320},{384,352},{416,384},{448,416},{480,448},{0,480... | collective-permute-start | bytes 589832 | tf_op jit(solution)/shard_map/ppermute | solution.py:207
  90.3 3.9 %collective-permute-done.14 = bf16[4,96,256]{2,1,0:T(8,128)(2,1)S(1)} collective-permute-done((bf16[4,96,256]{2,1,0:T(8,128)(2,1)S(1)}, bf16[4,96,256]{2,1,0:T(8,128)(2,1)S(1)}, u32[]{:S(2)}, u32[]{:S(2)}) %collective-permute-start.14) | collective-permute-done | bytes 196640 | tf_op jit(solution)/shard_map/ppermute | solution.py:207
  94.3 4.6 %shard_map.61 = (bf16[528,384]{1,0:T(8,128)(2,1)S(1)}, bf16[528,384]{1,0:T(8,128)(2,1)S(1)}, bf16[528,384]{1,0:T(8,128)(2,1)S(1)}) custom-call(s32[36]{0:T(128)S(1)} %copy-done.10, bf16[64,96,256]{2,1,0:T(8,128)(2,1)S(1)} %constant_dynamic-update-slice_fusion.kv_ref, bf16[528,384]{1,0:T(8,128)(2,1)S(1)} %copy-done.2, bf16[528,384]{1,0:T(8,128)(2,1)S(1)} %copy-done.4, ...), custom_call_target="tpu_custom_call" | custom-call | tf_op jit(solution)/shard_map/pallas_call | solution.py:245
  98.9 3.2 %collective-permute-start.19 = (bf16[528,384]{1,0:T(8,128)(2,1)S(1)}, bf16[528,384]{1,0:T(8,128)(2,1)S(1)}, u32[]{:S(2)}, u32[]{:S(2)}) collective-permute-start(bf16[528,384]{1,0:T(8,128)(2,1)S(1)} %get-tuple-element.12), channel_id=1, source_target_pairs={{0,16},{8,24},{16,0},{24,8},{1,17},{9,25},{17,1},{25,9},{2,18},{10... | collective-permute-start | bytes 1216520 | tf_op jit(solution)/shard_map/ppermute | solution.py:35
  102.1 2.8 %collective-permute-start.20 = (bf16[528,384]{1,0:T(8,128)(2,1)S(1)}, bf16[528,384]{1,0:T(8,128)(2,1)S(1)}, u32[]{:S(2)}, u32[]{:S(2)}) collective-permute-start(bf16[528,384]{1,0:T(8,128)(2,1)S(1)} %get-tuple-element.13), channel_id=1, source_target_pairs={{0,24},{8,0},{16,8},{24,16},{1,25},{9,1},{17,9},{25,17},{2,26},{10... | collective-permute-start | bytes 1216520 | tf_op jit(solution)/shard_map/ppermute | solution.py:35
  104.9 2.5 %collective-permute-start.21 = (bf16[528,384]{1,0:T(8,128)(2,1)S(1)}, bf16[528,384]{1,0:T(8,128)(2,1)S(1)}, u32[]{:S(2)}, u32[]{:S(2)}) collective-permute-start(bf16[528,384]{1,0:T(8,128)(2,1)S(1)} %get-tuple-element.14), channel_id=1, source_target_pairs={{0,8},{8,16},{16,24},{24,0},{1,9},{9,17},{17,25},{25,1},{2,10},{10... | collective-permute-start | bytes 1216520 | tf_op jit(solution)/shard_map/ppermute | solution.py:35
  112.1 7.0 %collective-permute-done.21.p3 = bf16[528,384]{1,0:T(8,128)(2,1)S(1)} collective-permute-done((bf16[528,384]{1,0:T(8,128)(2,1)S(1)}, bf16[528,384]{1,0:T(8,128)(2,1)S(1)}, u32[]{:S(2)}, u32[]{:S(2)}) %collective-permute-start.21) | collective-permute-done | bytes 405536 | tf_op jit(solution)/shard_map/ppermute | solution.py:35
  119.6 8.7 %collective-permute-start.22 = (bf16[512,384]{1,0:T(8,128)(2,1)S(1)}, bf16[512,384]{1,0:T(8,128)(2,1)S(1)}, u32[]{:S(2)}, u32[]{:S(2)}) collective-permute-start(bf16[512,384]{1,0:T(8,128)(2,1)S(1)} %shard_map.62.mine_ref), channel_id=1, source_target_pairs={{0,1},{1,0},{2,3},{3,2},{4,5},{5,4},{6,7},{7,6},{8,9},{9,8},{10,11... | collective-permute-start | bytes 1179656 | tf_op jit(solution)/shard_map/ppermute | solution.py:35
  132.4 2.6 %shard_map.56.w_got = bf16[4,512,512]{2,1,0:T(8,128)(2,1)S(1)} custom-call(s32[4]{0:T(128)S(1)} %fusion.2.cols_ref, bf16[512,4096]{1,0:T(8,128)(2,1)} %collective-permute-done.src_ref), custom_call_target="tpu_custom_call" | custom-call | tf_op jit(solution)/shard_map/pallas_call | solution.py:227
  135.7 4.4 %collective-permute-start.25 = (bf16[512,384]{1,0:T(8,128)(2,1)S(1)}, bf16[512,384]{1,0:T(8,128)(2,1)S(1)}, u32[]{:S(2)}, u32[]{:S(2)}) collective-permute-start(bf16[512,384]{1,0:T(8,128)(2,1)S(1)} %shard_map.66), channel_id=1, source_target_pairs={{0,6},{2,0},{4,2},{6,4},{1,7},{3,1},{5,3},{7,5},{8,14},{10,8},{12,... | collective-permute-start | bytes 1179656 | tf_op jit(solution)/shard_map/ppermute | solution.py:35
  143.4 3.6 %collective-permute-start.23 = (bf16[512,384]{1,0:T(8,128)(2,1)S(1)}, bf16[512,384]{1,0:T(8,128)(2,1)S(1)}, u32[]{:S(2)}, u32[]{:S(2)}) collective-permute-start(bf16[512,384]{1,0:T(8,128)(2,1)S(1)} %shard_map.64), channel_id=1, source_target_pairs={{0,4},{2,6},{4,0},{6,2},{1,5},{3,7},{5,1},{7,3},{8,12},{10,14},{12... | collective-permute-start | bytes 1179656 | tf_op jit(solution)/shard_map/ppermute | solution.py:35
  148.5 14.2 %collective-permute-done.24.g2 = bf16[512,384]{1,0:T(8,128)(2,1)S(1)} collective-permute-done((bf16[512,384]{1,0:T(8,128)(2,1)S(1)}, bf16[512,384]{1,0:T(8,128)(2,1)S(1)}, u32[]{:S(2)}, u32[]{:S(2)}) %collective-permute-start.24) | collective-permute-done | bytes 393248 | tf_op jit(solution)/shard_map/ppermute | solution.py:35
  (90 shorter events, 43.8 us)
Async XLA Ops:
  0.0 132.4 %collective-permute-start = (bf16[512,4096]{1,0:T(8,128)(2,1)}, bf16[512,4096]{1,0:T(8,128)(2,1)}, u32[]{:S(2)}, u32[]{:S(2)}) collective-permute-start(bf16[512,4096]{1,0:T(8,128)(2,1)} %src_ref.1), channel_id=1, source_target_pairs={{0,1},{1,0},{2,3},{3,2},{4,5},{5,4},{6,7},{7,6},{8,9},{9,8},{10,11... | collective-permute-start | bytes 12582920 | tf_op jit(solution)/shard_map/ppermute | solution.py:35
  10.4 10.1 %all-to-all-start = ((bf16[4,96,256]{2,1,0:T(8,128)(2,1)}), bf16[4,96,256]{2,1,0:T(8,128)(2,1)}, u32[]{:S(2)}, u32[]{:S(2)}) async-start(bf16[4,96,256]{2,1,0:T(8,128)(2,1)} %shard_map.59), calls=%async_computation | async-start | bytes 393216 | tf_op jit(solution)/shard_map/all_to_all | solution.py:194
  20.5 12.4 %collective-permute-start.1 = (bf16[4,96,256]{2,1,0:T(8,128)(2,1)}, bf16[4,96,256]{2,1,0:T(8,128)(2,1)}, u32[]{:S(2)}, u32[]{:S(2)}) collective-permute-start(bf16[4,96,256]{2,1,0:T(8,128)(2,1)} %all-to-all-done), channel_id=1, source_target_pairs={{0,32},{32,64},{64,96},{96,128},{128,160},{160,192},{192,224},{224... | collective-permute-start | bytes 589832 | tf_op jit(solution)/shard_map/ppermute | solution.py:204
  24.2 18.0 %collective-permute-start.16 = (bf16[528,384]{1,0:T(8,128)(2,1)S(1)}, bf16[528,384]{1,0:T(8,128)(2,1)S(1)}, u32[]{:S(2)}, u32[]{:S(2)}) collective-permute-start(bf16[528,384]{1,0:T(8,128)(2,1)S(1)} %shard_map.57.q_ref.rest_0_), channel_id=1, source_target_pairs={{0,16},{8,24},{16,0},{24,8},{1,17},{9,25},{17,1},{25,9},{2,18},{10... | collective-permute-start | bytes 1216520 | tf_op jit(solution)/shard_map/ppermute | solution.py:35
  26.4 22.7 %collective-permute-start.17 = (bf16[528,384]{1,0:T(8,128)(2,1)S(1)}, bf16[528,384]{1,0:T(8,128)(2,1)S(1)}, u32[]{:S(2)}, u32[]{:S(2)}) collective-permute-start(bf16[528,384]{1,0:T(8,128)(2,1)S(1)} %shard_map.57.q_ref.rest_0_), channel_id=1, source_target_pairs={{0,8},{8,16},{16,24},{24,0},{1,9},{9,17},{17,25},{25,1},{2,10},{10... | collective-permute-start | bytes 1216520 | tf_op jit(solution)/shard_map/ppermute | solution.py:35
  29.5 20.4 %collective-permute-start.18 = (bf16[528,384]{1,0:T(8,128)(2,1)S(1)}, bf16[528,384]{1,0:T(8,128)(2,1)S(1)}, u32[]{:S(2)}, u32[]{:S(2)}) collective-permute-start(bf16[528,384]{1,0:T(8,128)(2,1)S(1)} %shard_map.57.q_ref.rest_0_), channel_id=1, source_target_pairs={{0,24},{8,0},{16,8},{24,16},{1,25},{9,1},{17,9},{25,17},{2,26},{10... | collective-permute-start | bytes 1216520 | tf_op jit(solution)/shard_map/ppermute | solution.py:35
  32.9 7.9 %collective-permute-start.2 = (bf16[4,96,256]{2,1,0:T(8,128)(2,1)}, bf16[4,96,256]{2,1,0:T(8,128)(2,1)}, u32[]{:S(2)}, u32[]{:S(2)}) collective-permute-start(bf16[4,96,256]{2,1,0:T(8,128)(2,1)} %all-to-all-done), channel_id=1, source_target_pairs={{0,480},{32,0},{64,32},{96,64},{128,96},{160,128},{192,160},{1,481... | collective-permute-start | bytes 589832 | tf_op jit(solution)/shard_map/ppermute | solution.py:207
  40.9 11.7 %collective-permute-start.3 = (bf16[4,96,256]{2,1,0:T(8,128)(2,1)}, bf16[4,96,256]{2,1,0:T(8,128)(2,1)}, u32[]{:S(2)}, u32[]{:S(2)}) collective-permute-start(bf16[4,96,256]{2,1,0:T(8,128)(2,1)} %collective-permute-done.1), channel_id=1, source_target_pairs={{32,64},{64,96},{96,128},{128,160},{160,192},{192,224},{224,256},{... | collective-permute-start | bytes 589832 | tf_op jit(solution)/shard_map/ppermute | solution.py:204
  42.2 11.2 %collective-permute-start.4 = (bf16[4,96,256]{2,1,0:T(8,128)(2,1)}, bf16[4,96,256]{2,1,0:T(8,128)(2,1)}, u32[]{:S(2)}, u32[]{:S(2)}) collective-permute-start(bf16[4,96,256]{2,1,0:T(8,128)(2,1)} %collective-permute-done.2), channel_id=1, source_target_pairs={{480,448},{0,480},{32,0},{64,32},{96,64},{128,96},{160,128},{481,4... | collective-permute-start | bytes 589832 | tf_op jit(solution)/shard_map/ppermute | solution.py:207
  53.4 7.5 %collective-permute-start.6 = (bf16[4,96,256]{2,1,0:T(8,128)(2,1)}, bf16[4,96,256]{2,1,0:T(8,128)(2,1)S(1)}, u32[]{:S(2)}, u32[]{:S(2)}) collective-permute-start(bf16[4,96,256]{2,1,0:T(8,128)(2,1)} %collective-permute-done.4), channel_id=1, source_target_pairs={{448,416},{480,448},{0,480},{32,0},{64,32},{96,64},{128,96},{449,4... | collective-permute-start | bytes 589832 | tf_op jit(solution)/shard_map/ppermute | solution.py:207
  60.9 7.5 %collective-permute-start.8 = (bf16[4,96,256]{2,1,0:T(8,128)(2,1)S(1)}, bf16[4,96,256]{2,1,0:T(8,128)(2,1)S(1)}, u32[]{:S(2)}, u32[]{:S(2)}) collective-permute-start(bf16[4,96,256]{2,1,0:T(8,128)(2,1)S(1)} %collective-permute-done.6), channel_id=1, source_target_pairs={{416,384},{448,416},{480,448},{0,480},{32,0},{64,32},{96,64},{417,... | collective-permute-start | bytes 589832 | tf_op jit(solution)/shard_map/ppermute | solution.py:207
  65.9 7.6 %collective-permute-start.9 = (bf16[4,96,256]{2,1,0:T(8,128)(2,1)S(1)}, bf16[4,96,256]{2,1,0:T(8,128)(2,1)S(1)}, u32[]{:S(2)}, u32[]{:S(2)}) collective-permute-start(bf16[4,96,256]{2,1,0:T(8,128)(2,1)S(1)} %collective-permute-done.7), channel_id=1, source_target_pairs={{128,160},{160,192},{192,224},{224,256},{256,288},{288,320},{320,3... | collective-permute-start | bytes 589832 | tf_op jit(solution)/shard_map/ppermute | solution.py:204
  68.4 7.6 %collective-permute-start.10 = (bf16[4,96,256]{2,1,0:T(8,128)(2,1)S(1)}, bf16[4,96,256]{2,1,0:T(8,128)(2,1)S(1)}, u32[]{:S(2)}, u32[]{:S(2)}) collective-permute-start(bf16[4,96,256]{2,1,0:T(8,128)(2,1)S(1)} %collective-permute-done.8), channel_id=1, source_target_pairs={{384,352},{416,384},{448,416},{480,448},{0,480},{32,0},{64,32},{38... | collective-permute-start | bytes 589832 | tf_op jit(solution)/shard_map/ppermute | solution.py:207
  73.5 7.6 %collective-permute-start.11 = (bf16[4,96,256]{2,1,0:T(8,128)(2,1)S(1)}, bf16[4,96,256]{2,1,0:T(8,128)(2,1)S(1)}, u32[]{:S(2)}, u32[]{:S(2)}) collective-permute-start(bf16[4,96,256]{2,1,0:T(8,128)(2,1)S(1)} %collective-permute-done.9), channel_id=1, source_target_pairs={{160,192},{192,224},{224,256},{256,288},{288,320},{320,352},{352,3... | collective-permute-start | bytes 589832 | tf_op jit(solution)/shard_map/ppermute | solution.py:204
  76.1 8.5 %collective-permute-start.12 = (bf16[4,96,256]{2,1,0:T(8,128)(2,1)S(1)}, bf16[4,96,256]{2,1,0:T(8,128)(2,1)S(1)}, u32[]{:S(2)}, u32[]{:S(2)}) collective-permute-start(bf16[4,96,256]{2,1,0:T(8,128)(2,1)S(1)} %collective-permute-done.10), channel_id=1, source_target_pairs={{352,320},{384,352},{416,384},{448,416},{480,448},{0,480},{32,0},{... | collective-permute-start | bytes 589832 | tf_op jit(solution)/shard_map/ppermute | solution.py:207
  81.2 8.4 %collective-permute-start.13 = (bf16[4,96,256]{2,1,0:T(8,128)(2,1)S(1)}, bf16[4,96,256]{2,1,0:T(8,128)(2,1)S(1)}, u32[]{:S(2)}, u32[]{:S(2)}) collective-permute-start(bf16[4,96,256]{2,1,0:T(8,128)(2,1)S(1)} %collective-permute-done.11), channel_id=1, source_target_pairs={{192,224},{224,256},{256,288},{288,320},{320,352},{352,384},{384,4... | collective-permute-start | bytes 589832 | tf_op jit(solution)/shard_map/ppermute | solution.py:204
  84.5 9.7 %collective-permute-start.14 = (bf16[4,96,256]{2,1,0:T(8,128)(2,1)S(1)}, bf16[4,96,256]{2,1,0:T(8,128)(2,1)S(1)}, u32[]{:S(2)}, u32[]{:S(2)}) collective-permute-start(bf16[4,96,256]{2,1,0:T(8,128)(2,1)S(1)} %collective-permute-done.12), channel_id=1, source_target_pairs={{320,288},{352,320},{384,352},{416,384},{448,416},{480,448},{0,480... | collective-permute-start | bytes 589832 | tf_op jit(solution)/shard_map/ppermute | solution.py:207
  98.9 11.8 %collective-permute-start.19 = (bf16[528,384]{1,0:T(8,128)(2,1)S(1)}, bf16[528,384]{1,0:T(8,128)(2,1)S(1)}, u32[]{:S(2)}, u32[]{:S(2)}) collective-permute-start(bf16[528,384]{1,0:T(8,128)(2,1)S(1)} %get-tuple-element.12), channel_id=1, source_target_pairs={{0,16},{8,24},{16,0},{24,8},{1,17},{9,25},{17,1},{25,9},{2,18},{10... | collective-permute-start | bytes 1216520 | tf_op jit(solution)/shard_map/ppermute | solution.py:35
  102.1 10.0 %collective-permute-start.20 = (bf16[528,384]{1,0:T(8,128)(2,1)S(1)}, bf16[528,384]{1,0:T(8,128)(2,1)S(1)}, u32[]{:S(2)}, u32[]{:S(2)}) collective-permute-start(bf16[528,384]{1,0:T(8,128)(2,1)S(1)} %get-tuple-element.13), channel_id=1, source_target_pairs={{0,24},{8,0},{16,8},{24,16},{1,25},{9,1},{17,9},{25,17},{2,26},{10... | collective-permute-start | bytes 1216520 | tf_op jit(solution)/shard_map/ppermute | solution.py:35
  104.9 14.2 %collective-permute-start.21 = (bf16[528,384]{1,0:T(8,128)(2,1)S(1)}, bf16[528,384]{1,0:T(8,128)(2,1)S(1)}, u32[]{:S(2)}, u32[]{:S(2)}) collective-permute-start(bf16[528,384]{1,0:T(8,128)(2,1)S(1)} %get-tuple-element.14), channel_id=1, source_target_pairs={{0,8},{8,16},{16,24},{24,0},{1,9},{9,17},{17,25},{25,1},{2,10},{10... | collective-permute-start | bytes 1216520 | tf_op jit(solution)/shard_map/ppermute | solution.py:35
  119.6 15.3 %collective-permute-start.22 = (bf16[512,384]{1,0:T(8,128)(2,1)S(1)}, bf16[512,384]{1,0:T(8,128)(2,1)S(1)}, u32[]{:S(2)}, u32[]{:S(2)}) collective-permute-start(bf16[512,384]{1,0:T(8,128)(2,1)S(1)} %shard_map.62.mine_ref), channel_id=1, source_target_pairs={{0,1},{1,0},{2,3},{3,2},{4,5},{5,4},{6,7},{7,6},{8,9},{9,8},{10,11... | collective-permute-start | bytes 1179656 | tf_op jit(solution)/shard_map/ppermute | solution.py:35
  135.7 12.8 %collective-permute-start.25 = (bf16[512,384]{1,0:T(8,128)(2,1)S(1)}, bf16[512,384]{1,0:T(8,128)(2,1)S(1)}, u32[]{:S(2)}, u32[]{:S(2)}) collective-permute-start(bf16[512,384]{1,0:T(8,128)(2,1)S(1)} %shard_map.66), channel_id=1, source_target_pairs={{0,6},{2,0},{4,2},{6,4},{1,7},{3,1},{5,3},{7,5},{8,14},{10,8},{12,... | collective-permute-start | bytes 1179656 | tf_op jit(solution)/shard_map/ppermute | solution.py:35
  140.8 21.9 %collective-permute-start.24 = (bf16[512,384]{1,0:T(8,128)(2,1)S(1)}, bf16[512,384]{1,0:T(8,128)(2,1)S(1)}, u32[]{:S(2)}, u32[]{:S(2)}) collective-permute-start(bf16[512,384]{1,0:T(8,128)(2,1)S(1)} %shard_map.65), channel_id=1, source_target_pairs={{0,2},{2,4},{4,6},{6,0},{1,3},{3,5},{5,7},{7,1},{8,10},{10,12},{12... | collective-permute-start | bytes 1179656 | tf_op jit(solution)/shard_map/ppermute | solution.py:35
  143.4 19.3 %collective-permute-start.23 = (bf16[512,384]{1,0:T(8,128)(2,1)S(1)}, bf16[512,384]{1,0:T(8,128)(2,1)S(1)}, u32[]{:S(2)}, u32[]{:S(2)}) collective-permute-start(bf16[512,384]{1,0:T(8,128)(2,1)S(1)} %shard_map.64), channel_id=1, source_target_pairs={{0,4},{2,6},{4,0},{6,2},{1,5},{3,7},{5,1},{7,3},{8,12},{10,14},{12... | collective-permute-start | bytes 1179656 | tf_op jit(solution)/shard_map/ppermute | solution.py:35
  (14 other events, 242.6 us)
